TPU v7x, 32 devices: a whole 2x2x4 slice. The times are simulated.
32 devices in a mesh: vel: 8 (over z, y), gx: 4 (over x, core).
Axes of the slice: x: 2, y: 2, z: 4, core: 2. Of those that a mesh axis runs over, the one named last changes fastest.
Arguments:
- distribution: float32 [4096, 32, 128], P('vel', 'gx'), may hold values from 0.1 to 10
- velocity: float32 [3, 4096], P(None, 'vel'), may hold values from -3 to 3
- weights: float32 [4096], P('vel'), may hold values from 0.00012207031 to 0.00048828125
- collision: float32 [32, 128], P('gx'), may hold values from 0.2 to 2
- solid: int32 [32, 128], P('gx'), may hold values 0 or 1
- inflow: float32 [2, 4096, 128], P(None, 'vel'), may hold values from 0.1 to 10
Outputs:
- evolved: float32 [4096, 32, 128], P('vel', 'gx')
- macroscopic: float32 [5, 32, 128], P(None, 'gx')
All inputs are finite; a program needn't handle non-finite values. No bound on the sum of `solid` on one device may be relied on, other than what follows from the above.
Results may differ from a plain program's by a relative error of at most 0.0001.
Values sent between devices are 32-bit elements; how exact they have to be, the bound alone decides.
No kernel may reach another device: no remote copies, remote signals or barrier semaphores. Data moves between devices by JAX's collectives and lax.ppermute only.
A program may use at most 128 MiB of HBM per device.

v0:
```python
import functools
import math

import jax
import jax.numpy as jnp
from jax import lax
from jax.experimental import pallas as pl
from jax.experimental.pallas import tpu as pltpu
from jax.sharding import PartitionSpec as P

NY = 16
NZ = 8
ITERS = 2
JACOBI = 2
HALO = JACOBI + 1
pseudo_rate = 0.5
source_gain = 0.5
diffusion = (0.6, 0.8, 0.8, 0.8, 1.0)
viscous_conduction_ratio = 2.0 / 3.0
wall_rate = 4.0
box_volume = 216.0
LOG2E = math.log2(math.e)
LANES = 128
SUB = 8
PAIRS = ((0, 0), (0, 1), (1, 0), (0, 2), (2, 0), (1, 1))
FEATURES = 32
A, B, E, W, HB, HE, BASE, FA, BA, REST = range(10)
TABLE = 10


def f32(*shape):
    return jax.ShapeDtypeStruct(shape, jnp.float32)


def add_moments(acc, s, t_ref, rows):
    a, b, e = (t_ref[k, rows, :] for k in (A, B, E))
    g = s * t_ref[W, rows, :]
    ga, gb, ge = g * a, g * b, g * e
    gaa, gbb, gee = ga * a, gb * b, ge * e
    gs = gaa + gbb + gee
    terms = (g, ga, gb, ge, gs, gaa, gbb, ga * b, ga * e, gb * e, gs * a, gs * b, gs * e)
    return tuple(old + new for old, new in zip(acc, terms))


def write_moments(m_ref, x, acc):
    for field, value in enumerate(acc):
        m_ref[field, x : x + 1, :] = jnp.sum(value, axis=0, keepdims=True)


def moments_loop(m_ref, t_ref, width, groups, state_at):
    zero = tuple(jnp.zeros((SUB, LANES), jnp.float32) for _ in range(13))
    for x in range(width):

        def step(g, acc):
            rows = pl.ds(pl.multiple_of(g * SUB, SUB), SUB)
            return add_moments(acc, state_at(x, rows), t_ref, rows)

        write_moments(m_ref, x, lax.fori_loop(0, groups, step, zero, unroll=4))


def first_kernel(extent, v_ref, dist_ref, m_ref, t_ref, s_ref):
    count, width = dist_ref.shape[0], dist_ref.shape[1]
    columns = v_ref[...].T

    def wide(k):
        return jnp.broadcast_to(columns[:, k : k + 1], (count, LANES))

    a, b, e = wide(0), wide(1), wide(2)
    t_ref[A], t_ref[B], t_ref[E], t_ref[W] = a, b, e, wide(3)
    hb, he = 0.5 * jnp.abs(b), 0.5 * jnp.abs(e)
    t_ref[HB], t_ref[HE] = hb, he
    t_ref[BASE] = pseudo_rate + (hb + he) + jnp.abs(a) * extent
    t_ref[FA], t_ref[BA] = jnp.maximum(a, 0.0) * extent, jnp.maximum(-a, 0.0) * extent
    t_ref[REST] = (box_volume * (2.0 * math.pi) ** (-1.5)) * jnp.exp(-0.5 * (a * a + b * b + e * e))

    def state_at(x, rows):
        s = dist_ref[rows, x, :]
        s_ref[x, rows, :] = s
        return s

    moments_loop(m_ref, t_ref, width, count // SUB, state_at)


def gains_kernel(peers, me_ref, t_ref, rate_ref, rden_ref, p_ref, g_ref):
    width, count = rden_ref.shape[0], rden_ref.shape[1]
    me = me_ref[0]

    def step(g, carry):
        rows = pl.ds(pl.multiple_of(g * SUB, SUB), SUB)
        base, fa, ba = t_ref[BASE, rows, :], t_ref[FA, rows, :], t_ref[BA, rows, :]
        gain = fa + ba
        ahead = t_ref[A, rows, :] >= 0.0
        power = gain * gain
        power = power * power
        power = power * power if width == 8 else gain**width
        for d in range(peers):
            product = base + rate_ref[d ^ me, 0:1, :]
            for x in range(1, width):
                product = product * (base + rate_ref[d ^ me, x : x + 1, :])
            g_ref[d, rows, :] = power / product
        steps = []
        for x in range(width):
            rden = 1.0 / (base + rate_ref[0, x : x + 1, :])
            rden_ref[x, rows, :] = rden
            steps.append(gain * rden)
        up, down = [steps[0]], [steps[-1]]
        for x in range(1, width):
            up.append(up[-1] * steps[x])
            down.append(down[-1] * steps[width - 1 - x])
        for x in range(width):
            p_ref[x, rows, :] = jnp.where(ahead, up[x], down[width - 1 - x])
        return carry

    lax.fori_loop(0, count // SUB, step, 0)


def features_kernel(v_ref, f_ref):
    blocks = v_ref.shape[0]
    part = v_ref.shape[1] // 4
    for k in range(blocks):
        a, b, e, w = (v_ref[k, i * part : (i + 1) * part, :] for i in range(4))
        sides = [split(value) for value in (a, b, e, a * a + b * b + e * e)]
        one, zero = jnp.ones_like(a), jnp.zeros_like(a)
        rows = [side[i] for side in sides for i, _ in PAIRS] + [one] * 3 + split(jnp.log2(w))
        rows = rows + [zero] * (FEATURES - len(rows))
        for i, row in enumerate(rows):
            f_ref[i, k * part : (k + 1) * part, :] = row


def split(value):
    parts = []
    for _ in range(3):
        part = value.astype(jnp.bfloat16).astype(jnp.float32)
        parts.append(part)
        value = value - part
    return parts


def lane_z():
    return lax.broadcasted_iota(jnp.int32, (1, LANES), 1) % NZ


def y_less(v):
    return pltpu.roll(v, NZ, 1)


def y_more(v):
    return pltpu.roll(v, LANES - NZ, 1)


def z_less(v):
    return jnp.where(lane_z() == 0, pltpu.roll(v, LANES - NZ + 1, 1), pltpu.roll(v, 1, 1))


def z_more(v):
    return jnp.where(lane_z() == NZ - 1, pltpu.roll(v, NZ - 1, 1), pltpu.roll(v, LANES - 1, 1))


def dy(v):
    return 0.5 * (y_more(v) - y_less(v))


def dz(v):
    return 0.5 * (z_more(v) - z_less(v))


def x_less(v):
    return pltpu.roll(v, 1, 0)


def x_more(v):
    return pltpu.roll(v, v.shape[0] - 1, 0)


def fields_of(m):
    rho = m[0]
    inverse = 1.0 / rho
    u = [m[1 + i] * inverse for i in range(3)]
    square = u[0] * u[0] + u[1] * u[1] + u[2] * u[2]
    warm = (m[4] * inverse - square) * (1.0 / 3.0)
    force = rho * warm
    second = [[m[5], m[7], m[8]], [m[7], m[6], m[9]], [m[8], m[9], m[4] - m[5] - m[6]]]
    xx = second[0][0] - rho * u[0] * u[0] - force
    yy = second[1][1] - rho * u[1] * u[1] - force
    xy = second[0][1] - rho * u[0] * u[1]
    xz = second[0][2] - rho * u[0] * u[2]
    yz = second[1][2] - rho * u[1] * u[2]
    heat = []
    for i in range(3):
        inner = u[0] * second[i][0] + u[1] * second[i][1] + u[2] * second[i][2]
        heat.append(0.5 * (m[10 + i] - 2.0 * inner - u[i] * m[4] + 2.0 * rho * u[i] * square))
    return rho, inverse, u, warm, (xx, yy, xy, xz, yz), heat


def correction(rho, inverse, u, warm, stress, heat, inside):
    xx, yy, xy, xz, yz = stress
    zz = -(xx + yy)

    def dx(v):
        v = jnp.where(inside, v, 0.0)
        return 0.5 * (x_more(v) - x_less(v))

    source = [
        dx(rho * u[0]) + dy(rho * u[1]) + dz(rho * u[2]),
        dx(xx) + dy(xy) + dz(xz),
        dx(xy) + dy(yy) + dz(yz),
        dx(xz) + dy(yz) + dz(zz),
        dx(heat[0]) + dy(heat[1]) + dz(heat[2]),
    ]
    scale = [-source_gain * inverse] * 4 + [(-source_gain * 2.0 / 3.0) / (rho * warm)]
    source = [jnp.where(inside, s * c, 0.0) for s, c in zip(source, scale)]
    delta = source
    for _ in range(JACOBI):
        fresh = []
        for mu, s, d in zip(diffusion, source, delta):
            beside = x_less(d) + x_more(d) + y_less(d) + y_more(d) + z_less(d) + z_more(d)
            fresh.append(jnp.where(inside, (s + mu * beside) * (1.0 / (1.0 + 6.0 * mu)), 0.0))
        delta = fresh
    return delta


def kinetic_kernel(
    peers, me_ref, before_ref, m_ref, after_ref, f_ref, t_ref, rate_ref, wall_ref, state_ref, rden_ref,
    s_ref, c_ref, macro_ref, pad_ref, cell_ref, field_ref, total_ref,
):
    width, count = s_ref.shape[0], s_ref.shape[1]
    me = me_ref[0]
    tall = width + 2 * SUB
    own = slice(SUB, SUB + width)
    pad_ref[...] = jnp.ones_like(pad_ref)
    for k in range(13):
        pad_ref[k, SUB - HALO : SUB, :] = before_ref[k]
        pad_ref[k, own, :] = m_ref[k]
        pad_ref[k, SUB + width : SUB + width + HALO, :] = after_ref[k]
    row = lax.broadcasted_iota(jnp.int32, (tall, LANES), 0) + (me * width - SUB)
    inside = (row >= 0) & (row < peers * width)
    rho, inverse, u, warm, stress, heat = fields_of([pad_ref[k] for k in range(13)])
    delta = correction(rho, inverse, u, warm, stress, heat, inside)
    for k, value in enumerate(
        (rho * jnp.exp(delta[0]), u[0] + delta[1], u[1] + delta[2], u[2] + delta[3], warm * jnp.exp(delta[4]))
    ):
        pad_ref[k] = value
        macro_ref[k] = pad_ref[k, own, :]
    for k in range(3):
        pad_ref[5 + k] = heat[k]
    R, U, T = macro_ref[0], [macro_ref[1 + k] for k in range(3)], macro_ref[4]
    q = [pad_ref[5 + k, own, :] for k in range(3)]
    cold = 1.0 / T
    beta = (-0.5 * LOG2E) * cold
    alpha = [(LOG2E * cold) * U[k] for k in range(3)]
    gamma = beta * (U[0] * U[0] + U[1] * U[1] + U[2] * U[2])
    rows = [side[j] for side in (split(v) for v in (*alpha, beta)) for _, j in PAIRS]
    rows = rows + split(gamma) + [jnp.ones_like(T)] * 3
    rows = rows + [jnp.zeros_like(T)] * (FEATURES - len(rows))
    for i, value in enumerate(rows):
        for x in range(width):
            cell_ref[i : i + 1, x * LANES : (x + 1) * LANES] = value[x : x + 1, :]
    cells = cell_ref[...].astype(jnp.bfloat16)

    def mass(r, acc):
        some = f_ref[:, r, :].astype(jnp.bfloat16)
        power = lax.dot_general(some, cells, (((0,), (0,)), ((), ())), preferred_element_type=jnp.float32)
        weight = jnp.exp2(power)
        return acc + jnp.sum(weight.reshape(LANES // SUB, SUB, width * LANES), axis=0)

    acc = lax.fori_loop(0, f_ref.shape[1], mass, jnp.zeros((SUB, width * LANES), jnp.float32))
    acc = jnp.sum(acc, axis=0, keepdims=True)
    for x in range(width):
        total_ref[x : x + 1, :] = acc[:, x * LANES : (x + 1) * LANES]
    wall, rate = wall_ref[...], rate_ref[...]
    third = (1.0 - viscous_conduction_ratio) / (5.0 * R * T * T)
    values = [*U, beta, *(v * third for v in q), cold]
    values += [(1.0 - wall) * R * rate / total_ref[...], wall * R * rate]
    for k, value in enumerate(values):
        field_ref[k] = value

    for x in range(width):
        ux, uy, uz, power, qx, qy, qz, inv, maxwell, rest = (
            jnp.broadcast_to(field_ref[k, x : x + 1, :], (SUB, LANES)) for k in range(10)
        )

        def ahead(g, carry):
            rows = pl.ds(pl.multiple_of(g * SUB, SUB), SUB)
            a, b, e = (t_ref[k, rows, :] for k in (A, B, E))
            s = state_ref[x, rows, :]
            cx, cy, cz = a - ux, b - uy, e - uz
            square = cx * cx + cy * cy + cz * cz
            expo = jnp.exp2(square * power)
            flux = cx * qx + cy * qy + cz * qz
            target = (expo * maxwell) * (1.0 + flux * (square * inv - 5.0)) + rest * t_ref[REST, rows, :]
            driving = pseudo_rate * s + t_ref[HB, rows, :] * jnp.where(b > 0.0, y_less(s), y_more(s))
            driving = driving + t_ref[HE, rows, :] * jnp.where(e > 0.0, z_less(s), z_more(s))
            rden = rden_ref[x, rows, :]
            value = (driving + target) * rden
            if x:
                value = value + (t_ref[FA, rows, :] * rden) * s_ref[x - 1, rows, :]
            s_ref[x, rows, :] = value
            return carry

        lax.fori_loop(0, count // SUB, ahead, 0, unroll=2)

    def back(g, carry):
        rows = pl.ds(pl.multiple_of(g * SUB, SUB), SUB)
        ba = t_ref[BA, rows, :]
        value = s_ref[width - 1, rows, :]
        last = value
        for x in range(width - 2, -1, -1):
            value = s_ref[x, rows, :] + (ba * rden_ref[x, rows, :]) * value
            s_ref[x, rows, :] = value
        c_ref[rows, :] = jnp.where(t_ref[A, rows, :] >= 0.0, last, value)
        return carry

    lax.fori_loop(0, count // SUB, back, 0, unroll=2)


def entering(peers, me, t_ref, c_ref, g_ref, flow_ref, enter_ref):
    count = enter_ref.shape[0]

    def step(g, carry):
        rows = pl.ds(pl.multiple_of(g * SUB, SUB), SUB)
        up, down = flow_ref[0, rows, :], flow_ref[1, rows, :]
        for d in range(peers - 1):
            up = jnp.where(d < me, g_ref[d, rows, :] * up + c_ref[d ^ me, rows, :], up)
        for d in range(peers - 1, 0, -1):
            down = jnp.where(d > me, g_ref[d, rows, :] * down + c_ref[d ^ me, rows, :], down)
        enter_ref[rows, :] = jnp.where(t_ref[A, rows, :] >= 0.0, up, down)
        return carry

    lax.fori_loop(0, count // SUB, step, 0, unroll=2)


def next_kernel(peers, me_ref, t_ref, c_ref, g_ref, flow_ref, s_ref, p_ref, m_ref, state_ref, enter_ref):
    width, count = s_ref.shape[0], s_ref.shape[1]
    entering(peers, me_ref[0], t_ref, c_ref, g_ref, flow_ref, enter_ref)

    def state_at(x, rows):
        s = s_ref[x, rows, :] + p_ref[x, rows, :] * enter_ref[rows, :]
        state_ref[x, rows, :] = s
        return s

    moments_loop(m_ref, t_ref, width, count // SUB, state_at)


def last_kernel(peers, me_ref, t_ref, c_ref, g_ref, flow_ref, s_ref, p_ref, out_ref, enter_ref):
    width, count = s_ref.shape[0], s_ref.shape[1]
    entering(peers, me_ref[0], t_ref, c_ref, g_ref, flow_ref, enter_ref)

    def step(g, carry):
        rows = pl.ds(pl.multiple_of(g * SUB, SUB), SUB)
        enter = enter_ref[rows, :]
        for x in range(width):
            out_ref[rows, x, :] = s_ref[x, rows, :] + p_ref[x, rows, :] * enter
        return carry

    lax.fori_loop(0, count // SUB, step, 0, unroll=2)


def stages(size):
    found, stride = [], 1
    while size > 1:
        factor = next(f for f in range(2, size + 1) if size % f == 0)
        if factor == 2 and size % 4 == 0 and (stride > 1 or size % 8):
            factor = 4
        found.append((factor, stride))
        size, stride = size // factor, stride * factor
    return found


def reduce_over(axis, value, extra=None):
    size = lax.axis_size(axis)
    rows = value.shape[0]
    for factor, stride in stages(size):
        sent = value if extra is None else jnp.concatenate([value, extra.reshape(-1, LANES)])
        got = []
        for turn in range(1, factor):
            pairs = []
            for i in range(size):
                digit = i // stride % factor
                pairs.append((i, i + ((digit + turn) % factor - digit) * stride))
            got.append(lax.ppermute(sent, axis, pairs))
        for piece in got:
            value = value + piece[:rows]
        if extra is not None:
            shape = (-1,) + extra.shape[1:]
            extra = jnp.concatenate([extra] + [piece[rows:].reshape(shape) for piece in got])
    return value, extra


def gather_over(axis, value):
    size = lax.axis_size(axis)
    blocks = value[None]
    order = [0]
    bit = size // 2
    while bit:
        got = lax.ppermute(blocks, axis, [(i, i ^ bit) for i in range(size)])
        blocks = jnp.concatenate([blocks, got])
        order = order + [k ^ bit for k in order]
        bit //= 2
    return jnp.concatenate([blocks[order.index(k)][None] for k in range(size)])


def neighbours(axis, value, width):
    size, me = lax.axis_size(axis), lax.axis_index(axis)
    odd = me % 2 == 1
    first, last = value[:, :width], value[:, value.shape[1] - width :]
    near = [(i, i ^ 1) for i in range(size)]
    far = [(i, i + 1) for i in range(1, size - 1, 2)]
    near = lax.ppermute(jnp.where(odd, first, last), axis, near)
    far = lax.ppermute(jnp.where(odd, last, first), axis, far + [(j, i) for i, j in far])
    return jnp.where(odd, near, far), jnp.where(odd, far, near)


def per_device(distribution, velocity, weights, collision, solid, inflow):
    count, width, cells = distribution.shape
    peers = lax.axis_size("gx")
    me = lax.axis_index("gx").astype(jnp.int32).reshape(1)
    wall = solid.astype(jnp.float32)
    rate = collision + wall_rate * wall
    rates = gather_over("gx", rate)
    vw = jnp.concatenate([velocity, weights[None]])
    smem = pl.BlockSpec(memory_space=pltpu.SMEM)
    vmem = pl.BlockSpec(memory_space=pltpu.VMEM)

    def run(kernel, out_shape, args, scratch=(), scalar=True):
        return pl.pallas_call(
            kernel,
            out_shape=out_shape,
            in_specs=([smem] if scalar else []) + [vmem] * (len(args) - (1 if scalar else 0)),
            out_specs=jax.tree.map(lambda _: vmem, out_shape),
            scratch_shapes=scratch,
            compiler_params=pltpu.CompilerParams(vmem_limit_bytes=32 * 1024 * 1024),
        )(*args)

    padded = jnp.concatenate([vw, jnp.zeros((4, count), jnp.float32)])
    m, table, state = run(
        functools.partial(first_kernel, float(width * peers)),
        (f32(13, width, cells), f32(TABLE, count, cells), f32(width, count, cells)),
        (padded, distribution),
        scalar=False,
    )
    extra = vw.reshape(1, 4 * count // LANES, LANES)
    rden, prefix, gains = run(
        functools.partial(gains_kernel, peers),
        (f32(width, count, cells), f32(width, count, cells), f32(peers, count, cells)),
        (me, table, rates),
    )
    for repeat in range(ITERS):
        m, extra = reduce_over("vel", m.reshape(13 * width, cells), extra)
        m = m.reshape(13, width, cells)
        if repeat == 0:
            everyone = f32(FEATURES, extra.shape[0] * extra.shape[1] // 4, LANES)
            features = run(features_kernel, everyone, (extra,), scalar=False)
            extra = None
        before, after = neighbours("gx", m, HALO)
        local, carry, macro = run(
            functools.partial(kinetic_kernel, peers),
            (f32(width, count, cells), f32(count, cells), f32(5, width, cells)),
            (me, before, m, after, features, table, rate, wall, state, rden),
            scratch=(
                pltpu.VMEM((13, width + 2 * SUB, cells), jnp.float32),
                pltpu.VMEM((FEATURES, width * cells), jnp.float32),
                pltpu.VMEM((10, width, cells), jnp.float32),
                pltpu.VMEM((width, cells), jnp.float32),
            ),
        )
        carries = gather_over("gx", carry)
        args = (me, table, carries, gains, inflow, local, prefix)
        scratch = (pltpu.VMEM((count, cells), jnp.float32),)
        if repeat < ITERS - 1:
            m, state = run(
                functools.partial(next_kernel, peers),
                (f32(13, width, cells), f32(width, count, cells)),
                args,
                scratch,
            )
        else:
            state = run(functools.partial(last_kernel, peers), f32(count, width, cells), args, scratch)
    return state, macro


def solution(mesh):
    return jax.shard_map(
        per_device,
        mesh=mesh,
        in_specs=(
            P("vel", "gx", None),
            P(None, "vel"),
            P("vel"),
            P("gx", None),
            P("gx", None),
            P(None, "vel", None),
        ),
        out_specs=(P("vel", "gx", None), P(None, "gx", None)),
        check_vma=False,
    )
```

profile of v0, /device:TPU:0, one launch (start us, length us, event | category | flops | bytes accessed | tf_op | source)
XLA Modules:
  0.0 142.0 jit_solution(14347406121674907703)
XLA Ops:
  0.6 0.0 copy-start.4
  0.6 0.8 multiply_add_fusion.rate_ref
  1.4 3.0 %collective-permute-start.6 = (f32[1,8,128]{2,1,0:T(8,128)S(1)}, f32[1,8,128]{2,1,0:T(8,128)S(1)}, u32[]{:S(2)}, u32[]{:S(2)}) collective-permute-start(f32[1,8,128]{2,1,0:T(8,128)S(1)} %bitcast.28), channel_id=1, source_target_pairs={{0,2},{1,3},{2,0},{3,1},{4,6},{5,7},{6,4},{7,5},{8,10},{9,11},{10,... | collective-permute-start | bytes 12296 | tf_op jit(solution)/shard_map/ppermute | solution.py:395
  4.4 0.7 pad_maximum_fusion.8
  5.1 0.1 pad.28.clone
  5.2 0.8 maximum_maximum_fusion.v_ref
  6.0 0.0 copy-start.1
  6.0 1.6 %copy-done.1 = f32[512,8,128]{2,1,0:T(8,128)S(1)} copy-done((f32[512,8,128]{2,1,0:T(8,128)S(1)}, f32[512,8,128]{2,1,0:T(8,128)}, u32[]{:S(2)}) %copy-start.1) | copy-done | bytes 2097176
  7.6 4.3 %shard_map.77 = (f32[13,8,128]{2,1,0:T(8,128)S(1)}, f32[10,512,128]{2,1,0:T(8,128)S(1)}, f32[8,512,128]{2,1,0:T(8,128)S(1)}) custom-call(f32[8,512]{1,0:T(8,128)S(1)} %maximum_maximum_fusion.v_ref, f32[512,8,128]{2,1,0:T(8,128)S(1)} %copy-done.1), custom_call_target="tpu_custom_call" | custom-call | tf_op jit(solution)/shard_map/pallas_call | solution.py:425
  11.8 0.0 copy-start.2
  11.9 1.3 copy-done.2
  13.2 1.5 %collective-permute-start = (f32[120,128]{1,0:T(8,128)S(1)}, f32[120,128]{1,0:T(8,128)S(1)}, u32[]{:S(2)}, u32[]{:S(2)}) collective-permute-start(f32[120,128]{1,0:T(8,128)S(1)} %pad_maximum_fusion.5), channel_id=1, source_target_pairs={{0,4},{4,0},{8,12},{12,8},{16,20},{20,16},{24,28},{28,24},{1,5},{5... | collective-permute-start | bytes 184328 | tf_op jit(solution)/shard_map/ppermute | solution.py:380
  14.7 0.0 collective-permute-done.6
  14.7 0.1 collective-permute-start.7
  14.8 0.0 copy-done.4
  14.8 1.1 collective-permute-done.7
  16.0 0.0 copy-start.3
  16.0 1.9 %shard_map.79 = (f32[8,512,128]{2,1,0:T(8,128)S(1)}, f32[8,512,128]{2,1,0:T(8,128)S(1)}, f32[4,512,128]{2,1,0:T(8,128)S(1)}) custom-call(s32[1]{0:T(128)} %bitcast.me_ref, f32[10,512,128]{2,1,0:T(8,128)S(1)} %get-tuple-element.15.t_ref, f32[4,8,128]{2,1,0:T(8,128)S(1)} %pad_maximum_fusion.7.rate_ref), custom_call_target="tpu_custom_call" | custom-call | tf_op jit(solution)/shard_map/pallas_call | solution.py:425
  17.9 0.0 collective-permute-done
  17.9 3.7 %collective-permute-start.3 = (f32[136,128]{1,0:T(8,128)S(1)}, f32[136,128]{1,0:T(8,128)S(1)}, u32[]{:S(2)}, u32[]{:S(2)}) collective-permute-start(f32[136,128]{1,0:T(8,128)S(1)} %pad_maximum_fusion.4), channel_id=1, source_target_pairs={{0,24},{4,28},{8,0},{12,4},{16,8},{20,12},{24,16},{28,20},{1,25},{... | collective-permute-start | bytes 208904 | tf_op jit(solution)/shard_map/ppermute | solution.py:380
  21.6 0.0 collective-permute-start.2
  21.6 1.0 collective-permute-start.1
  22.6 1.6 %collective-permute-done.3 = f32[136,128]{1,0:T(8,128)S(1)} collective-permute-done((f32[136,128]{1,0:T(8,128)S(1)}, f32[136,128]{1,0:T(8,128)S(1)}, u32[]{:S(2)}, u32[]{:S(2)}) %collective-permute-start.3) | collective-permute-done | bytes 69664 | tf_op jit(solution)/shard_map/ppermute | solution.py:380
  24.2 4.5 %collective-permute-done.2 = f32[136,128]{1,0:T(8,128)S(1)} collective-permute-done((f32[136,128]{1,0:T(8,128)S(1)}, f32[136,128]{1,0:T(8,128)S(1)}, u32[]{:S(2)}, u32[]{:S(2)}) %collective-permute-start.2) | collective-permute-done | bytes 69664 | tf_op jit(solution)/shard_map/ppermute | solution.py:380
  28.7 0.0 collective-permute-done.1
  28.7 0.7 collective-permute-start.5
  29.4 2.0 %collective-permute-start.4 = (f32[13,3,128]{2,1,0:T(4,128)S(1)}, f32[13,3,128]{2,1,0:T(4,128)S(1)}, u32[]{:S(2)}, u32[]{:S(2)}) collective-permute-start(f32[13,3,128]{2,1,0:T(4,128)S(1)} %get-tuple-element.39), channel_id=1, source_target_pairs={{0,1},{1,0},{2,3},{3,2},{4,5},{5,4},{6,7},{7,6},{8,9},{9,8},{10,11... | collective-permute-start | bytes 59912 | tf_op jit(solution)/shard_map/ppermute | solution.py:408
  31.4 0.1 shard_map.78.f_ref
  31.5 0.0 collective-permute-done.5
  31.5 0.7 collective-permute-done.4
  32.2 0.0 copy-done.3
  32.3 32.4 %shard_map.80 = (f32[8,512,128]{2,1,0:T(8,128)S(1)}, f32[512,128]{1,0:T(8,128)S(1)}, f32[5,8,128]{2,1,0:T(8,128)}) custom-call(s32[1]{0:T(128)} %bitcast.me_ref, f32[13,3,128]{2,1,0:T(4,128)S(1)} %get-tuple-element.37.before_ref, f32[13,8,128]{2,1,0:T(8,128)S(1)} %fusion.m_ref, f32[13,3,128]{2,1,0:T(4,128)S(1)} %get-tuple-element.36.after_ref, ...), custom_call_target="tpu_custom_call" | custom-call | tf_op jit(solution)/shard_map/pallas_call | solution.py:425
  64.6 0.0 copy-start
  64.6 2.2 %collective-permute-start.8 = (f32[1,512,128]{2,1,0:T(8,128)S(1)}, f32[1,512,128]{2,1,0:T(8,128)S(1)}, u32[]{:S(2)}, u32[]{:S(2)}) collective-permute-start(f32[1,512,128]{2,1,0:T(8,128)S(1)} %bitcast.24), channel_id=1, source_target_pairs={{0,2},{1,3},{2,0},{3,1},{4,6},{5,7},{6,4},{7,5},{8,10},{9,11},{10,... | collective-permute-start | bytes 786440 | tf_op jit(solution)/shard_map/ppermute | solution.py:395
  66.9 6.7 %collective-permute-done.8 = f32[1,512,128]{2,1,0:T(8,128)S(1)} collective-permute-done((f32[1,512,128]{2,1,0:T(8,128)S(1)}, f32[1,512,128]{2,1,0:T(8,128)S(1)}, u32[]{:S(2)}, u32[]{:S(2)}) %collective-permute-start.8) | collective-permute-done | bytes 262176 | tf_op jit(solution)/shard_map/ppermute | solution.py:395
  73.6 0.4 collective-permute-start.9
  73.9 1.6 %collective-permute-done.9 = f32[2,512,128]{2,1,0:T(8,128)S(1)} collective-permute-done((f32[2,512,128]{2,1,0:T(8,128)S(1)}, f32[2,512,128]{2,1,0:T(8,128)S(1)}, u32[]{:S(2)}, u32[]{:S(2)}) %collective-permute-start.9) | collective-permute-done | bytes 524320 | tf_op jit(solution)/shard_map/ppermute | solution.py:395
  75.6 0.1 pad_maximum_fusion.c_ref
  75.7 0.0 copy-done
  75.7 3.8 %shard_map.81 = (f32[13,8,128]{2,1,0:T(8,128)S(1)}, f32[8,512,128]{2,1,0:T(8,128)S(1)}) custom-call(s32[1]{0:T(128)} %bitcast.me_ref, f32[10,512,128]{2,1,0:T(8,128)S(1)} %get-tuple-element.15.t_ref, f32[4,512,128]{2,1,0:T(8,128)S(1)} %pad_maximum_fusion.c_ref, f32[4,512,128]{2,1,0:T(8,128)S(1)} %get-tuple-element.20.g_ref, f32[2,512,128]{2,1,0:T(8,128)S(1)} %copy-done, ...), custom_call_target="tpu_custom_call" | custom-call | tf_op jit(solution)/shard_map/pallas_call | solution.py:425
  79.4 0.6 collective-permute-start.10
  80.0 3.6 %collective-permute-done.10 = f32[104,128]{1,0:T(8,128)S(1)} collective-permute-done((f32[104,128]{1,0:T(8,128)S(1)}, f32[104,128]{1,0:T(8,128)S(1)}, u32[]{:S(2)}, u32[]{:S(2)}) %collective-permute-start.10) | collective-permute-done | bytes 53280 | tf_op jit(solution)/shard_map/ppermute | solution.py:380
  83.7 1.8 %collective-permute-start.13 = (f32[104,128]{1,0:T(8,128)S(1)}, f32[104,128]{1,0:T(8,128)S(1)}, u32[]{:S(2)}, u32[]{:S(2)}) collective-permute-start(f32[104,128]{1,0:T(8,128)S(1)} %bitcast_add_fusion), channel_id=1, source_target_pairs={{0,24},{4,28},{8,0},{12,4},{16,8},{20,12},{24,16},{28,20},{1,25},{... | collective-permute-start | bytes 159752 | tf_op jit(solution)/shard_map/ppermute | solution.py:380
  85.5 0.5 collective-permute-start.12
  86.0 1.9 %collective-permute-start.11 = (f32[104,128]{1,0:T(8,128)S(1)}, f32[104,128]{1,0:T(8,128)S(1)}, u32[]{:S(2)}, u32[]{:S(2)}) collective-permute-start(f32[104,128]{1,0:T(8,128)S(1)} %bitcast_add_fusion), channel_id=1, source_target_pairs={{0,8},{4,12},{8,16},{12,20},{16,24},{20,28},{24,0},{28,4},{1,9},{5... | collective-permute-start | bytes 159752 | tf_op jit(solution)/shard_map/ppermute | solution.py:380
  88.0 0.0 collective-permute-done.13
  88.0 3.3 %collective-permute-done.12 = f32[104,128]{1,0:T(8,128)S(1)} collective-permute-done((f32[104,128]{1,0:T(8,128)S(1)}, f32[104,128]{1,0:T(8,128)S(1)}, u32[]{:S(2)}, u32[]{:S(2)}) %collective-permute-start.12) | collective-permute-done | bytes 53280 | tf_op jit(solution)/shard_map/ppermute | solution.py:380
  91.2 0.7 collective-permute-done.11
  92.0 0.7 collective-permute-start.15
  92.7 1.7 %collective-permute-start.14 = (f32[13,3,128]{2,1,0:T(4,128)S(1)}, f32[13,3,128]{2,1,0:T(4,128)S(1)}, u32[]{:S(2)}, u32[]{:S(2)}) collective-permute-start(f32[13,3,128]{2,1,0:T(4,128)S(1)} %get-tuple-element.35), channel_id=1, source_target_pairs={{0,1},{1,0},{2,3},{3,2},{4,5},{5,4},{6,7},{7,6},{8,9},{9,8},{10,11... | collective-permute-start | bytes 59912 | tf_op jit(solution)/shard_map/ppermute | solution.py:408
  94.4 0.0 collective-permute-done.15
  94.4 0.8 collective-permute-done.14
  95.2 32.4 %shard_map.82 = (f32[8,512,128]{2,1,0:T(8,128)S(1)}, f32[512,128]{1,0:T(8,128)S(1)}, f32[5,8,128]{2,1,0:T(8,128)}) custom-call(s32[1]{0:T(128)} %bitcast.me_ref, f32[13,3,128]{2,1,0:T(4,128)S(1)} %get-tuple-element.33.before_ref, f32[13,8,128]{2,1,0:T(8,128)S(1)} %add_bitcast_fusion.m_ref, f32[13,3,128]{2,1,0:T(4,128)S(1)} %get-tuple-element.32.after_ref, ...), custom_call_target="tpu_custom_call" | custom-call | tf_op jit(solution)/shard_map/pallas_call | solution.py:425
  127.6 2.2 %collective-permute-start.16 = (f32[1,512,128]{2,1,0:T(8,128)S(1)}, f32[1,512,128]{2,1,0:T(8,128)S(1)}, u32[]{:S(2)}, u32[]{:S(2)}) collective-permute-start(f32[1,512,128]{2,1,0:T(8,128)S(1)} %bitcast.21), channel_id=1, source_target_pairs={{0,2},{1,3},{2,0},{3,1},{4,6},{5,7},{6,4},{7,5},{8,10},{9,11},{10,... | collective-permute-start | bytes 786440 | tf_op jit(solution)/shard_map/ppermute | solution.py:395
  129.8 6.6 %collective-permute-done.16 = f32[1,512,128]{2,1,0:T(8,128)S(1)} collective-permute-done((f32[1,512,128]{2,1,0:T(8,128)S(1)}, f32[1,512,128]{2,1,0:T(8,128)S(1)}, u32[]{:S(2)}, u32[]{:S(2)}) %collective-permute-start.16) | collective-permute-done | bytes 262176 | tf_op jit(solution)/shard_map/ppermute | solution.py:395
  136.4 0.1 pad_maximum_fusion.3
  136.5 0.1 collective-permute-start.17
  136.5 1.9 %collective-permute-done.17 = f32[2,512,128]{2,1,0:T(8,128)S(1)} collective-permute-done((f32[2,512,128]{2,1,0:T(8,128)S(1)}, f32[2,512,128]{2,1,0:T(8,128)S(1)}, u32[]{:S(2)}, u32[]{:S(2)}) %collective-permute-start.17) | collective-permute-done | bytes 524320 | tf_op jit(solution)/shard_map/ppermute | solution.py:395
  138.5 0.1 pad_maximum_fusion.1.c_ref
  138.6 3.4 %shard_map.83 = f32[512,8,128]{2,1,0:T(8,128)} custom-call(s32[1]{0:T(128)} %bitcast.me_ref, f32[10,512,128]{2,1,0:T(8,128)S(1)} %get-tuple-element.15.t_ref, f32[4,512,128]{2,1,0:T(8,128)S(1)} %pad_maximum_fusion.1.c_ref, f32[4,512,128]{2,1,0:T(8,128)S(1)} %get-tuple-element.20.g_ref, f32[2,512,128]{2,1,0:T(8,128)S(1)} %copy-done, ...), custom_call_target="tpu_custom_call" | custom-call | tf_op jit(solution)/shard_map/pallas_call | solution.py:425
  (30 shorter events, 0.3 us)
Async XLA Ops:
  0.6 14.2 %copy-start.4 = (s32[8,128]{1,0:T(8,128)S(1)}, s32[8,128]{1,0:T(8,128)}, u32[]{:S(2)}) copy-start(s32[8,128]{1,0:T(8,128)} %param.10) | copy-start | bytes 12292
  1.4 13.3 %collective-permute-start.6 = (f32[1,8,128]{2,1,0:T(8,128)S(1)}, f32[1,8,128]{2,1,0:T(8,128)S(1)}, u32[]{:S(2)}, u32[]{:S(2)}) collective-permute-start(f32[1,8,128]{2,1,0:T(8,128)S(1)} %bitcast.28), channel_id=1, source_target_pairs={{0,2},{1,3},{2,0},{3,1},{4,6},{5,7},{6,4},{7,5},{8,10},{9,11},{10,... | collective-permute-start | bytes 12296 | tf_op jit(solution)/shard_map/ppermute | solution.py:395
  6.0 1.6 %copy-start.1 = (f32[512,8,128]{2,1,0:T(8,128)S(1)}, f32[512,8,128]{2,1,0:T(8,128)}, u32[]{:S(2)}) copy-start(f32[512,8,128]{2,1,0:T(8,128)} %dist_ref.1) | copy-start | bytes 6291460
  11.8 1.3 copy-start.2
  13.2 4.7 %collective-permute-start = (f32[120,128]{1,0:T(8,128)S(1)}, f32[120,128]{1,0:T(8,128)S(1)}, u32[]{:S(2)}, u32[]{:S(2)}) collective-permute-start(f32[120,128]{1,0:T(8,128)S(1)} %pad_maximum_fusion.5), channel_id=1, source_target_pairs={{0,4},{4,0},{8,12},{12,8},{16,20},{20,16},{24,28},{28,24},{1,5},{5... | collective-permute-start | bytes 184328 | tf_op jit(solution)/shard_map/ppermute | solution.py:380
  14.7 1.2 collective-permute-start.7
  16.0 16.3 %copy-start.3 = (f32[8,512,128]{2,1,0:T(8,128)S(1)}, f32[8,512,128]{2,1,0:T(8,128)}, u32[]{:S(2)}) copy-start(f32[8,512,128]{2,1,0:T(8,128)} %copy-done.2) | copy-start | bytes 6291460
  17.9 6.3 %collective-permute-start.3 = (f32[136,128]{1,0:T(8,128)S(1)}, f32[136,128]{1,0:T(8,128)S(1)}, u32[]{:S(2)}, u32[]{:S(2)}) collective-permute-start(f32[136,128]{1,0:T(8,128)S(1)} %pad_maximum_fusion.4), channel_id=1, source_target_pairs={{0,24},{4,28},{8,0},{12,4},{16,8},{20,12},{24,16},{28,20},{1,25},{... | collective-permute-start | bytes 208904 | tf_op jit(solution)/shard_map/ppermute | solution.py:380
  21.6 7.1 %collective-permute-start.2 = (f32[136,128]{1,0:T(8,128)S(1)}, f32[136,128]{1,0:T(8,128)S(1)}, u32[]{:S(2)}, u32[]{:S(2)}) collective-permute-start(f32[136,128]{1,0:T(8,128)S(1)} %pad_maximum_fusion.4), channel_id=1, source_target_pairs={{0,16},{4,20},{8,24},{12,28},{16,0},{20,4},{24,8},{28,12},{1,17},{... | collective-permute-start | bytes 208904 | tf_op jit(solution)/shard_map/ppermute | solution.py:380
  21.6 7.1 %collective-permute-start.1 = (f32[136,128]{1,0:T(8,128)S(1)}, f32[136,128]{1,0:T(8,128)S(1)}, u32[]{:S(2)}, u32[]{:S(2)}) collective-permute-start(f32[136,128]{1,0:T(8,128)S(1)} %pad_maximum_fusion.4), channel_id=1, source_target_pairs={{0,8},{4,12},{8,16},{12,20},{16,24},{20,28},{24,0},{28,4},{1,9},{5... | collective-permute-start | bytes 208904 | tf_op jit(solution)/shard_map/ppermute | solution.py:380
  28.7 2.8 %collective-permute-start.5 = (f32[13,3,128]{2,1,0:T(4,128)S(1)}, f32[13,3,128]{2,1,0:T(4,128)S(1)}, u32[]{:S(2)}, u32[]{:S(2)}) collective-permute-start(f32[13,3,128]{2,1,0:T(4,128)S(1)} %get-tuple-element.38), channel_id=1, source_target_pairs={{1,2},{2,1},{5,6},{6,5},{9,10},{10,9},{13,14},{14,13},{17,18},{18,... | collective-permute-start | bytes 59912 | tf_op jit(solution)/shard_map/ppermute | solution.py:409
  29.4 2.8 %collective-permute-start.4 = (f32[13,3,128]{2,1,0:T(4,128)S(1)}, f32[13,3,128]{2,1,0:T(4,128)S(1)}, u32[]{:S(2)}, u32[]{:S(2)}) collective-permute-start(f32[13,3,128]{2,1,0:T(4,128)S(1)} %get-tuple-element.39), channel_id=1, source_target_pairs={{0,1},{1,0},{2,3},{3,2},{4,5},{5,4},{6,7},{7,6},{8,9},{9,8},{10,11... | collective-permute-start | bytes 59912 | tf_op jit(solution)/shard_map/ppermute | solution.py:408
  64.6 11.1 %copy-start = (f32[2,512,128]{2,1,0:T(8,128)S(1)}, f32[2,512,128]{2,1,0:T(8,128)}, u32[]{:S(2)}) copy-start(f32[2,512,128]{2,1,0:T(8,128)} %flow_ref.3) | copy-start | bytes 1572868
  64.6 8.9 %collective-permute-start.8 = (f32[1,512,128]{2,1,0:T(8,128)S(1)}, f32[1,512,128]{2,1,0:T(8,128)S(1)}, u32[]{:S(2)}, u32[]{:S(2)}) collective-permute-start(f32[1,512,128]{2,1,0:T(8,128)S(1)} %bitcast.24), channel_id=1, source_target_pairs={{0,2},{1,3},{2,0},{3,1},{4,6},{5,7},{6,4},{7,5},{8,10},{9,11},{10,... | collective-permute-start | bytes 786440 | tf_op jit(solution)/shard_map/ppermute | solution.py:395
  73.6 2.0 %collective-permute-start.9 = (f32[2,512,128]{2,1,0:T(8,128)S(1)}, f32[2,512,128]{2,1,0:T(8,128)S(1)}, u32[]{:S(2)}, u32[]{:S(2)}) collective-permute-start(f32[2,512,128]{2,1,0:T(8,128)S(1)} %pad_maximum_fusion.2), channel_id=1, source_target_pairs={{0,1},{1,0},{2,3},{3,2},{4,5},{5,4},{6,7},{7,6},{8,9},{9,8},{10,11... | collective-permute-start | bytes 1572872 | tf_op jit(solution)/shard_map/ppermute | solution.py:395
  79.4 4.2 %collective-permute-start.10 = (f32[104,128]{1,0:T(8,128)S(1)}, f32[104,128]{1,0:T(8,128)S(1)}, u32[]{:S(2)}, u32[]{:S(2)}) collective-permute-start(f32[104,128]{1,0:T(8,128)S(1)} %bitcast.31), channel_id=1, source_target_pairs={{0,4},{4,0},{8,12},{12,8},{16,20},{20,16},{24,28},{28,24},{1,5},{5... | collective-permute-start | bytes 159752 | tf_op jit(solution)/shard_map/ppermute | solution.py:380
  83.7 4.3 %collective-permute-start.13 = (f32[104,128]{1,0:T(8,128)S(1)}, f32[104,128]{1,0:T(8,128)S(1)}, u32[]{:S(2)}, u32[]{:S(2)}) collective-permute-start(f32[104,128]{1,0:T(8,128)S(1)} %bitcast_add_fusion), channel_id=1, source_target_pairs={{0,24},{4,28},{8,0},{12,4},{16,8},{20,12},{24,16},{28,20},{1,25},{... | collective-permute-start | bytes 159752 | tf_op jit(solution)/shard_map/ppermute | solution.py:380
  85.5 5.7 %collective-permute-start.12 = (f32[104,128]{1,0:T(8,128)S(1)}, f32[104,128]{1,0:T(8,128)S(1)}, u32[]{:S(2)}, u32[]{:S(2)}) collective-permute-start(f32[104,128]{1,0:T(8,128)S(1)} %bitcast_add_fusion), channel_id=1, source_target_pairs={{0,16},{4,20},{8,24},{12,28},{16,0},{20,4},{24,8},{28,12},{1,17},{... | collective-permute-start | bytes 159752 | tf_op jit(solution)/shard_map/ppermute | solution.py:380
  86.0 5.9 %collective-permute-start.11 = (f32[104,128]{1,0:T(8,128)S(1)}, f32[104,128]{1,0:T(8,128)S(1)}, u32[]{:S(2)}, u32[]{:S(2)}) collective-permute-start(f32[104,128]{1,0:T(8,128)S(1)} %bitcast_add_fusion), channel_id=1, source_target_pairs={{0,8},{4,12},{8,16},{12,20},{16,24},{20,28},{24,0},{28,4},{1,9},{5... | collective-permute-start | bytes 159752 | tf_op jit(solution)/shard_map/ppermute | solution.py:380
  92.0 2.4 %collective-permute-start.15 = (f32[13,3,128]{2,1,0:T(4,128)S(1)}, f32[13,3,128]{2,1,0:T(4,128)S(1)}, u32[]{:S(2)}, u32[]{:S(2)}) collective-permute-start(f32[13,3,128]{2,1,0:T(4,128)S(1)} %get-tuple-element.34), channel_id=1, source_target_pairs={{1,2},{2,1},{5,6},{6,5},{9,10},{10,9},{13,14},{14,13},{17,18},{18,... | collective-permute-start | bytes 59912 | tf_op jit(solution)/shard_map/ppermute | solution.py:409
  92.7 2.6 %collective-permute-start.14 = (f32[13,3,128]{2,1,0:T(4,128)S(1)}, f32[13,3,128]{2,1,0:T(4,128)S(1)}, u32[]{:S(2)}, u32[]{:S(2)}) collective-permute-start(f32[13,3,128]{2,1,0:T(4,128)S(1)} %get-tuple-element.35), channel_id=1, source_target_pairs={{0,1},{1,0},{2,3},{3,2},{4,5},{5,4},{6,7},{7,6},{8,9},{9,8},{10,11... | collective-permute-start | bytes 59912 | tf_op jit(solution)/shard_map/ppermute | solution.py:408
  127.6 8.8 %collective-permute-start.16 = (f32[1,512,128]{2,1,0:T(8,128)S(1)}, f32[1,512,128]{2,1,0:T(8,128)S(1)}, u32[]{:S(2)}, u32[]{:S(2)}) collective-permute-start(f32[1,512,128]{2,1,0:T(8,128)S(1)} %bitcast.21), channel_id=1, source_target_pairs={{0,2},{1,3},{2,0},{3,1},{4,6},{5,7},{6,4},{7,5},{8,10},{9,11},{10,... | collective-permute-start | bytes 786440 | tf_op jit(solution)/shard_map/ppermute | solution.py:395
  136.5 2.0 %collective-permute-start.17 = (f32[2,512,128]{2,1,0:T(8,128)S(1)}, f32[2,512,128]{2,1,0:T(8,128)S(1)}, u32[]{:S(2)}, u32[]{:S(2)}) collective-permute-start(f32[2,512,128]{2,1,0:T(8,128)S(1)} %pad_maximum_fusion.3), channel_id=1, source_target_pairs={{0,1},{1,0},{2,3},{3,2},{4,5},{5,4},{6,7},{7,6},{8,9},{9,8},{10,11... | collective-permute-start | bytes 1572872 | tf_op jit(solution)/shard_map/ppermute | solution.py:395
where the time goes:
time: 142 us
  Pallas kernels  78.2 us (55%)
  waiting for transfers between devices  33.2 us (23%)
  starting transfers between devices  23.9 us (17%)
  local copies, waits for them, and re-layouts  3.11 us (2%)
  other arithmetic  2.66 us (2%)
    pallas_call x7, Pallas kernels, run(): pl.pallas_call(kernel, out_shape=out_shape, in_specs=([smem] if scalar el...  78.2 us
    ppermute x6, waiting for transfers between devices, gather_over(): got = lax.ppermute(blocks, axis, [(i, i ^ bit) for i in range(size)])  17.9 us
    ppermute x8, waiting for transfers between devices, reduce_over(): got.append(lax.ppermute(sent, axis, pairs))  13.7 us
    ppermute x8, starting transfers between devices, reduce_over(): got.append(lax.ppermute(sent, axis, pairs))  11 us
    ppermute x6, starting transfers between devices, gather_over(): got = lax.ppermute(blocks, axis, [(i, i ^ bit) for i in range(size)])  7.91 us
    ppermute x2, starting transfers between devices, neighbours(): near = lax.ppermute(jnp.where(odd, first, last), axis, near)  3.67 us
    unnamed x14, local copies, waits for them, and re-layouts  2.93 us
  transfers between devices with their start and end apart: 18, of which 12 were waited for; matrix products, arithmetic and copies ran while one was open for 1% of the time, Pallas kernels for 4%

commit v1 on v0

--- a/solution.py
+++ b/solution.py
@@ -114,7 +114,7 @@
     lax.fori_loop(0, count // SUB, step, 0)
 
 
-def features_kernel(v_ref, f_ref):
+def features_kernel(v_ref, f_ref, row_ref):
     blocks = v_ref.shape[0]
     part = v_ref.shape[1] // 4
     for k in range(blocks):
@@ -124,7 +124,15 @@
         rows = [side[i] for side in sides for i, _ in PAIRS] + [one] * 3 + split(jnp.log2(w))
         rows = rows + [zero] * (FEATURES - len(rows))
         for i, row in enumerate(rows):
-            f_ref[i, k * part : (k + 1) * part, :] = row
+            for j in range(part):
+                row_ref[k * part + j, i : i + 1, :] = row[j : j + 1, :]
+
+    def turn(r, carry):
+        where = pl.ds(pl.multiple_of(r * LANES, LANES), LANES)
+        f_ref[where, :] = row_ref[r].T.astype(jnp.bfloat16)
+        return carry
+
+    lax.fori_loop(0, blocks * part, turn, 0, unroll=4)
 
 
 def split(value):
@@ -219,8 +227,30 @@
     return delta
 
 
+def transport_kernel(t_ref, s_ref, drive_ref):
+    width, count = s_ref.shape[0], s_ref.shape[1]
+    lane = lax.broadcasted_iota(jnp.int32, (SUB, LANES), 1)
+    z = lane % NZ
+    y_down, y_up = (lane + LANES - NZ) % LANES, (lane + NZ) % LANES
+    z_down, z_up = lane - z + (z + NZ - 1) % NZ, lane - z + (z + 1) % NZ
+
+    def step(g, carry):
+        rows = pl.ds(pl.multiple_of(g * SUB, SUB), SUB)
+        hb, he = t_ref[HB, rows, :], t_ref[HE, rows, :]
+        from_y = jnp.where(t_ref[B, rows, :] > 0.0, y_down, y_up)
+        from_z = jnp.where(t_ref[E, rows, :] > 0.0, z_down, z_up)
+        for x in range(width):
+            s = s_ref[x, rows, :]
+            sy = jnp.take_along_axis(s, from_y, axis=1, mode="promise_in_bounds")
+            sz = jnp.take_along_axis(s, from_z, axis=1, mode="promise_in_bounds")
+            drive_ref[x, rows, :] = pseudo_rate * s + hb * sy + he * sz
+        return carry
+
+    lax.fori_loop(0, count // SUB, step, 0, unroll=8)
+
+
 def kinetic_kernel(
-    peers, me_ref, before_ref, m_ref, after_ref, f_ref, t_ref, rate_ref, wall_ref, state_ref, rden_ref,
+    peers, me_ref, before_ref, m_ref, after_ref, f_ref, t_ref, rate_ref, wall_ref, drive_ref, rden_ref,
     s_ref, c_ref, macro_ref, pad_ref, cell_ref, field_ref, total_ref,
 ):
     width, count = s_ref.shape[0], s_ref.shape[1]
@@ -258,12 +288,12 @@
     cells = cell_ref[...].astype(jnp.bfloat16)
 
     def mass(r, acc):
-        some = f_ref[:, r, :].astype(jnp.bfloat16)
-        power = lax.dot_general(some, cells, (((0,), (0,)), ((), ())), preferred_element_type=jnp.float32)
+        some = f_ref[pl.ds(pl.multiple_of(r * LANES, LANES), LANES), :]
+        power = jnp.dot(some, cells, preferred_element_type=jnp.float32)
         weight = jnp.exp2(power)
         return acc + jnp.sum(weight.reshape(LANES // SUB, SUB, width * LANES), axis=0)
 
-    acc = lax.fori_loop(0, f_ref.shape[1], mass, jnp.zeros((SUB, width * LANES), jnp.float32))
+    acc = lax.fori_loop(0, f_ref.shape[0] // LANES, mass, jnp.zeros((SUB, width * LANES), jnp.float32), unroll=8)
     acc = jnp.sum(acc, axis=0, keepdims=True)
     for x in range(width):
         total_ref[x : x + 1, :] = acc[:, x * LANES : (x + 1) * LANES]
@@ -282,22 +312,19 @@
         def ahead(g, carry):
             rows = pl.ds(pl.multiple_of(g * SUB, SUB), SUB)
             a, b, e = (t_ref[k, rows, :] for k in (A, B, E))
-            s = state_ref[x, rows, :]
             cx, cy, cz = a - ux, b - uy, e - uz
             square = cx * cx + cy * cy + cz * cz
             expo = jnp.exp2(square * power)
             flux = cx * qx + cy * qy + cz * qz
             target = (expo * maxwell) * (1.0 + flux * (square * inv - 5.0)) + rest * t_ref[REST, rows, :]
-            driving = pseudo_rate * s + t_ref[HB, rows, :] * jnp.where(b > 0.0, y_less(s), y_more(s))
-            driving = driving + t_ref[HE, rows, :] * jnp.where(e > 0.0, z_less(s), z_more(s))
             rden = rden_ref[x, rows, :]
-            value = (driving + target) * rden
+            value = (drive_ref[x, rows, :] + target) * rden
             if x:
                 value = value + (t_ref[FA, rows, :] * rden) * s_ref[x - 1, rows, :]
             s_ref[x, rows, :] = value
             return carry
 
-        lax.fori_loop(0, count // SUB, ahead, 0, unroll=2)
+        lax.fori_loop(0, count // SUB, ahead, 0, unroll=16)
 
     def back(g, carry):
         rows = pl.ds(pl.multiple_of(g * SUB, SUB), SUB)
@@ -310,7 +337,7 @@
         c_ref[rows, :] = jnp.where(t_ref[A, rows, :] >= 0.0, last, value)
         return carry
 
-    lax.fori_loop(0, count // SUB, back, 0, unroll=2)
+    lax.fori_loop(0, count // SUB, back, 0, unroll=4)
 
 
 def entering(peers, me, t_ref, c_ref, g_ref, flow_ref, enter_ref):
@@ -448,14 +475,21 @@
         m, extra = reduce_over("vel", m.reshape(13 * width, cells), extra)
         m = m.reshape(13, width, cells)
         if repeat == 0:
-            everyone = f32(FEATURES, extra.shape[0] * extra.shape[1] // 4, LANES)
-            features = run(features_kernel, everyone, (extra,), scalar=False)
+            lines = extra.shape[0] * extra.shape[1] // 4
+            features = run(
+                features_kernel,
+                jax.ShapeDtypeStruct((lines * LANES, FEATURES), jnp.bfloat16),
+                (extra,),
+                scratch=(pltpu.VMEM((lines, FEATURES, LANES), jnp.float32),),
+                scalar=False,
+            )
             extra = None
+        drive = run(transport_kernel, f32(width, count, cells), (table, state), scalar=False)
         before, after = neighbours("gx", m, HALO)
         local, carry, macro = run(
             functools.partial(kinetic_kernel, peers),
             (f32(width, count, cells), f32(count, cells), f32(5, width, cells)),
-            (me, before, m, after, features, table, rate, wall, state, rden),
+            (me, before, m, after, features, table, rate, wall, drive, rden),
             scratch=(
                 pltpu.VMEM((13, width + 2 * SUB, cells), jnp.float32),
                 pltpu.VMEM((FEATURES, width * cells), jnp.float32),

time: 142 us -> 95.4 us (0.67)
  Pallas kernels: 78.2 us -> 33 us
  starting transfers between devices: 23.9 us -> 21.2 us
  local copies, waits for them, and re-layouts: 3.11 us -> 4.7 us
    pallas_call x7 -> x9, Pallas kernels: 78.2 us -> 33 us  [run(): pl.pallas_call(kernel, out_shape=out_shape, in_specs=([smem] if scalar el...]
    ppermute x6, starting transfers between devices: 7.91 us -> 5.5 us  [gather_over(): got = lax.ppermute(blocks, axis, [(i, i ^ bit) for i in range(size)])]
    unnamed x14, local copies, waits for them, and re-layouts: 2.93 us -> 4.51 us
    ppermute x2, waiting for transfers between devices: 1.56 us -> 0.01 us  [neighbours(): near = lax.ppermute(jnp.where(odd, first, last), axis, near)]
  transfers between devices with their start and end apart: 18 -> 18, of which waited for: 12 -> 10; matrix products, arithmetic and copies ran while one was open for 1% -> 2% of each run, Pallas kernels for 4% -> 13%
where the time goes in v1:
time: 95.4 us; the launch traced here: 95 us
  Pallas kernels  33 us (35%)
  waiting for transfers between devices  32.6 us (34%)
  starting transfers between devices  21.2 us (22%)
  local copies, waits for them, and re-layouts  4.7 us (5%)
  other arithmetic  2.6 us (3%)
  between operations  0.97 us (1%)
    pallas_call x9, Pallas kernels, run(): pl.pallas_call(kernel, out_shape=out_shape, in_specs=([smem] if scalar el...  33 us
    ppermute x6, waiting for transfers between devices, gather_over(): got = lax.ppermute(blocks, axis, [(i, i ^ bit) for i in range(size)])  18.5 us
    ppermute x8, waiting for transfers between devices, reduce_over(): got.append(lax.ppermute(sent, axis, pairs))  14 us
    ppermute x8, starting transfers between devices, reduce_over(): got.append(lax.ppermute(sent, axis, pairs))  10.7 us
    ppermute x6, starting transfers between devices, gather_over(): got = lax.ppermute(blocks, axis, [(i, i ^ bit) for i in range(size)])  5.5 us
    unnamed x14, local copies, waits for them, and re-layouts  4.51 us
    ppermute x2, starting transfers between devices, neighbours(): near = lax.ppermute(jnp.where(odd, first, last), axis, near)  3.67 us
  transfers between devices with their start and end apart: 18, of which 10 were waited for; matrix products, arithmetic and copies ran while one was open for 2% of the time, Pallas kernels for 13%

profile of v1, /device:TPU:0, one launch (start us, length us, event | category | flops | bytes accessed | tf_op | source)
XLA Modules:
  0.0 95.0 jit_solution(10733463580128790277)
XLA Ops:
  0.6 0.0 copy-start.4
  0.6 0.8 multiply_add_fusion.rate_ref
  1.4 3.0 %collective-permute-start.6 = (f32[1,8,128]{2,1,0:T(8,128)S(1)}, f32[1,8,128]{2,1,0:T(8,128)S(1)}, u32[]{:S(2)}, u32[]{:S(2)}) collective-permute-start(f32[1,8,128]{2,1,0:T(8,128)S(1)} %bitcast.28), channel_id=1, source_target_pairs={{0,2},{1,3},{2,0},{3,1},{4,6},{5,7},{6,4},{7,5},{8,10},{9,11},{10,... | collective-permute-start | bytes 12296 | tf_op jit(solution)/shard_map/ppermute | solution.py:422
  4.4 0.7 pad_maximum_fusion.8
  5.1 0.1 pad.28.clone
  5.2 0.8 maximum_maximum_fusion.v_ref
  6.0 0.0 copy-start.1
  6.0 1.6 %copy-done.1 = f32[512,8,128]{2,1,0:T(8,128)S(1)} copy-done((f32[512,8,128]{2,1,0:T(8,128)S(1)}, f32[512,8,128]{2,1,0:T(8,128)}, u32[]{:S(2)}) %copy-start.1) | copy-done | bytes 2097176
  7.6 4.3 %shard_map.77 = (f32[13,8,128]{2,1,0:T(8,128)S(1)}, f32[10,512,128]{2,1,0:T(8,128)S(1)}, f32[8,512,128]{2,1,0:T(8,128)S(1)}) custom-call(f32[8,512]{1,0:T(8,128)S(1)} %maximum_maximum_fusion.v_ref, f32[512,8,128]{2,1,0:T(8,128)S(1)} %copy-done.1), custom_call_target="tpu_custom_call" | custom-call | tf_op jit(solution)/shard_map/pallas_call | solution.py:452
  11.8 0.0 copy-start.2
  11.9 1.3 %copy-done.2 = f32[8,512,128]{2,1,0:T(8,128)} copy-done((f32[8,512,128]{2,1,0:T(8,128)}, f32[8,512,128]{2,1,0:T(8,128)S(1)}, u32[]{:S(2)}) %copy-start.2) | copy-done | bytes 2097176
  13.2 1.5 %collective-permute-start = (f32[120,128]{1,0:T(8,128)S(1)}, f32[120,128]{1,0:T(8,128)S(1)}, u32[]{:S(2)}, u32[]{:S(2)}) collective-permute-start(f32[120,128]{1,0:T(8,128)S(1)} %pad_maximum_fusion.5), channel_id=1, source_target_pairs={{0,4},{4,0},{8,12},{12,8},{16,20},{20,16},{24,28},{28,24},{1,5},{5... | collective-permute-start | bytes 184328 | tf_op jit(solution)/shard_map/ppermute | solution.py:407
  14.7 0.0 collective-permute-done.6
  14.7 0.1 collective-permute-start.7
  14.8 0.0 copy-done.4
  14.8 0.0 copy-start.3
  14.8 1.6 %copy-done.3 = f32[8,512,128]{2,1,0:T(8,128)S(1)} copy-done((f32[8,512,128]{2,1,0:T(8,128)S(1)}, f32[8,512,128]{2,1,0:T(8,128)}, u32[]{:S(2)}) %copy-start.3) | copy-done | bytes 2097176
  16.4 2.6 %shard_map.79.drive_ref = f32[8,512,128]{2,1,0:T(8,128)S(1)} custom-call(f32[10,512,128]{2,1,0:T(8,128)S(1)} %get-tuple-element.15.t_ref, f32[8,512,128]{2,1,0:T(8,128)S(1)} %copy-done.3), custom_call_target="tpu_custom_call" | custom-call | tf_op jit(solution)/shard_map/pallas_call | solution.py:452
  19.1 0.0 collective-permute-done.7
  19.1 1.9 %shard_map.80 = (f32[8,512,128]{2,1,0:T(8,128)S(1)}, f32[8,512,128]{2,1,0:T(8,128)S(1)}, f32[4,512,128]{2,1,0:T(8,128)S(1)}) custom-call(s32[1]{0:T(128)} %bitcast.me_ref, f32[10,512,128]{2,1,0:T(8,128)S(1)} %get-tuple-element.15.t_ref, f32[4,8,128]{2,1,0:T(8,128)S(1)} %pad_maximum_fusion.7.rate_ref), custom_call_target="tpu_custom_call" | custom-call | tf_op jit(solution)/shard_map/pallas_call | solution.py:452
  21.0 0.0 collective-permute-done
  21.1 3.7 %collective-permute-start.3 = (f32[136,128]{1,0:T(8,128)S(1)}, f32[136,128]{1,0:T(8,128)S(1)}, u32[]{:S(2)}, u32[]{:S(2)}) collective-permute-start(f32[136,128]{1,0:T(8,128)S(1)} %pad_maximum_fusion.4), channel_id=1, source_target_pairs={{0,24},{4,28},{8,0},{12,4},{16,8},{20,12},{24,16},{28,20},{1,25},{... | collective-permute-start | bytes 208904 | tf_op jit(solution)/shard_map/ppermute | solution.py:407
  24.8 0.0 collective-permute-start.2
  24.8 1.0 %collective-permute-start.1 = (f32[136,128]{1,0:T(8,128)S(1)}, f32[136,128]{1,0:T(8,128)S(1)}, u32[]{:S(2)}, u32[]{:S(2)}) collective-permute-start(f32[136,128]{1,0:T(8,128)S(1)} %pad_maximum_fusion.4), channel_id=1, source_target_pairs={{0,8},{4,12},{8,16},{12,20},{16,24},{20,28},{24,0},{28,4},{1,9},{5... | collective-permute-start | bytes 208904 | tf_op jit(solution)/shard_map/ppermute | solution.py:407
  25.8 1.6 %collective-permute-done.3 = f32[136,128]{1,0:T(8,128)S(1)} collective-permute-done((f32[136,128]{1,0:T(8,128)S(1)}, f32[136,128]{1,0:T(8,128)S(1)}, u32[]{:S(2)}, u32[]{:S(2)}) %collective-permute-start.3) | collective-permute-done | bytes 69664 | tf_op jit(solution)/shard_map/ppermute | solution.py:407
  27.4 4.8 %collective-permute-done.2 = f32[136,128]{1,0:T(8,128)S(1)} collective-permute-done((f32[136,128]{1,0:T(8,128)S(1)}, f32[136,128]{1,0:T(8,128)S(1)}, u32[]{:S(2)}, u32[]{:S(2)}) %collective-permute-start.2) | collective-permute-done | bytes 69664 | tf_op jit(solution)/shard_map/ppermute | solution.py:407
  32.2 0.0 collective-permute-done.1
  32.2 0.7 collective-permute-start.5
  32.9 2.0 %collective-permute-start.4 = (f32[13,3,128]{2,1,0:T(4,128)S(1)}, f32[13,3,128]{2,1,0:T(4,128)S(1)}, u32[]{:S(2)}, u32[]{:S(2)}) collective-permute-start(f32[13,3,128]{2,1,0:T(4,128)S(1)} %get-tuple-element.39), channel_id=1, source_target_pairs={{0,1},{1,0},{2,3},{3,2},{4,5},{5,4},{6,7},{7,6},{8,9},{9,8},{10,11... | collective-permute-start | bytes 59912 | tf_op jit(solution)/shard_map/ppermute | solution.py:435
  34.9 1.2 %shard_map.78.f_ref = bf16[4096,32]{1,0:T(8,128)(2,1)S(1)} custom-call(f32[8,16,128]{2,1,0:T(8,128)S(1)} %constant_dynamic-update-slice_fusion.v_ref), custom_call_target="tpu_custom_call" | custom-call | tf_op jit(solution)/shard_map/pallas_call | solution.py:452
  36.1 0.0 collective-permute-done.5
  36.1 0.0 collective-permute-done.4
  36.2 6.5 %shard_map.81 = (f32[8,512,128]{2,1,0:T(8,128)S(1)}, f32[512,128]{1,0:T(8,128)S(1)}, f32[5,8,128]{2,1,0:T(8,128)}) custom-call(s32[1]{0:T(128)} %bitcast.me_ref, f32[13,3,128]{2,1,0:T(4,128)S(1)} %get-tuple-element.37.before_ref, f32[13,8,128]{2,1,0:T(8,128)S(1)} %fusion.m_ref, f32[13,3,128]{2,1,0:T(4,128)S(1)} %get-tuple-element.36.after_ref, ...), custom_call_target="tpu_custom_call" | custom-call | tf_op jit(solution)/shard_map/pallas_call | solution.py:452
  42.7 0.0 copy-start
  42.7 1.8 %collective-permute-start.8 = (f32[1,512,128]{2,1,0:T(8,128)S(1)}, f32[1,512,128]{2,1,0:T(8,128)S(1)}, u32[]{:S(2)}, u32[]{:S(2)}) collective-permute-start(f32[1,512,128]{2,1,0:T(8,128)S(1)} %bitcast.24), channel_id=1, source_target_pairs={{0,2},{1,3},{2,0},{3,1},{4,6},{5,7},{6,4},{7,5},{8,10},{9,11},{10,... | collective-permute-start | bytes 786440 | tf_op jit(solution)/shard_map/ppermute | solution.py:422
  44.5 7.0 %collective-permute-done.8 = f32[1,512,128]{2,1,0:T(8,128)S(1)} collective-permute-done((f32[1,512,128]{2,1,0:T(8,128)S(1)}, f32[1,512,128]{2,1,0:T(8,128)S(1)}, u32[]{:S(2)}, u32[]{:S(2)}) %collective-permute-start.8) | collective-permute-done | bytes 262176 | tf_op jit(solution)/shard_map/ppermute | solution.py:422
  51.6 0.2 collective-permute-start.9
  51.8 1.7 %collective-permute-done.9 = f32[2,512,128]{2,1,0:T(8,128)S(1)} collective-permute-done((f32[2,512,128]{2,1,0:T(8,128)S(1)}, f32[2,512,128]{2,1,0:T(8,128)S(1)}, u32[]{:S(2)}, u32[]{:S(2)}) %collective-permute-start.9) | collective-permute-done | bytes 524320 | tf_op jit(solution)/shard_map/ppermute | solution.py:422
  53.6 0.1 pad_maximum_fusion.c_ref
  53.7 0.0 copy-done
  53.7 3.8 %shard_map.82 = (f32[13,8,128]{2,1,0:T(8,128)S(1)}, f32[8,512,128]{2,1,0:T(8,128)S(1)}) custom-call(s32[1]{0:T(128)} %bitcast.me_ref, f32[10,512,128]{2,1,0:T(8,128)S(1)} %get-tuple-element.15.t_ref, f32[4,512,128]{2,1,0:T(8,128)S(1)} %pad_maximum_fusion.c_ref, f32[4,512,128]{2,1,0:T(8,128)S(1)} %get-tuple-element.20.g_ref, f32[2,512,128]{2,1,0:T(8,128)S(1)} %copy-done, ...), custom_call_target="tpu_custom_call" | custom-call | tf_op jit(solution)/shard_map/pallas_call | solution.py:452
  57.4 0.6 collective-permute-start.10
  58.0 3.6 %collective-permute-done.10 = f32[104,128]{1,0:T(8,128)S(1)} collective-permute-done((f32[104,128]{1,0:T(8,128)S(1)}, f32[104,128]{1,0:T(8,128)S(1)}, u32[]{:S(2)}, u32[]{:S(2)}) %collective-permute-start.10) | collective-permute-done | bytes 53280 | tf_op jit(solution)/shard_map/ppermute | solution.py:407
  61.7 1.4 %collective-permute-start.13 = (f32[104,128]{1,0:T(8,128)S(1)}, f32[104,128]{1,0:T(8,128)S(1)}, u32[]{:S(2)}, u32[]{:S(2)}) collective-permute-start(f32[104,128]{1,0:T(8,128)S(1)} %bitcast_add_fusion), channel_id=1, source_target_pairs={{0,24},{4,28},{8,0},{12,4},{16,8},{20,12},{24,16},{28,20},{1,25},{... | collective-permute-start | bytes 159752 | tf_op jit(solution)/shard_map/ppermute | solution.py:407
  63.1 0.5 collective-permute-start.12
  63.6 1.9 %collective-permute-start.11 = (f32[104,128]{1,0:T(8,128)S(1)}, f32[104,128]{1,0:T(8,128)S(1)}, u32[]{:S(2)}, u32[]{:S(2)}) collective-permute-start(f32[104,128]{1,0:T(8,128)S(1)} %bitcast_add_fusion), channel_id=1, source_target_pairs={{0,8},{4,12},{8,16},{12,20},{16,24},{20,28},{24,0},{28,4},{1,9},{5... | collective-permute-start | bytes 159752 | tf_op jit(solution)/shard_map/ppermute | solution.py:407
  65.6 0.4 collective-permute-done.13
  66.0 2.9 %collective-permute-done.12 = f32[104,128]{1,0:T(8,128)S(1)} collective-permute-done((f32[104,128]{1,0:T(8,128)S(1)}, f32[104,128]{1,0:T(8,128)S(1)}, u32[]{:S(2)}, u32[]{:S(2)}) %collective-permute-start.12) | collective-permute-done | bytes 53280 | tf_op jit(solution)/shard_map/ppermute | solution.py:407
  68.8 0.7 collective-permute-done.11
  69.6 0.7 collective-permute-start.15
  70.3 1.7 %collective-permute-start.14 = (f32[13,3,128]{2,1,0:T(4,128)S(1)}, f32[13,3,128]{2,1,0:T(4,128)S(1)}, u32[]{:S(2)}, u32[]{:S(2)}) collective-permute-start(f32[13,3,128]{2,1,0:T(4,128)S(1)} %get-tuple-element.35), channel_id=1, source_target_pairs={{0,1},{1,0},{2,3},{3,2},{4,5},{5,4},{6,7},{7,6},{8,9},{9,8},{10,11... | collective-permute-start | bytes 59912 | tf_op jit(solution)/shard_map/ppermute | solution.py:435
  72.0 2.7 %shard_map.83.drive_ref = f32[8,512,128]{2,1,0:T(8,128)S(1)} custom-call(f32[10,512,128]{2,1,0:T(8,128)S(1)} %get-tuple-element.15.t_ref, f32[8,512,128]{2,1,0:T(8,128)S(1)} %get-tuple-element.24.s_ref), custom_call_target="tpu_custom_call" | custom-call | tf_op jit(solution)/shard_map/pallas_call | solution.py:452
  74.6 0.0 collective-permute-done.15
  74.6 0.0 collective-permute-done.14
  74.7 6.6 %shard_map.84 = (f32[8,512,128]{2,1,0:T(8,128)S(1)}, f32[512,128]{1,0:T(8,128)S(1)}, f32[5,8,128]{2,1,0:T(8,128)}) custom-call(s32[1]{0:T(128)} %bitcast.me_ref, f32[13,3,128]{2,1,0:T(4,128)S(1)} %get-tuple-element.33.before_ref, f32[13,8,128]{2,1,0:T(8,128)S(1)} %add_bitcast_fusion.m_ref, f32[13,3,128]{2,1,0:T(4,128)S(1)} %get-tuple-element.32.after_ref, ...), custom_call_target="tpu_custom_call" | custom-call | tf_op jit(solution)/shard_map/pallas_call | solution.py:452
  81.2 0.4 collective-permute-start.16
  81.6 7.8 %collective-permute-done.16 = f32[1,512,128]{2,1,0:T(8,128)S(1)} collective-permute-done((f32[1,512,128]{2,1,0:T(8,128)S(1)}, f32[1,512,128]{2,1,0:T(8,128)S(1)}, u32[]{:S(2)}, u32[]{:S(2)}) %collective-permute-start.16) | collective-permute-done | bytes 262176 | tf_op jit(solution)/shard_map/ppermute | solution.py:422
  89.5 0.1 collective-permute-start.17
  89.6 1.9 %collective-permute-done.17 = f32[2,512,128]{2,1,0:T(8,128)S(1)} collective-permute-done((f32[2,512,128]{2,1,0:T(8,128)S(1)}, f32[2,512,128]{2,1,0:T(8,128)S(1)}, u32[]{:S(2)}, u32[]{:S(2)}) %collective-permute-start.17) | collective-permute-done | bytes 524320 | tf_op jit(solution)/shard_map/ppermute | solution.py:422
  91.5 0.1 pad_maximum_fusion.1.c_ref
  91.6 3.4 %shard_map.85 = f32[512,8,128]{2,1,0:T(8,128)} custom-call(s32[1]{0:T(128)} %bitcast.me_ref, f32[10,512,128]{2,1,0:T(8,128)S(1)} %get-tuple-element.15.t_ref, f32[4,512,128]{2,1,0:T(8,128)S(1)} %pad_maximum_fusion.1.c_ref, f32[4,512,128]{2,1,0:T(8,128)S(1)} %get-tuple-element.20.g_ref, f32[2,512,128]{2,1,0:T(8,128)S(1)} %copy-done, ...), custom_call_target="tpu_custom_call" | custom-call | tf_op jit(solution)/shard_map/pallas_call | solution.py:452
  (31 shorter events, 0.3 us)
Async XLA Ops:
  0.6 14.2 %copy-start.4 = (s32[8,128]{1,0:T(8,128)S(1)}, s32[8,128]{1,0:T(8,128)}, u32[]{:S(2)}) copy-start(s32[8,128]{1,0:T(8,128)} %param.10) | copy-start | bytes 12292
  1.4 13.3 %collective-permute-start.6 = (f32[1,8,128]{2,1,0:T(8,128)S(1)}, f32[1,8,128]{2,1,0:T(8,128)S(1)}, u32[]{:S(2)}, u32[]{:S(2)}) collective-permute-start(f32[1,8,128]{2,1,0:T(8,128)S(1)} %bitcast.28), channel_id=1, source_target_pairs={{0,2},{1,3},{2,0},{3,1},{4,6},{5,7},{6,4},{7,5},{8,10},{9,11},{10,... | collective-permute-start | bytes 12296 | tf_op jit(solution)/shard_map/ppermute | solution.py:422
  6.0 1.6 %copy-start.1 = (f32[512,8,128]{2,1,0:T(8,128)S(1)}, f32[512,8,128]{2,1,0:T(8,128)}, u32[]{:S(2)}) copy-start(f32[512,8,128]{2,1,0:T(8,128)} %dist_ref.1) | copy-start | bytes 6291460
  11.8 1.3 %copy-start.2 = (f32[8,512,128]{2,1,0:T(8,128)}, f32[8,512,128]{2,1,0:T(8,128)S(1)}, u32[]{:S(2)}) copy-start(f32[8,512,128]{2,1,0:T(8,128)S(1)} %get-tuple-element.17.s_ref) | copy-start | bytes 6291460
  13.2 7.9 %collective-permute-start = (f32[120,128]{1,0:T(8,128)S(1)}, f32[120,128]{1,0:T(8,128)S(1)}, u32[]{:S(2)}, u32[]{:S(2)}) collective-permute-start(f32[120,128]{1,0:T(8,128)S(1)} %pad_maximum_fusion.5), channel_id=1, source_target_pairs={{0,4},{4,0},{8,12},{12,8},{16,20},{20,16},{24,28},{28,24},{1,5},{5... | collective-permute-start | bytes 184328 | tf_op jit(solution)/shard_map/ppermute | solution.py:407
  14.7 4.4 %collective-permute-start.7 = (f32[2,8,128]{2,1,0:T(8,128)S(1)}, f32[2,8,128]{2,1,0:T(8,128)S(1)}, u32[]{:S(2)}, u32[]{:S(2)}) collective-permute-start(f32[2,8,128]{2,1,0:T(8,128)S(1)} %pad_maximum_fusion.9), channel_id=1, source_target_pairs={{0,1},{1,0},{2,3},{3,2},{4,5},{5,4},{6,7},{7,6},{8,9},{9,8},{10,11... | collective-permute-start | bytes 24584 | tf_op jit(solution)/shard_map/ppermute | solution.py:422
  14.8 1.6 %copy-start.3 = (f32[8,512,128]{2,1,0:T(8,128)S(1)}, f32[8,512,128]{2,1,0:T(8,128)}, u32[]{:S(2)}) copy-start(f32[8,512,128]{2,1,0:T(8,128)} %copy-done.2) | copy-start | bytes 6291460
  21.1 6.3 %collective-permute-start.3 = (f32[136,128]{1,0:T(8,128)S(1)}, f32[136,128]{1,0:T(8,128)S(1)}, u32[]{:S(2)}, u32[]{:S(2)}) collective-permute-start(f32[136,128]{1,0:T(8,128)S(1)} %pad_maximum_fusion.4), channel_id=1, source_target_pairs={{0,24},{4,28},{8,0},{12,4},{16,8},{20,12},{24,16},{28,20},{1,25},{... | collective-permute-start | bytes 208904 | tf_op jit(solution)/shard_map/ppermute | solution.py:407
  24.8 7.4 %collective-permute-start.2 = (f32[136,128]{1,0:T(8,128)S(1)}, f32[136,128]{1,0:T(8,128)S(1)}, u32[]{:S(2)}, u32[]{:S(2)}) collective-permute-start(f32[136,128]{1,0:T(8,128)S(1)} %pad_maximum_fusion.4), channel_id=1, source_target_pairs={{0,16},{4,20},{8,24},{12,28},{16,0},{20,4},{24,8},{28,12},{1,17},{... | collective-permute-start | bytes 208904 | tf_op jit(solution)/shard_map/ppermute | solution.py:407
  24.8 7.4 %collective-permute-start.1 = (f32[136,128]{1,0:T(8,128)S(1)}, f32[136,128]{1,0:T(8,128)S(1)}, u32[]{:S(2)}, u32[]{:S(2)}) collective-permute-start(f32[136,128]{1,0:T(8,128)S(1)} %pad_maximum_fusion.4), channel_id=1, source_target_pairs={{0,8},{4,12},{8,16},{12,20},{16,24},{20,28},{24,0},{28,4},{1,9},{5... | collective-permute-start | bytes 208904 | tf_op jit(solution)/shard_map/ppermute | solution.py:407
  32.2 3.9 %collective-permute-start.5 = (f32[13,3,128]{2,1,0:T(4,128)S(1)}, f32[13,3,128]{2,1,0:T(4,128)S(1)}, u32[]{:S(2)}, u32[]{:S(2)}) collective-permute-start(f32[13,3,128]{2,1,0:T(4,128)S(1)} %get-tuple-element.38), channel_id=1, source_target_pairs={{1,2},{2,1},{5,6},{6,5},{9,10},{10,9},{13,14},{14,13},{17,18},{18,... | collective-permute-start | bytes 59912 | tf_op jit(solution)/shard_map/ppermute | solution.py:436
  32.9 3.2 %collective-permute-start.4 = (f32[13,3,128]{2,1,0:T(4,128)S(1)}, f32[13,3,128]{2,1,0:T(4,128)S(1)}, u32[]{:S(2)}, u32[]{:S(2)}) collective-permute-start(f32[13,3,128]{2,1,0:T(4,128)S(1)} %get-tuple-element.39), channel_id=1, source_target_pairs={{0,1},{1,0},{2,3},{3,2},{4,5},{5,4},{6,7},{7,6},{8,9},{9,8},{10,11... | collective-permute-start | bytes 59912 | tf_op jit(solution)/shard_map/ppermute | solution.py:435
  42.7 11.0 %copy-start = (f32[2,512,128]{2,1,0:T(8,128)S(1)}, f32[2,512,128]{2,1,0:T(8,128)}, u32[]{:S(2)}) copy-start(f32[2,512,128]{2,1,0:T(8,128)} %flow_ref.3) | copy-start | bytes 1572868
  42.7 8.8 %collective-permute-start.8 = (f32[1,512,128]{2,1,0:T(8,128)S(1)}, f32[1,512,128]{2,1,0:T(8,128)S(1)}, u32[]{:S(2)}, u32[]{:S(2)}) collective-permute-start(f32[1,512,128]{2,1,0:T(8,128)S(1)} %bitcast.24), channel_id=1, source_target_pairs={{0,2},{1,3},{2,0},{3,1},{4,6},{5,7},{6,4},{7,5},{8,10},{9,11},{10,... | collective-permute-start | bytes 786440 | tf_op jit(solution)/shard_map/ppermute | solution.py:422
  51.6 2.0 %collective-permute-start.9 = (f32[2,512,128]{2,1,0:T(8,128)S(1)}, f32[2,512,128]{2,1,0:T(8,128)S(1)}, u32[]{:S(2)}, u32[]{:S(2)}) collective-permute-start(f32[2,512,128]{2,1,0:T(8,128)S(1)} %pad_maximum_fusion.2), channel_id=1, source_target_pairs={{0,1},{1,0},{2,3},{3,2},{4,5},{5,4},{6,7},{7,6},{8,9},{9,8},{10,11... | collective-permute-start | bytes 1572872 | tf_op jit(solution)/shard_map/ppermute | solution.py:422
  57.4 4.2 %collective-permute-start.10 = (f32[104,128]{1,0:T(8,128)S(1)}, f32[104,128]{1,0:T(8,128)S(1)}, u32[]{:S(2)}, u32[]{:S(2)}) collective-permute-start(f32[104,128]{1,0:T(8,128)S(1)} %bitcast.31), channel_id=1, source_target_pairs={{0,4},{4,0},{8,12},{12,8},{16,20},{20,16},{24,28},{28,24},{1,5},{5... | collective-permute-start | bytes 159752 | tf_op jit(solution)/shard_map/ppermute | solution.py:407
  61.7 4.3 %collective-permute-start.13 = (f32[104,128]{1,0:T(8,128)S(1)}, f32[104,128]{1,0:T(8,128)S(1)}, u32[]{:S(2)}, u32[]{:S(2)}) collective-permute-start(f32[104,128]{1,0:T(8,128)S(1)} %bitcast_add_fusion), channel_id=1, source_target_pairs={{0,24},{4,28},{8,0},{12,4},{16,8},{20,12},{24,16},{28,20},{1,25},{... | collective-permute-start | bytes 159752 | tf_op jit(solution)/shard_map/ppermute | solution.py:407
  63.1 5.7 %collective-permute-start.12 = (f32[104,128]{1,0:T(8,128)S(1)}, f32[104,128]{1,0:T(8,128)S(1)}, u32[]{:S(2)}, u32[]{:S(2)}) collective-permute-start(f32[104,128]{1,0:T(8,128)S(1)} %bitcast_add_fusion), channel_id=1, source_target_pairs={{0,16},{4,20},{8,24},{12,28},{16,0},{20,4},{24,8},{28,12},{1,17},{... | collective-permute-start | bytes 159752 | tf_op jit(solution)/shard_map/ppermute | solution.py:407
  63.6 5.9 %collective-permute-start.11 = (f32[104,128]{1,0:T(8,128)S(1)}, f32[104,128]{1,0:T(8,128)S(1)}, u32[]{:S(2)}, u32[]{:S(2)}) collective-permute-start(f32[104,128]{1,0:T(8,128)S(1)} %bitcast_add_fusion), channel_id=1, source_target_pairs={{0,8},{4,12},{8,16},{12,20},{16,24},{20,28},{24,0},{28,4},{1,9},{5... | collective-permute-start | bytes 159752 | tf_op jit(solution)/shard_map/ppermute | solution.py:407
  69.6 5.1 %collective-permute-start.15 = (f32[13,3,128]{2,1,0:T(4,128)S(1)}, f32[13,3,128]{2,1,0:T(4,128)S(1)}, u32[]{:S(2)}, u32[]{:S(2)}) collective-permute-start(f32[13,3,128]{2,1,0:T(4,128)S(1)} %get-tuple-element.34), channel_id=1, source_target_pairs={{1,2},{2,1},{5,6},{6,5},{9,10},{10,9},{13,14},{14,13},{17,18},{18,... | collective-permute-start | bytes 59912 | tf_op jit(solution)/shard_map/ppermute | solution.py:436
  70.3 4.4 %collective-permute-start.14 = (f32[13,3,128]{2,1,0:T(4,128)S(1)}, f32[13,3,128]{2,1,0:T(4,128)S(1)}, u32[]{:S(2)}, u32[]{:S(2)}) collective-permute-start(f32[13,3,128]{2,1,0:T(4,128)S(1)} %get-tuple-element.35), channel_id=1, source_target_pairs={{0,1},{1,0},{2,3},{3,2},{4,5},{5,4},{6,7},{7,6},{8,9},{9,8},{10,11... | collective-permute-start | bytes 59912 | tf_op jit(solution)/shard_map/ppermute | solution.py:435
  81.2 8.2 %collective-permute-start.16 = (f32[1,512,128]{2,1,0:T(8,128)S(1)}, f32[1,512,128]{2,1,0:T(8,128)S(1)}, u32[]{:S(2)}, u32[]{:S(2)}) collective-permute-start(f32[1,512,128]{2,1,0:T(8,128)S(1)} %bitcast.21), channel_id=1, source_target_pairs={{0,2},{1,3},{2,0},{3,1},{4,6},{5,7},{6,4},{7,5},{8,10},{9,11},{10,... | collective-permute-start | bytes 786440 | tf_op jit(solution)/shard_map/ppermute | solution.py:422
  89.5 2.0 %collective-permute-start.17 = (f32[2,512,128]{2,1,0:T(8,128)S(1)}, f32[2,512,128]{2,1,0:T(8,128)S(1)}, u32[]{:S(2)}, u32[]{:S(2)}) collective-permute-start(f32[2,512,128]{2,1,0:T(8,128)S(1)} %pad_maximum_fusion.3), channel_id=1, source_target_pairs={{0,1},{1,0},{2,3},{3,2},{4,5},{5,4},{6,7},{7,6},{8,9},{9,8},{10,11... | collective-permute-start | bytes 1572872 | tf_op jit(solution)/shard_map/ppermute | solution.py:422

commit v2 on v1

v2 whole, which is shorter than its diff:
```python
import functools
import math

import jax
import jax.numpy as jnp
from jax import lax
from jax.experimental import pallas as pl
from jax.experimental.pallas import tpu as pltpu
from jax.sharding import PartitionSpec as P


NZ = 8
ITERS = 2
JACOBI = 2
HALO = JACOBI + 1
pseudo_rate = 0.5
source_gain = 0.5
diffusion = (0.6, 0.8, 0.8, 0.8, 1.0)
viscous_conduction_ratio = 2.0 / 3.0
wall_rate = 4.0
box_volume = 216.0
LOG2E = math.log2(math.e)
LANES = 128
SUB = 8
PAIRS = ((0, 0), (0, 1), (1, 0), (0, 2), (2, 0), (1, 1))
FEATURES = 32
A, B, E, W, HB, HE, BASE, FA, BA, REST = range(10)
TABLE = 10
CHUNKS = 2
BLOCKS = 2


SMEM = pl.BlockSpec(memory_space=pltpu.SMEM)
VMEM = pl.BlockSpec(memory_space=pltpu.VMEM)
PARAMS = pltpu.CompilerParams(vmem_limit_bytes=16 * 1024 * 1024)


def run(kernel, out_shape, args, scratch=(), scalar=True):
    return pl.pallas_call(
        kernel,
        out_shape=out_shape,
        in_specs=([SMEM] if scalar else []) + [VMEM] * (len(args) - (1 if scalar else 0)),
        out_specs=jax.tree.map(lambda _: VMEM, out_shape),
        scratch_shapes=scratch,
        compiler_params=PARAMS,
    )(*args)


def f32(*shape):
    return jax.ShapeDtypeStruct(shape, jnp.float32)


def add_moments(acc, s, t_ref, rows):
    a, b, e = (t_ref[k, rows, :] for k in (A, B, E))
    g = s * t_ref[W, rows, :]
    ga, gb, ge = g * a, g * b, g * e
    gaa, gbb, gee = ga * a, gb * b, ge * e
    gs = gaa + gbb + gee
    terms = (g, ga, gb, ge, gs, gaa, gbb, ga * b, ga * e, gb * e, gs * a, gs * b, gs * e)
    return tuple(old + new for old, new in zip(acc, terms))


def write_moments(m_ref, x, acc):
    for field, value in enumerate(acc):
        m_ref[field, x : x + 1, :] = jnp.sum(value, axis=0, keepdims=True)


def moments_loop(acc_ref, t_ref, first, groups, state_at):
    for x in range(acc_ref.shape[1]):

        def step(g, acc):
            rows = pl.ds(pl.multiple_of(g * SUB, SUB), SUB)
            table_rows = pl.ds(pl.multiple_of(first + g * SUB, SUB), SUB)
            return add_moments(acc, state_at(x, rows), t_ref, table_rows)

        acc = tuple(acc_ref[k, x] for k in range(13))
        acc = lax.fori_loop(0, groups, step, acc, unroll=4)
        for k, value in enumerate(acc):
            acc_ref[k, x] = value


def write_moments(m_ref, acc_ref):
    width = acc_ref.shape[1]
    for k in range(13):
        m_ref[k * width : (k + 1) * width, :] = jnp.sum(acc_ref[k], axis=1)


def first_kernel(
    extent, steps, v_ref, w_ref, collision_ref, solid_ref, dist_ref, m_ref, t_ref, rate_ref, wall_ref, vw_ref, acc_ref
):
    block, width = dist_ref.shape[0], dist_ref.shape[1]
    i = pl.program_id(0)
    start = pl.multiple_of(i * block, block)

    @pl.when(i == 0)
    def _():
        wall = solid_ref[...].astype(jnp.float32)
        wall_ref[...] = wall
        rate_ref[...] = collision_ref[...] + wall_rate * wall
        acc_ref[...] = jnp.zeros_like(acc_ref)
        vw_ref[0:3, :] = v_ref[...]
        vw_ref[3:4, :] = w_ref[...]
        vw_ref[4:8, :] = jnp.zeros((4, vw_ref.shape[1]), jnp.float32)
        lines = vw_ref.shape[1] // LANES
        for k in range(4):
            for j in range(lines):
                row = 13 * width + k * lines + j
                m_ref[row : row + 1, :] = vw_ref[k : k + 1, j * LANES : (j + 1) * LANES]

    part = max(block, LANES)

    @pl.when(start % part == 0)
    def _():
        here = pl.ds(pl.multiple_of(start, part), part)
        columns = vw_ref[:, here].T

        def wide(k):
            return jnp.broadcast_to(columns[:, k : k + 1], (part, LANES))

        a, b, e = wide(0), wide(1), wide(2)
        t_ref[A, here], t_ref[B, here], t_ref[E, here], t_ref[W, here] = a, b, e, wide(3)
        hb, he = 0.5 * jnp.abs(b), 0.5 * jnp.abs(e)
        t_ref[HB, here], t_ref[HE, here] = hb, he
        t_ref[BASE, here] = pseudo_rate + (hb + he) + jnp.abs(a) * extent
        t_ref[FA, here] = jnp.maximum(a, 0.0) * extent
        t_ref[BA, here] = jnp.maximum(-a, 0.0) * extent
        t_ref[REST, here] = (box_volume * (2.0 * math.pi) ** (-1.5)) * jnp.exp(-0.5 * (a * a + b * b + e * e))

    moments_loop(acc_ref, t_ref, start, block // SUB, lambda x, rows: dist_ref[rows, x, :])

    @pl.when(i == steps - 1)
    def _():
        write_moments(m_ref, acc_ref)


def gains_kernel(t_ref, rate_ref, rden_ref, p_ref):
    width, count = rden_ref.shape[0], rden_ref.shape[1]

    def step(g, carry):
        rows = pl.ds(pl.multiple_of(g * SUB, SUB), SUB)
        base = t_ref[BASE, rows, :]
        gain = t_ref[FA, rows, :] + t_ref[BA, rows, :]
        ahead = t_ref[A, rows, :] >= 0.0
        steps = []
        for x in range(width):
            rden = 1.0 / (base + rate_ref[x : x + 1, :])
            rden_ref[x, rows, :] = rden
            steps.append(gain * rden)
        up, down = [steps[0]], [steps[-1]]
        for x in range(1, width):
            up.append(up[-1] * steps[x])
            down.append(down[-1] * steps[width - 1 - x])
        for x in range(width):
            p_ref[x, rows, :] = jnp.where(ahead, up[x], down[width - 1 - x])
        return carry

    lax.fori_loop(0, count // SUB, step, 0, unroll=2)


def slabs_kernel(peers, width, me_ref, t_ref, c_ref, g_ref):
    count = g_ref.shape[1]
    below = c_ref.shape[1] - width
    me = me_ref[0]

    def step(g, carry):
        rows = pl.ds(pl.multiple_of(g * SUB, SUB), SUB)
        base = t_ref[BASE, rows, :]
        gain = t_ref[FA, rows, :] + t_ref[BA, rows, :]
        for d in range(peers):
            slab = jnp.ones_like(gain)
            for x in range(0, width, 2):
                product = base + c_ref[d ^ me, below + x : below + x + 1, :]
                power = gain
                if x + 1 < width:
                    product = product * (base + c_ref[d ^ me, below + x + 1 : below + x + 2, :])
                    power = power * gain
                slab = slab * (power / product)
            g_ref[d, rows, :] = slab
        return carry

    lax.fori_loop(0, count // SUB, step, 0, unroll=2)


def features_kernel(v_ref, f_ref, row_ref):
    blocks = v_ref.shape[0]
    part = v_ref.shape[1] // 4
    for k in range(blocks):
        a, b, e, w = (v_ref[k, i * part : (i + 1) * part, :] for i in range(4))
        sides = [split(value) for value in (a, b, e, a * a + b * b + e * e)]
        one, zero = jnp.ones_like(a), jnp.zeros_like(a)
        rows = [side[i] for side in sides for i, _ in PAIRS] + [one] * 3 + split(jnp.log2(w))
        rows = rows + [zero] * (FEATURES - len(rows))
        for i, row in enumerate(rows):
            for j in range(part):
                row_ref[k * part + j, i : i + 1, :] = row[j : j + 1, :]

    def turn(r, carry):
        where = pl.ds(pl.multiple_of(r * LANES, LANES), LANES)
        f_ref[where, :] = row_ref[r].T.astype(jnp.bfloat16)
        return carry

    lax.fori_loop(0, blocks * part, turn, 0, unroll=4)


def split(value):
    parts = []
    for _ in range(3):
        part = value.astype(jnp.bfloat16).astype(jnp.float32)
        parts.append(part)
        value = value - part
    return parts


def lane_z():
    return lax.broadcasted_iota(jnp.int32, (1, LANES), 1) % NZ


def y_less(v):
    return pltpu.roll(v, NZ, 1)


def y_more(v):
    return pltpu.roll(v, LANES - NZ, 1)


def z_less(v):
    return jnp.where(lane_z() == 0, pltpu.roll(v, LANES - NZ + 1, 1), pltpu.roll(v, 1, 1))


def z_more(v):
    return jnp.where(lane_z() == NZ - 1, pltpu.roll(v, NZ - 1, 1), pltpu.roll(v, LANES - 1, 1))


def dy(v):
    return 0.5 * (y_more(v) - y_less(v))


def dz(v):
    return 0.5 * (z_more(v) - z_less(v))


def x_less(v):
    return pltpu.roll(v, 1, 0)


def x_more(v):
    return pltpu.roll(v, v.shape[0] - 1, 0)


def fields_of(m):
    rho = m[0]
    inverse = 1.0 / rho
    u = [m[1 + i] * inverse for i in range(3)]
    square = u[0] * u[0] + u[1] * u[1] + u[2] * u[2]
    warm = (m[4] * inverse - square) * (1.0 / 3.0)
    force = rho * warm
    second = [[m[5], m[7], m[8]], [m[7], m[6], m[9]], [m[8], m[9], m[4] - m[5] - m[6]]]
    xx = second[0][0] - rho * u[0] * u[0] - force
    yy = second[1][1] - rho * u[1] * u[1] - force
    xy = second[0][1] - rho * u[0] * u[1]
    xz = second[0][2] - rho * u[0] * u[2]
    yz = second[1][2] - rho * u[1] * u[2]
    heat = []
    for i in range(3):
        inner = u[0] * second[i][0] + u[1] * second[i][1] + u[2] * second[i][2]
        heat.append(0.5 * (m[10 + i] - 2.0 * inner - u[i] * m[4] + 2.0 * rho * u[i] * square))
    return rho, inverse, u, warm, (xx, yy, xy, xz, yz), heat


def correction(rho, inverse, u, warm, stress, heat, inside):
    xx, yy, xy, xz, yz = stress
    zz = -(xx + yy)

    def dx(v):
        v = jnp.where(inside, v, 0.0)
        return 0.5 * (x_more(v) - x_less(v))

    source = [
        dx(rho * u[0]) + dy(rho * u[1]) + dz(rho * u[2]),
        dx(xx) + dy(xy) + dz(xz),
        dx(xy) + dy(yy) + dz(yz),
        dx(xz) + dy(yz) + dz(zz),
        dx(heat[0]) + dy(heat[1]) + dz(heat[2]),
    ]
    scale = [-source_gain * inverse] * 4 + [(-source_gain * 2.0 / 3.0) / (rho * warm)]
    source = [jnp.where(inside, s * c, 0.0) for s, c in zip(source, scale)]
    delta = source
    for _ in range(JACOBI):
        fresh = []
        for mu, s, d in zip(diffusion, source, delta):
            beside = x_less(d) + x_more(d) + y_less(d) + y_more(d) + z_less(d) + z_more(d)
            fresh.append(jnp.where(inside, (s + mu * beside) * (1.0 / (1.0 + 6.0 * mu)), 0.0))
        delta = fresh
    return delta


def transport_kernel(first, raw, t_ref, s_ref, drive_ref):
    width = drive_ref.shape[0]
    count = s_ref.shape[0] if raw else s_ref.shape[1]
    start = pl.program_id(0) * count
    lane = lax.broadcasted_iota(jnp.int32, (SUB, LANES), 1)
    z = lane % NZ
    y_down, y_up = (lane + LANES - NZ) % LANES, (lane + NZ) % LANES
    z_down, z_up = lane - z + (z + NZ - 1) % NZ, lane - z + (z + 1) % NZ

    def step(g, carry):
        rows = pl.ds(pl.multiple_of(g * SUB, SUB), SUB)
        out = pl.ds(pl.multiple_of(start + g * SUB, SUB), SUB)
        table_rows = pl.ds(pl.multiple_of(first + start + g * SUB, SUB), SUB)
        hb, he = t_ref[HB, table_rows, :], t_ref[HE, table_rows, :]
        from_y = jnp.where(t_ref[B, table_rows, :] > 0.0, y_down, y_up)
        from_z = jnp.where(t_ref[E, table_rows, :] > 0.0, z_down, z_up)
        for x in range(width):
            s = s_ref[rows, x, :] if raw else s_ref[x, rows, :]
            sy = jnp.take_along_axis(s, from_y, axis=1, mode="promise_in_bounds")
            sz = jnp.take_along_axis(s, from_z, axis=1, mode="promise_in_bounds")
            drive_ref[x, out, :] = pseudo_rate * s + hb * sy + he * sz
        return carry

    lax.fori_loop(0, count // SUB, step, 0, unroll=8)


def kinetic_kernel(
    peers, me_ref, before_ref, m_ref, after_ref, f_ref, t_ref, rate_ref, wall_ref, drive_ref, rden_ref,
    s_ref, c_ref, macro_ref, field_ref, pad_ref, cell_ref, total_ref,
):
    width, count = s_ref.shape[0], s_ref.shape[1]
    me = me_ref[0]
    tall = width + 2 * SUB
    own = slice(SUB, SUB + width)
    pad_ref[...] = jnp.ones_like(pad_ref)
    for k in range(13):
        pad_ref[k, SUB - HALO : SUB, :] = before_ref[k]
        pad_ref[k, own, :] = m_ref[k]
        pad_ref[k, SUB + width : SUB + width + HALO, :] = after_ref[k]
    row = lax.broadcasted_iota(jnp.int32, (tall, LANES), 0) + (me * width - SUB)
    inside = (row >= 0) & (row < peers * width)
    rho, inverse, u, warm, stress, heat = fields_of([pad_ref[k] for k in range(13)])
    delta = correction(rho, inverse, u, warm, stress, heat, inside)
    for k, value in enumerate(
        (rho * jnp.exp(delta[0]), u[0] + delta[1], u[1] + delta[2], u[2] + delta[3], warm * jnp.exp(delta[4]))
    ):
        pad_ref[k] = value
        macro_ref[k] = pad_ref[k, own, :]
    for k in range(3):
        pad_ref[5 + k] = heat[k]
    R, U, T = macro_ref[0], [macro_ref[1 + k] for k in range(3)], macro_ref[4]
    q = [pad_ref[5 + k, own, :] for k in range(3)]
    cold = 1.0 / T
    beta = (-0.5 * LOG2E) * cold
    alpha = [(LOG2E * cold) * U[k] for k in range(3)]
    gamma = beta * (U[0] * U[0] + U[1] * U[1] + U[2] * U[2])
    rows = [side[j] for side in (split(v) for v in (*alpha, beta)) for _, j in PAIRS]
    rows = rows + split(gamma) + [jnp.ones_like(T)] * 3
    rows = rows + [jnp.zeros_like(T)] * (FEATURES - len(rows))
    for i, value in enumerate(rows):
        for x in range(width):
            cell_ref[i : i + 1, x * LANES : (x + 1) * LANES] = value[x : x + 1, :]
    cells = cell_ref[...].astype(jnp.bfloat16)

    def mass(r, acc):
        some = f_ref[pl.ds(pl.multiple_of(r * LANES, LANES), LANES), :]
        power = jnp.dot(some, cells, preferred_element_type=jnp.float32)
        weight = jnp.exp2(power)
        return acc + jnp.sum(weight.reshape(LANES // SUB, SUB, width * LANES), axis=0)

    acc = lax.fori_loop(0, f_ref.shape[0] // LANES, mass, jnp.zeros((SUB, width * LANES), jnp.float32), unroll=8)
    acc = jnp.sum(acc, axis=0, keepdims=True)
    for x in range(width):
        total_ref[x : x + 1, :] = acc[:, x * LANES : (x + 1) * LANES]
    wall, rate = wall_ref[...], rate_ref[...]
    third = (1.0 - viscous_conduction_ratio) / (5.0 * R * T * T)
    values = [*U, beta, *(v * third for v in q), cold]
    values += [(1.0 - wall) * R * rate / total_ref[...], wall * R * rate]
    for k, value in enumerate(values):
        field_ref[k] = value

    sweep(0, field_ref, t_ref, drive_ref, rden_ref, s_ref, c_ref)
    c_ref[count : count + width, :] = rate


def sweep_kernel(first, t_ref, field_ref, drive_ref, rden_ref, s_ref, c_ref):
    sweep(first, field_ref, t_ref, drive_ref, rden_ref, s_ref, c_ref)


def sweep(first, field_ref, t_ref, drive_ref, rden_ref, s_ref, c_ref):
    width, count = s_ref.shape[0], s_ref.shape[1]

    def both(g):
        return (
            pl.ds(pl.multiple_of(g * SUB, SUB), SUB),
            pl.ds(pl.multiple_of(first + g * SUB, SUB), SUB),
        )

    for x in range(width):
        ux, uy, uz, power, qx, qy, qz, inv, maxwell, rest = (
            jnp.broadcast_to(field_ref[k, x : x + 1, :], (SUB, LANES)) for k in range(10)
        )

        def ahead(g, carry):
            rows, wide = both(g)
            a, b, e = (t_ref[k, wide, :] for k in (A, B, E))
            cx, cy, cz = a - ux, b - uy, e - uz
            square = cx * cx + cy * cy + cz * cz
            expo = jnp.exp2(square * power)
            flux = cx * qx + cy * qy + cz * qz
            target = (expo * maxwell) * (1.0 + flux * (square * inv - 5.0)) + rest * t_ref[REST, wide, :]
            rden = rden_ref[x, wide, :]
            value = (drive_ref[x, rows, :] + target) * rden
            if x:
                value = value + (t_ref[FA, wide, :] * rden) * s_ref[x - 1, rows, :]
            s_ref[x, rows, :] = value
            return carry

        lax.fori_loop(0, count // SUB, ahead, 0, unroll=16)

    def back(g, carry):
        rows, wide = both(g)
        ba = t_ref[BA, wide, :]
        value = s_ref[width - 1, rows, :]
        last = value
        for x in range(width - 2, -1, -1):
            value = s_ref[x, rows, :] + (ba * rden_ref[x, wide, :]) * value
            s_ref[x, rows, :] = value
        c_ref[rows, :] = jnp.where(t_ref[A, wide, :] >= 0.0, last, value)
        return carry

    lax.fori_loop(0, count // SUB, back, 0, unroll=4)


def entering(peers, me, first, rows, t_ref, c_ref, g_ref, flow_ref):
    wide = pl.ds(pl.multiple_of(first + rows.start, SUB), SUB)
    up, down = flow_ref[0, wide, :], flow_ref[1, wide, :]
    for d in range(peers - 1):
        up = jnp.where(d < me, g_ref[d, wide, :] * up + c_ref[d ^ me, rows, :], up)
    for d in range(peers - 1, 0, -1):
        down = jnp.where(d > me, g_ref[d, wide, :] * down + c_ref[d ^ me, rows, :], down)
    return jnp.where(t_ref[A, wide, :] >= 0.0, up, down)


def next_kernel(peers, first, me_ref, t_ref, c_ref, g_ref, flow_ref, s_ref, p_ref, *refs):
    partial_ref, (m_ref, state_ref, enter_ref, acc_ref) = refs[:-4], refs[-4:]
    count = s_ref.shape[1]
    me = me_ref[0]

    def enter(g, carry):
        rows = pl.ds(pl.multiple_of(g * SUB, SUB), SUB)
        enter_ref[rows, :] = entering(peers, me, first, rows, t_ref, c_ref, g_ref, flow_ref)
        return carry

    lax.fori_loop(0, count // SUB, enter, 0, unroll=2)
    acc_ref[...] = jnp.zeros_like(acc_ref)

    def state_at(x, rows):
        wide = pl.ds(pl.multiple_of(first + rows.start, SUB), SUB)
        s = s_ref[x, rows, :] + p_ref[x, wide, :] * enter_ref[rows, :]
        state_ref[x, rows, :] = s
        return s

    moments_loop(acc_ref, t_ref, first, count // SUB, state_at)
    write_moments(m_ref, acc_ref)
    if partial_ref:
        m_ref[...] += partial_ref[0][...]


def last_kernel(peers, first, me_ref, t_ref, c_ref, g_ref, flow_ref, s_ref, p_ref, *refs):
    out_ref = refs[-1]
    width, block = out_ref.shape[1], out_ref.shape[0]
    me = me_ref[0]
    start = pl.program_id(0) * block

    def step(g, carry):
        rows = pl.ds(pl.multiple_of(start + g * SUB, SUB), SUB)
        wide = pl.ds(pl.multiple_of(first + start + g * SUB, SUB), SUB)
        out = pl.ds(pl.multiple_of(g * SUB, SUB), SUB)
        enter = entering(peers, me, first, rows, t_ref, c_ref, g_ref, flow_ref)
        for x in range(width):
            out_ref[out, x, :] = s_ref[x, rows, :] + p_ref[x, wide, :] * enter
        return carry

    lax.fori_loop(0, block // SUB, step, 0, unroll=2)


def stages(size):
    found, stride = [], 1
    while size > 1:
        factor = next(f for f in range(2, size + 1) if size % f == 0)
        if factor == 2 and size % 4 == 0 and (stride > 1 or size % 8):
            factor = 4
        found.append((factor, stride))
        size, stride = size // factor, stride * factor
    return found


def reduce_over(axis, value, rows):
    size = lax.axis_size(axis)
    value, extra = value[:rows], value[None, rows:]
    done = []
    for factor, stride in stages(size):
        sent = jnp.concatenate([value, extra.reshape(-1, LANES)]) if extra.size else value
        got = []
        for turn in range(1, factor):
            pairs = []
            for i in range(size):
                digit = i // stride % factor
                pairs.append((i, i + ((digit + turn) % factor - digit) * stride))
            got.append(lax.ppermute(sent, axis, pairs))
        done.append(factor)
        for piece in got:
            value = value + piece[:rows]
        if extra.size:
            shape = (-1,) + extra.shape[1:]
            extra = jnp.concatenate([extra] + [piece[rows:].reshape(shape) for piece in got])
    return value, extra


def gather_over(axis, value):
    size = lax.axis_size(axis)
    blocks = value[None]
    order = [0]
    bit = size // 2
    while bit:
        got = lax.ppermute(blocks, axis, [(i, i ^ bit) for i in range(size)])
        blocks = jnp.concatenate([blocks, got])
        order = order + [k ^ bit for k in order]
        bit //= 2
    return jnp.concatenate([blocks[order.index(k)][None] for k in range(size)])


def neighbours(axis, value, width):
    size, me = lax.axis_size(axis), lax.axis_index(axis)
    odd = me % 2 == 1
    first, last = value[:, :width], value[:, value.shape[1] - width :]
    near = [(i, i ^ 1) for i in range(size)]
    far = [(i, i + 1) for i in range(1, size - 1, 2)]
    far = lax.ppermute(jnp.where(odd, last, first), axis, far + [(j, i) for i, j in far])
    near = lax.ppermute(jnp.where(odd, first, last), axis, near)
    return jnp.where(odd, near, far), jnp.where(odd, far, near)


def iteration(repeat, m, states, table, rate, wall, me, inflow, kept):
    width, cells = rate.shape
    count, peers = table.shape[1], lax.axis_size("gx")
    chunk = count // len(states)
    block = chunk // BLOCKS
    if repeat == 0:
        kept["gains"] = run(gains_kernel, (f32(width, count, cells),) * 2, (table, rate), scalar=False)
    rden, prefix = kept["gains"]
    drives = []
    for k, state in enumerate(states):
        kernel = functools.partial(transport_kernel, k * chunk, repeat == 0)
        at = (lambda i, k=k: (k * BLOCKS + i, 0, 0)) if repeat == 0 else None
        source = pl.BlockSpec((block, width, cells), at) if repeat == 0 else VMEM
        drives.append(
            pl.pallas_call(
                kernel,
                grid=(BLOCKS if repeat == 0 else 1,),
                out_shape=f32(width, chunk, cells),
                in_specs=[VMEM, source],
                out_specs=VMEM,
                compiler_params=PARAMS,
            )(table, state)
        )
    m, extra = reduce_over("vel", m, 13 * width)
    m = m.reshape(13, width, cells)
    before, after = neighbours("gx", m, HALO)
    if repeat == 0:
        total = extra.shape[0] * extra.shape[1] // 4
        kept["features"] = run(
            features_kernel,
            jax.ShapeDtypeStruct((total * LANES, FEATURES), jnp.bfloat16),
            (extra,),
            scratch=(pltpu.VMEM((total, FEATURES, LANES), jnp.float32),),
            scalar=False,
        )
    local, carry, macro, fields = run(
        functools.partial(kinetic_kernel, peers),
        (f32(width, chunk, cells), f32(chunk + width, cells), f32(5, width, cells), f32(10, width, cells)),
        (me, before, m, after, kept["features"], table, rate, wall, drives[0], rden),
        scratch=(
            pltpu.VMEM((13, width + 2 * SUB, cells), jnp.float32),
            pltpu.VMEM((FEATURES, width * cells), jnp.float32),
            pltpu.VMEM((width, cells), jnp.float32),
        ),
    )
    locals_, carries = [local], [gather_over("gx", carry)]
    for k in range(1, len(states)):
        local, carry = run(
            functools.partial(sweep_kernel, k * chunk),
            (f32(width, chunk, cells), f32(chunk, cells)),
            (table, fields, drives[k], rden),
            scalar=False,
        )
        locals_.append(local)
        carries.append(gather_over("gx", carry))
    if repeat == 0:
        kernel = functools.partial(slabs_kernel, peers, width)
        kept["slabs"] = run(kernel, f32(peers, count, cells), (me, table, carries[0]))
    states, m, state = [], None, None
    for k in range(len(locals_)):
        args = (me, table, carries[k], kept["slabs"], inflow, locals_[k], prefix)
        if repeat < ITERS - 1:
            m, state = run(
                functools.partial(next_kernel, peers, k * chunk),
                (f32(13 * width, cells), f32(width, chunk, cells)),
                args if m is None else args + (m,),
                (pltpu.VMEM((chunk, cells), jnp.float32), pltpu.VMEM((13, width, SUB, cells), jnp.float32)),
            )
            states.append(state)
        else:
            rest = [] if k == 0 else [states]
            states = pl.pallas_call(
                functools.partial(last_kernel, peers, k * chunk),
                grid=(BLOCKS,),
                out_shape=f32(count, width, cells),
                in_specs=[SMEM] + [VMEM] * 6 + [pl.BlockSpec(memory_space=pl.ANY)] * len(rest),
                out_specs=pl.BlockSpec((block, width, cells), lambda i, k=k: (k * BLOCKS + i, 0, 0)),
                input_output_aliases={len(args): 0} if rest else {},
                compiler_params=PARAMS,
            )(*args, *rest)
    return m, states, macro


def per_device(distribution, velocity, weights, collision, solid, inflow):
    count, width, cells = distribution.shape
    peers = lax.axis_size("gx")
    me = lax.axis_index("gx").astype(jnp.int32).reshape(1)
    chunk = count // CHUNKS
    block = chunk // BLOCKS
    distribution = pltpu.with_memory_space_constraint(distribution, pltpu.HBM)
    lines = 4 * count // LANES
    outs = (f32(13 * width + lines, cells), f32(TABLE, count, cells))
    outs += (f32(width, cells), f32(width, cells))
    m, table, rate, wall = pl.pallas_call(
        functools.partial(first_kernel, float(width * peers), count // block),
        grid=(count // block,),
        out_shape=outs,
        in_specs=[VMEM] * 4 + [pl.BlockSpec((block, width, cells), lambda i: (i, 0, 0))],
        out_specs=(VMEM,) * len(outs),
        scratch_shapes=(pltpu.VMEM((8, count), jnp.float32), pltpu.VMEM((13, width, SUB, cells), jnp.float32)),
        compiler_params=PARAMS,
    )(velocity, weights.reshape(1, count), collision, solid, distribution)
    kept, states = {}, (distribution,) * CHUNKS
    for repeat in range(ITERS):
        m, states, macro = iteration(repeat, m, states, table, rate, wall, me, inflow, kept)
    return states, macro


def solution(mesh):
    return jax.shard_map(
        per_device,
        mesh=mesh,
        in_specs=(
            P("vel", "gx", None),
            P(None, "vel"),
            P("vel"),
            P("gx", None),
            P("gx", None),
            P(None, "vel", None),
        ),
        out_specs=(P("vel", "gx", None), P(None, "gx", None)),
        check_vma=False,
    )
```

time: 95.4 us -> 102 us (1.069)
  Pallas kernels: 33 us -> 37.7 us
  starting transfers between devices: 21.2 us -> 24.2 us
  other arithmetic: 2.6 us -> 0.4 us
  waiting for transfers between devices: 32.6 us -> 33.7 us
    pallas_call x9 -> x16, Pallas kernels: 33 us -> 37.7 us  [the longest x9 20 us: run(): pl.pallas_call(kernel, out_shape=out_shape, in_specs=([SMEM] if scalar el...]
    ppermute x6 -> x8, starting transfers between devices: 5.5 us -> 9.92 us  [gather_over(): got = lax.ppermute(blocks, axis, [(i, i ^ bit) for i in range(size)])]
    ppermute x6 -> x8, waiting for transfers between devices: 18.5 us -> 22.1 us  [gather_over(): got = lax.ppermute(blocks, axis, [(i, i ^ bit) for i in range(size)])]
    ppermute x2, starting transfers between devices: 3.67 us -> 0.14 us  [neighbours(): near = lax.ppermute(jnp.where(odd, first, last), axis, near)]
    ppermute x8, waiting for transfers between devices: 14 us -> 11.6 us  [reduce_over(): got.append(lax.ppermute(sent, axis, pairs))]
    ppermute x8, starting transfers between devices: 10.7 us -> 12.8 us  [reduce_over(): got.append(lax.ppermute(sent, axis, pairs))]
    concatenate x2 -> x0, other arithmetic: 1.5 us -> none  [the longest x1 0.78 us: per_device(): padded = jnp.concatenate([vw, jnp.zeros((4, count), jnp.float32)])]
    unnamed x14 -> x22, local copies, waits for them, and re-layouts: 4.51 us -> 4.71 us
  transfers between devices with their start and end apart: 18 -> 20, of which waited for: 10 -> 12; matrix products, arithmetic and copies ran while one was open for 2% -> 0% of each run, Pallas kernels for 13% -> 10%
where the time goes in v2:
time: 102 us
  Pallas kernels  37.7 us (37%)
  waiting for transfers between devices  33.7 us (33%)
  starting transfers between devices  24.2 us (24%)
  local copies, waits for them, and re-layouts  4.8 us (5%)
  between operations  1.05 us (1%)
    ppermute x8, waiting for transfers between devices, gather_over(): got = lax.ppermute(blocks, axis, [(i, i ^ bit) for i in range(size)])  22.1 us
    pallas_call x9, Pallas kernels, run(): pl.pallas_call(kernel, out_shape=out_shape, in_specs=([SMEM] if scalar el...  20 us
    ppermute x8, starting transfers between devices, reduce_over(): got.append(lax.ppermute(sent, axis, pairs))  12.8 us
    ppermute x8, waiting for transfers between devices, reduce_over(): got.append(lax.ppermute(sent, axis, pairs))  11.6 us
    ppermute x8, starting transfers between devices, gather_over(): got = lax.ppermute(blocks, axis, [(i, i ^ bit) for i in range(size)])  9.92 us
    pallas_call x4, Pallas kernels, iteration(): pl.pallas_call(kernel, grid=(BLOCKS if repeat == 0 else 1,), out_shape=f3...  8 us
    pallas_call x1, Pallas kernels, per_device(): pl.pallas_call(functools.partial(first_kernel, float(width * peers), coun...  5.95 us
    unnamed x22, local copies, waits for them, and re-layouts  4.71 us
  transfers between devices with their start and end apart: 20, of which 12 were waited for; matrix products, arithmetic and copies ran while one was open for 0% of the time, Pallas kernels for 10%

profile of v2, /device:TPU:0, one launch (start us, length us, event | category | flops | bytes accessed | tf_op | source)
XLA Modules:
  0.0 101.8 jit_solution(12103114867981958590)
XLA Ops:
  0.6 0.7 copy-done.5
  1.3 0.7 copy-done.6
  2.0 0.7 copy-done.7
  2.7 0.7 copy-done.8
  3.4 6.0 %shard_map.77 = (f32[120,128]{1,0:T(8,128)S(1)}, f32[10,512,128]{2,1,0:T(8,128)S(1)}, f32[8,128]{1,0:T(8,128)S(1)}, f32[8,128]{1,0:T(8,128)S(1)}) custom-call(f32[3,512]{1,0:T(4,128)S(1)} %copy-done.5, f32[1,512]{1,0:T(1,128)S(1)} %bitcast.34, f32[8,128]{1,0:T(8,128)S(1)} %copy-done.6, s32[8,128]{1,0:T(8,128)S(1)} %copy-done.7, f32[512,8,128]{2,1,0:T(8,128)} %s_ref.3), custom_call_target="tpu_custom_call" | custom-call | tf_op jit(solution)/shard_map/pallas_call | solution.py:634
  9.3 3.1 %collective-permute-start = (f32[120,128]{1,0:T(8,128)S(1)}, f32[120,128]{1,0:T(8,128)S(1)}, u32[]{:S(2)}, u32[]{:S(2)}) collective-permute-start(f32[120,128]{1,0:T(8,128)S(1)} %get-tuple-element.24), channel_id=1, source_target_pairs={{0,4},{4,0},{8,12},{12,8},{16,20},{20,16},{24,28},{28,24},{1,5},{5... | collective-permute-start | bytes 184328 | tf_op jit(solution)/shard_map/ppermute | solution.py:507
  12.4 2.7 %shard_map.79.drive_ref = f32[8,256,128]{2,1,0:T(8,128)S(1)} custom-call(f32[10,512,128]{2,1,0:T(8,128)S(1)} %get-tuple-element.23.t_ref, f32[512,8,128]{2,1,0:T(8,128)} %s_ref.3), custom_call_target="tpu_custom_call" | custom-call | tf_op jit(solution)/shard_map/pallas_call | solution.py:555
  15.1 0.0 copy-start.3
  15.1 1.0 copy-done.3
  16.1 2.7 %shard_map.82.drive_ref = f32[8,256,128]{2,1,0:T(8,128)S(1)} custom-call(f32[10,512,128]{2,1,0:T(8,128)S(1)} %get-tuple-element.23.t_ref, f32[512,8,128]{2,1,0:T(8,128)} %s_ref.3), custom_call_target="tpu_custom_call" | custom-call | tf_op jit(solution)/shard_map/pallas_call | solution.py:555
  18.7 1.0 copy-done.1
  19.7 0.8 shard_map.80
  20.6 0.0 collective-permute-done
  20.6 1.6 %collective-permute-start.1 = (f32[136,128]{1,0:T(8,128)S(1)}, f32[136,128]{1,0:T(8,128)S(1)}, u32[]{:S(2)}, u32[]{:S(2)}) collective-permute-start(f32[136,128]{1,0:T(8,128)S(1)} %pad_maximum_fusion.8), channel_id=1, source_target_pairs={{0,8},{4,12},{8,16},{12,20},{16,24},{20,28},{24,0},{28,4},{1,9},{5... | collective-permute-start | bytes 208904 | tf_op jit(solution)/shard_map/ppermute | solution.py:507
  22.3 2.6 %collective-permute-start.2 = (f32[136,128]{1,0:T(8,128)S(1)}, f32[136,128]{1,0:T(8,128)S(1)}, u32[]{:S(2)}, u32[]{:S(2)}) collective-permute-start(f32[136,128]{1,0:T(8,128)S(1)} %pad_maximum_fusion.8), channel_id=1, source_target_pairs={{0,16},{4,20},{8,24},{12,28},{16,0},{20,4},{24,8},{28,12},{1,17},{... | collective-permute-start | bytes 208904 | tf_op jit(solution)/shard_map/ppermute | solution.py:507
  24.9 1.3 %collective-permute-start.3 = (f32[136,128]{1,0:T(8,128)S(1)}, f32[136,128]{1,0:T(8,128)S(1)}, u32[]{:S(2)}, u32[]{:S(2)}) collective-permute-start(f32[136,128]{1,0:T(8,128)S(1)} %pad_maximum_fusion.8), channel_id=1, source_target_pairs={{0,24},{4,28},{8,0},{12,4},{16,8},{20,12},{24,16},{28,20},{1,25},{... | collective-permute-start | bytes 208904 | tf_op jit(solution)/shard_map/ppermute | solution.py:507
  26.2 1.4 %collective-permute-done.1 = f32[136,128]{1,0:T(8,128)S(1)} collective-permute-done((f32[136,128]{1,0:T(8,128)S(1)}, f32[136,128]{1,0:T(8,128)S(1)}, u32[]{:S(2)}, u32[]{:S(2)}) %collective-permute-start.1) | collective-permute-done | bytes 69664 | tf_op jit(solution)/shard_map/ppermute | solution.py:507
  27.6 2.2 %collective-permute-done.2 = f32[136,128]{1,0:T(8,128)S(1)} collective-permute-done((f32[136,128]{1,0:T(8,128)S(1)}, f32[136,128]{1,0:T(8,128)S(1)}, u32[]{:S(2)}, u32[]{:S(2)}) %collective-permute-start.2) | collective-permute-done | bytes 69664 | tf_op jit(solution)/shard_map/ppermute | solution.py:507
  29.9 0.0 collective-permute-done.3
  29.9 0.1 collective-permute-start.4
  30.0 0.7 collective-permute-start.5
  30.7 1.2 %shard_map.78.f_ref = bf16[4096,32]{1,0:T(8,128)(2,1)S(1)} custom-call(f32[8,16,128]{2,1,0:T(8,128)S(1)} %constant_dynamic-update-slice_fusion.v_ref), custom_call_target="tpu_custom_call" | custom-call | tf_op jit(solution)/shard_map/pallas_call | solution.py:39
  31.9 0.0 collective-permute-done.4
  32.0 0.0 collective-permute-done.5
  32.0 5.2 %shard_map.81 = (f32[8,256,128]{2,1,0:T(8,128)S(1)}, f32[264,128]{1,0:T(8,128)S(1)}, f32[5,8,128]{2,1,0:T(8,128)}, f32[10,8,128]{2,1,0:T(8,128)S(1)}) custom-call(s32[1]{0:T(128)} %bitcast.me_ref, f32[13,3,128]{2,1,0:T(4,128)S(1)} %get-tuple-element.57.before_ref, f32[13,8,128]{2,1,0:T(8,128)S(1)} %fusion.m_ref, ...), custom_call_target="tpu_custom_call" | custom-call | tf_op jit(solution)/shard_map/pallas_call | solution.py:39
  37.2 1.4 %shard_map.83 = (f32[8,256,128]{2,1,0:T(8,128)S(1)}, f32[256,128]{1,0:T(8,128)S(1)}) custom-call(f32[10,512,128]{2,1,0:T(8,128)S(1)} %get-tuple-element.23.t_ref, f32[10,8,128]{2,1,0:T(8,128)S(1)} %get-tuple-element.28.field_ref, f32[8,256,128]{2,1,0:T(8,128)S(1)} %copy-done.2, f32[8,512,128]{2,1,0:T(8,128)S(1)} %get-tuple-element.27.rden_ref), custom_call_target="tpu_custom_call" | custom-call | tf_op jit(solution)/shard_map/pallas_call | solution.py:39
  38.5 4.8 %collective-permute-start.6 = (f32[1,256,128]{2,1,0:T(8,128)S(1)}, f32[1,256,128]{2,1,0:T(8,128)S(1)}, u32[]{:S(2)}, u32[]{:S(2)}) collective-permute-start(f32[1,256,128]{2,1,0:T(8,128)S(1)} %bitcast.31), channel_id=1, source_target_pairs={{0,2},{1,3},{2,0},{3,1},{4,6},{5,7},{6,4},{7,5},{8,10},{9,11},{10,... | collective-permute-start | bytes 393224 | tf_op jit(solution)/shard_map/ppermute | solution.py:523
  43.3 4.3 %collective-permute-done.6 = f32[1,256,128]{2,1,0:T(8,128)S(1)} collective-permute-done((f32[1,256,128]{2,1,0:T(8,128)S(1)}, f32[1,256,128]{2,1,0:T(8,128)S(1)}, u32[]{:S(2)}, u32[]{:S(2)}) %collective-permute-start.6) | collective-permute-done | bytes 131104 | tf_op jit(solution)/shard_map/ppermute | solution.py:523
  47.6 0.2 collective-permute-start.7
  47.8 0.6 collective-permute-start.8
  48.4 5.3 %collective-permute-done.8 = f32[1,264,128]{2,1,0:T(8,128)S(1)} collective-permute-done((f32[1,264,128]{2,1,0:T(8,128)S(1)}, f32[1,264,128]{2,1,0:T(8,128)S(1)}, u32[]{:S(2)}, u32[]{:S(2)}) %collective-permute-start.8) | collective-permute-done | bytes 135200 | tf_op jit(solution)/shard_map/ppermute | solution.py:523
  53.7 0.1 collective-permute-start.9
  53.9 1.5 %collective-permute-done.9 = f32[2,264,128]{2,1,0:T(8,128)S(1)} collective-permute-done((f32[2,264,128]{2,1,0:T(8,128)S(1)}, f32[2,264,128]{2,1,0:T(8,128)S(1)}, u32[]{:S(2)}, u32[]{:S(2)}) %collective-permute-start.9) | collective-permute-done | bytes 270368 | tf_op jit(solution)/shard_map/ppermute | solution.py:523
  55.4 0.1 pad_maximum_fusion.c_ref
  55.4 0.0 copy-start
  55.4 1.1 %shard_map.84.g_ref = f32[4,512,128]{2,1,0:T(8,128)S(1)} custom-call(s32[1]{0:T(128)} %bitcast.me_ref, f32[10,512,128]{2,1,0:T(8,128)S(1)} %get-tuple-element.23.t_ref, f32[4,264,128]{2,1,0:T(8,128)S(1)} %pad_maximum_fusion.c_ref), custom_call_target="tpu_custom_call" | custom-call | tf_op jit(solution)/shard_map/pallas_call | solution.py:39
  56.6 1.9 %shard_map.85 = (f32[104,128]{1,0:T(8,128)S(1)}, f32[8,256,128]{2,1,0:T(8,128)S(1)}) custom-call(s32[1]{0:T(128)} %bitcast.me_ref, f32[10,512,128]{2,1,0:T(8,128)S(1)} %get-tuple-element.23.t_ref, f32[4,264,128]{2,1,0:T(8,128)S(1)} %pad_maximum_fusion.c_ref, f32[4,512,128]{2,1,0:T(8,128)S(1)} %shard_map.84.g_ref, f32[2,512,128]{2,1,0:T(8,128)S(1)} %copy-done, ...), custom_call_target="tpu_custom_call" | custom-call | tf_op jit(solution)/shard_map/pallas_call | solution.py:39
  58.5 1.9 %shard_map.86 = (f32[104,128]{1,0:T(8,128)S(1)}, f32[8,256,128]{2,1,0:T(8,128)S(1)}) custom-call(s32[1]{0:T(128)} %bitcast.me_ref, f32[10,512,128]{2,1,0:T(8,128)S(1)} %get-tuple-element.23.t_ref, f32[4,256,128]{2,1,0:T(8,128)S(1)} %pad_maximum_fusion.2.c_ref, f32[4,512,128]{2,1,0:T(8,128)S(1)} %shard_map.84.g_ref, f32[2,512,128]{2,1,0:T(8,128)S(1)} %copy-done, ...), custom_call_target="tpu_custom_call" | custom-call | tf_op jit(solution)/shard_map/pallas_call | solution.py:39
  60.4 0.3 collective-permute-start.10
  60.7 3.9 %collective-permute-done.10 = f32[104,128]{1,0:T(8,128)S(1)} collective-permute-done((f32[104,128]{1,0:T(8,128)S(1)}, f32[104,128]{1,0:T(8,128)S(1)}, u32[]{:S(2)}, u32[]{:S(2)}) %collective-permute-start.10) | collective-permute-done | bytes 53280 | tf_op jit(solution)/shard_map/ppermute | solution.py:507
  64.6 1.4 %collective-permute-start.11 = (f32[104,128]{1,0:T(8,128)S(1)}, f32[104,128]{1,0:T(8,128)S(1)}, u32[]{:S(2)}, u32[]{:S(2)}) collective-permute-start(f32[104,128]{1,0:T(8,128)S(1)} %add.34), channel_id=1, source_target_pairs={{0,8},{4,12},{8,16},{12,20},{16,24},{20,28},{24,0},{28,4},{1,9},{5... | collective-permute-start | bytes 159752 | tf_op jit(solution)/shard_map/ppermute | solution.py:507
  66.0 2.0 %collective-permute-start.12 = (f32[104,128]{1,0:T(8,128)S(1)}, f32[104,128]{1,0:T(8,128)S(1)}, u32[]{:S(2)}, u32[]{:S(2)}) collective-permute-start(f32[104,128]{1,0:T(8,128)S(1)} %add.34), channel_id=1, source_target_pairs={{0,16},{4,20},{8,24},{12,28},{16,0},{20,4},{24,8},{28,12},{1,17},{... | collective-permute-start | bytes 159752 | tf_op jit(solution)/shard_map/ppermute | solution.py:507
  68.0 0.5 collective-permute-start.13
  68.5 2.2 %collective-permute-done.11 = f32[104,128]{1,0:T(8,128)S(1)} collective-permute-done((f32[104,128]{1,0:T(8,128)S(1)}, f32[104,128]{1,0:T(8,128)S(1)}, u32[]{:S(2)}, u32[]{:S(2)}) %collective-permute-start.11) | collective-permute-done | bytes 53280 | tf_op jit(solution)/shard_map/ppermute | solution.py:507
  70.7 1.4 %collective-permute-done.12 = f32[104,128]{1,0:T(8,128)S(1)} collective-permute-done((f32[104,128]{1,0:T(8,128)S(1)}, f32[104,128]{1,0:T(8,128)S(1)}, u32[]{:S(2)}, u32[]{:S(2)}) %collective-permute-start.12) | collective-permute-done | bytes 53280 | tf_op jit(solution)/shard_map/ppermute | solution.py:507
  72.1 0.4 collective-permute-done.13
  72.6 0.1 collective-permute-start.14
  72.7 0.7 collective-permute-start.15
  73.3 1.3 %shard_map.87.drive_ref = f32[8,256,128]{2,1,0:T(8,128)S(1)} custom-call(f32[10,512,128]{2,1,0:T(8,128)S(1)} %get-tuple-element.23.t_ref, f32[8,256,128]{2,1,0:T(8,128)S(1)} %get-tuple-element.36.s_ref), custom_call_target="tpu_custom_call" | custom-call | tf_op jit(solution)/shard_map/pallas_call | solution.py:555
  74.7 1.3 %shard_map.89.drive_ref = f32[8,256,128]{2,1,0:T(8,128)S(1)} custom-call(f32[10,512,128]{2,1,0:T(8,128)S(1)} %get-tuple-element.23.t_ref, f32[8,256,128]{2,1,0:T(8,128)S(1)} %get-tuple-element.38.s_ref), custom_call_target="tpu_custom_call" | custom-call | tf_op jit(solution)/shard_map/pallas_call | solution.py:555
  76.0 0.0 collective-permute-done.14
  76.0 0.0 collective-permute-done.15
  76.0 5.2 %shard_map.88 = (f32[8,256,128]{2,1,0:T(8,128)S(1)}, f32[264,128]{1,0:T(8,128)S(1)}, f32[5,8,128]{2,1,0:T(8,128)}, f32[10,8,128]{2,1,0:T(8,128)S(1)}) custom-call(s32[1]{0:T(128)} %bitcast.me_ref, f32[13,3,128]{2,1,0:T(4,128)S(1)} %get-tuple-element.53.before_ref, f32[13,8,128]{2,1,0:T(8,128)S(1)} %add_bitcast_fusion.m_ref, ...), custom_call_target="tpu_custom_call" | custom-call | tf_op jit(solution)/shard_map/pallas_call | solution.py:39
  81.2 1.3 %shard_map.90 = (f32[8,256,128]{2,1,0:T(8,128)S(1)}, f32[256,128]{1,0:T(8,128)S(1)}) custom-call(f32[10,512,128]{2,1,0:T(8,128)S(1)} %get-tuple-element.23.t_ref, f32[10,8,128]{2,1,0:T(8,128)S(1)} %get-tuple-element.37.field_ref, f32[8,256,128]{2,1,0:T(8,128)S(1)} %shard_map.89.drive_ref, f32[8,512,128]{2,1,0:T(8,128)S(1)} %get-tuple-element.27.rden_ref), custom_call_target="tpu_custom_call" | custom-call | tf_op jit(solution)/shard_map/pallas_call | solution.py:39
  82.6 3.4 %collective-permute-start.16 = (f32[1,256,128]{2,1,0:T(8,128)S(1)}, f32[1,256,128]{2,1,0:T(8,128)S(1)}, u32[]{:S(2)}, u32[]{:S(2)}) collective-permute-start(f32[1,256,128]{2,1,0:T(8,128)S(1)} %bitcast.28), channel_id=1, source_target_pairs={{0,2},{1,3},{2,0},{3,1},{4,6},{5,7},{6,4},{7,5},{8,10},{9,11},{10,... | collective-permute-start | bytes 393224 | tf_op jit(solution)/shard_map/ppermute | solution.py:523
  86.0 4.3 %collective-permute-done.16 = f32[1,256,128]{2,1,0:T(8,128)S(1)} collective-permute-done((f32[1,256,128]{2,1,0:T(8,128)S(1)}, f32[1,256,128]{2,1,0:T(8,128)S(1)}, u32[]{:S(2)}, u32[]{:S(2)}) %collective-permute-start.16) | collective-permute-done | bytes 131104 | tf_op jit(solution)/shard_map/ppermute | solution.py:523
  90.4 0.1 collective-permute-start.17
  90.5 0.7 collective-permute-start.18
  91.2 5.3 %collective-permute-done.18 = f32[1,264,128]{2,1,0:T(8,128)S(1)} collective-permute-done((f32[1,264,128]{2,1,0:T(8,128)S(1)}, f32[1,264,128]{2,1,0:T(8,128)S(1)}, u32[]{:S(2)}, u32[]{:S(2)}) %collective-permute-start.18) | collective-permute-done | bytes 135200 | tf_op jit(solution)/shard_map/ppermute | solution.py:523
  96.5 0.1 collective-permute-start.19
  96.5 0.0 collective-permute-done.17
  96.6 1.4 %collective-permute-done.19 = f32[2,264,128]{2,1,0:T(8,128)S(1)} collective-permute-done((f32[2,264,128]{2,1,0:T(8,128)S(1)}, f32[2,264,128]{2,1,0:T(8,128)S(1)}, u32[]{:S(2)}, u32[]{:S(2)}) %collective-permute-start.19) | collective-permute-done | bytes 270368 | tf_op jit(solution)/shard_map/ppermute | solution.py:523
  98.1 1.9 %shard_map.91.refs_0_ = f32[512,8,128]{2,1,0:T(8,128)} custom-call(s32[1]{0:T(128)} %bitcast.me_ref, f32[10,512,128]{2,1,0:T(8,128)S(1)} %get-tuple-element.23.t_ref, f32[4,264,128]{2,1,0:T(8,128)S(1)} %pad_maximum_fusion.1.c_ref, f32[4,512,128]{2,1,0:T(8,128)S(1)} %shard_map.84.g_ref, f32[2,512,128]{2,1,0:T(8,128)S(1)} %copy-done, ...), custom_call_target="tpu_custom_call" | custom-call | tf_op jit(solution)/shard_map/pallas_call | solution.py:612
  100.0 1.9 %shard_map.92 = f32[512,8,128]{2,1,0:T(8,128)} custom-call(s32[1]{0:T(128)} %bitcast.me_ref, f32[10,512,128]{2,1,0:T(8,128)S(1)} %get-tuple-element.23.t_ref, f32[4,256,128]{2,1,0:T(8,128)S(1)} %pad_maximum_fusion.3.c_ref, f32[4,512,128]{2,1,0:T(8,128)S(1)} %shard_map.84.g_ref, f32[2,512,128]{2,1,0:T(8,128)S(1)} %copy-done, ...), custom_call_target="tpu_custom_call", output_to_operand_aliasing={{}: (7, {})} | custom-call | tf_op jit(solution)/shard_map/pallas_call | solution.py:612
  (42 shorter events, 0.5 us)
Async XLA Ops:
  0.6 0.7 copy-start.5
  1.3 0.7 copy-start.6
  2.0 0.7 copy-start.7
  2.7 0.7 copy-start.8
  9.3 11.2 %collective-permute-start = (f32[120,128]{1,0:T(8,128)S(1)}, f32[120,128]{1,0:T(8,128)S(1)}, u32[]{:S(2)}, u32[]{:S(2)}) collective-permute-start(f32[120,128]{1,0:T(8,128)S(1)} %get-tuple-element.24), channel_id=1, source_target_pairs={{0,4},{4,0},{8,12},{12,8},{16,20},{20,16},{24,28},{28,24},{1,5},{5... | collective-permute-start | bytes 184328 | tf_op jit(solution)/shard_map/ppermute | solution.py:507
  15.1 1.0 copy-start.3
  18.7 1.0 copy-start.1
  19.7 12.3 %copy-start.4 = (f32[8,256,128]{2,1,0:T(8,128)S(1)}, f32[8,256,128]{2,1,0:T(8,128)}, u32[]{:S(2)}) copy-start(f32[8,256,128]{2,1,0:T(8,128)} %copy-done.3) | copy-start | bytes 3145732
  20.6 7.0 %collective-permute-start.1 = (f32[136,128]{1,0:T(8,128)S(1)}, f32[136,128]{1,0:T(8,128)S(1)}, u32[]{:S(2)}, u32[]{:S(2)}) collective-permute-start(f32[136,128]{1,0:T(8,128)S(1)} %pad_maximum_fusion.8), channel_id=1, source_target_pairs={{0,8},{4,12},{8,16},{12,20},{16,24},{20,28},{24,0},{28,4},{1,9},{5... | collective-permute-start | bytes 208904 | tf_op jit(solution)/shard_map/ppermute | solution.py:507
  22.3 7.6 %collective-permute-start.2 = (f32[136,128]{1,0:T(8,128)S(1)}, f32[136,128]{1,0:T(8,128)S(1)}, u32[]{:S(2)}, u32[]{:S(2)}) collective-permute-start(f32[136,128]{1,0:T(8,128)S(1)} %pad_maximum_fusion.8), channel_id=1, source_target_pairs={{0,16},{4,20},{8,24},{12,28},{16,0},{20,4},{24,8},{28,12},{1,17},{... | collective-permute-start | bytes 208904 | tf_op jit(solution)/shard_map/ppermute | solution.py:507
  24.9 5.0 %collective-permute-start.3 = (f32[136,128]{1,0:T(8,128)S(1)}, f32[136,128]{1,0:T(8,128)S(1)}, u32[]{:S(2)}, u32[]{:S(2)}) collective-permute-start(f32[136,128]{1,0:T(8,128)S(1)} %pad_maximum_fusion.8), channel_id=1, source_target_pairs={{0,24},{4,28},{8,0},{12,4},{16,8},{20,12},{24,16},{28,20},{1,25},{... | collective-permute-start | bytes 208904 | tf_op jit(solution)/shard_map/ppermute | solution.py:507
  29.9 2.0 %collective-permute-start.4 = (f32[13,3,128]{2,1,0:T(4,128)S(1)}, f32[13,3,128]{2,1,0:T(4,128)S(1)}, u32[]{:S(2)}, u32[]{:S(2)}) collective-permute-start(f32[13,3,128]{2,1,0:T(4,128)S(1)} %get-tuple-element.59), channel_id=1, source_target_pairs={{0,1},{1,0},{2,3},{3,2},{4,5},{5,4},{6,7},{7,6},{8,9},{9,8},{10,11... | collective-permute-start | bytes 59912 | tf_op jit(solution)/shard_map/ppermute | solution.py:537
  30.0 2.0 %collective-permute-start.5 = (f32[13,3,128]{2,1,0:T(4,128)S(1)}, f32[13,3,128]{2,1,0:T(4,128)S(1)}, u32[]{:S(2)}, u32[]{:S(2)}) collective-permute-start(f32[13,3,128]{2,1,0:T(4,128)S(1)} %get-tuple-element.58), channel_id=1, source_target_pairs={{1,2},{2,1},{5,6},{6,5},{9,10},{10,9},{13,14},{14,13},{17,18},{18,... | collective-permute-start | bytes 59912 | tf_op jit(solution)/shard_map/ppermute | solution.py:536
  32.0 5.2 %copy-start.2 = (f32[8,256,128]{2,1,0:T(8,128)S(1)}, f32[8,256,128]{2,1,0:T(8,128)}, u32[]{:S(2)}) copy-start(f32[8,256,128]{2,1,0:T(8,128)} %copy-done.1) | copy-start | bytes 3145732
  38.5 9.1 %collective-permute-start.6 = (f32[1,256,128]{2,1,0:T(8,128)S(1)}, f32[1,256,128]{2,1,0:T(8,128)S(1)}, u32[]{:S(2)}, u32[]{:S(2)}) collective-permute-start(f32[1,256,128]{2,1,0:T(8,128)S(1)} %bitcast.31), channel_id=1, source_target_pairs={{0,2},{1,3},{2,0},{3,1},{4,6},{5,7},{6,4},{7,5},{8,10},{9,11},{10,... | collective-permute-start | bytes 393224 | tf_op jit(solution)/shard_map/ppermute | solution.py:523
  47.6 6.2 %collective-permute-start.7 = (f32[2,256,128]{2,1,0:T(8,128)S(1)}, f32[2,256,128]{2,1,0:T(8,128)S(1)}, u32[]{:S(2)}, u32[]{:S(2)}) collective-permute-start(f32[2,256,128]{2,1,0:T(8,128)S(1)} %pad_maximum_fusion.6), channel_id=1, source_target_pairs={{0,1},{1,0},{2,3},{3,2},{4,5},{5,4},{6,7},{7,6},{8,9},{9,8},{10,11... | collective-permute-start | bytes 786440 | tf_op jit(solution)/shard_map/ppermute | solution.py:523
  47.8 5.9 %collective-permute-start.8 = (f32[1,264,128]{2,1,0:T(8,128)S(1)}, f32[1,264,128]{2,1,0:T(8,128)S(1)}, u32[]{:S(2)}, u32[]{:S(2)}) collective-permute-start(f32[1,264,128]{2,1,0:T(8,128)S(1)} %bitcast.25), channel_id=1, source_target_pairs={{0,2},{1,3},{2,0},{3,1},{4,6},{5,7},{6,4},{7,5},{8,10},{9,11},{10,... | collective-permute-start | bytes 405512 | tf_op jit(solution)/shard_map/ppermute | solution.py:523
  53.7 1.6 %collective-permute-start.9 = (f32[2,264,128]{2,1,0:T(8,128)S(1)}, f32[2,264,128]{2,1,0:T(8,128)S(1)}, u32[]{:S(2)}, u32[]{:S(2)}) collective-permute-start(f32[2,264,128]{2,1,0:T(8,128)S(1)} %pad_maximum_fusion.4), channel_id=1, source_target_pairs={{0,1},{1,0},{2,3},{3,2},{4,5},{5,4},{6,7},{7,6},{8,9},{9,8},{10,11... | collective-permute-start | bytes 811016 | tf_op jit(solution)/shard_map/ppermute | solution.py:523
  55.4 1.2 %copy-start = (f32[2,512,128]{2,1,0:T(8,128)S(1)}, f32[2,512,128]{2,1,0:T(8,128)}, u32[]{:S(2)}) copy-start(f32[2,512,128]{2,1,0:T(8,128)} %flow_ref.7) | copy-start | bytes 1572868
  60.4 4.2 %collective-permute-start.10 = (f32[104,128]{1,0:T(8,128)S(1)}, f32[104,128]{1,0:T(8,128)S(1)}, u32[]{:S(2)}, u32[]{:S(2)}) collective-permute-start(f32[104,128]{1,0:T(8,128)S(1)} %get-tuple-element.35), channel_id=1, source_target_pairs={{0,4},{4,0},{8,12},{12,8},{16,20},{20,16},{24,28},{28,24},{1,5},{5... | collective-permute-start | bytes 159752 | tf_op jit(solution)/shard_map/ppermute | solution.py:507
  64.6 6.1 %collective-permute-start.11 = (f32[104,128]{1,0:T(8,128)S(1)}, f32[104,128]{1,0:T(8,128)S(1)}, u32[]{:S(2)}, u32[]{:S(2)}) collective-permute-start(f32[104,128]{1,0:T(8,128)S(1)} %add.34), channel_id=1, source_target_pairs={{0,8},{4,12},{8,16},{12,20},{16,24},{20,28},{24,0},{28,4},{1,9},{5... | collective-permute-start | bytes 159752 | tf_op jit(solution)/shard_map/ppermute | solution.py:507
  66.0 6.1 %collective-permute-start.12 = (f32[104,128]{1,0:T(8,128)S(1)}, f32[104,128]{1,0:T(8,128)S(1)}, u32[]{:S(2)}, u32[]{:S(2)}) collective-permute-start(f32[104,128]{1,0:T(8,128)S(1)} %add.34), channel_id=1, source_target_pairs={{0,16},{4,20},{8,24},{12,28},{16,0},{20,4},{24,8},{28,12},{1,17},{... | collective-permute-start | bytes 159752 | tf_op jit(solution)/shard_map/ppermute | solution.py:507
  68.0 4.6 %collective-permute-start.13 = (f32[104,128]{1,0:T(8,128)S(1)}, f32[104,128]{1,0:T(8,128)S(1)}, u32[]{:S(2)}, u32[]{:S(2)}) collective-permute-start(f32[104,128]{1,0:T(8,128)S(1)} %add.34), channel_id=1, source_target_pairs={{0,24},{4,28},{8,0},{12,4},{16,8},{20,12},{24,16},{28,20},{1,25},{... | collective-permute-start | bytes 159752 | tf_op jit(solution)/shard_map/ppermute | solution.py:507
  72.6 3.4 %collective-permute-start.14 = (f32[13,3,128]{2,1,0:T(4,128)S(1)}, f32[13,3,128]{2,1,0:T(4,128)S(1)}, u32[]{:S(2)}, u32[]{:S(2)}) collective-permute-start(f32[13,3,128]{2,1,0:T(4,128)S(1)} %get-tuple-element.55), channel_id=1, source_target_pairs={{0,1},{1,0},{2,3},{3,2},{4,5},{5,4},{6,7},{7,6},{8,9},{9,8},{10,11... | collective-permute-start | bytes 59912 | tf_op jit(solution)/shard_map/ppermute | solution.py:537
  72.7 3.4 %collective-permute-start.15 = (f32[13,3,128]{2,1,0:T(4,128)S(1)}, f32[13,3,128]{2,1,0:T(4,128)S(1)}, u32[]{:S(2)}, u32[]{:S(2)}) collective-permute-start(f32[13,3,128]{2,1,0:T(4,128)S(1)} %get-tuple-element.54), channel_id=1, source_target_pairs={{1,2},{2,1},{5,6},{6,5},{9,10},{10,9},{13,14},{14,13},{17,18},{18,... | collective-permute-start | bytes 59912 | tf_op jit(solution)/shard_map/ppermute | solution.py:536
  82.6 7.8 %collective-permute-start.16 = (f32[1,256,128]{2,1,0:T(8,128)S(1)}, f32[1,256,128]{2,1,0:T(8,128)S(1)}, u32[]{:S(2)}, u32[]{:S(2)}) collective-permute-start(f32[1,256,128]{2,1,0:T(8,128)S(1)} %bitcast.28), channel_id=1, source_target_pairs={{0,2},{1,3},{2,0},{3,1},{4,6},{5,7},{6,4},{7,5},{8,10},{9,11},{10,... | collective-permute-start | bytes 393224 | tf_op jit(solution)/shard_map/ppermute | solution.py:523
  90.4 6.2 %collective-permute-start.17 = (f32[2,256,128]{2,1,0:T(8,128)S(1)}, f32[2,256,128]{2,1,0:T(8,128)S(1)}, u32[]{:S(2)}, u32[]{:S(2)}) collective-permute-start(f32[2,256,128]{2,1,0:T(8,128)S(1)} %pad_maximum_fusion.7), channel_id=1, source_target_pairs={{0,1},{1,0},{2,3},{3,2},{4,5},{5,4},{6,7},{7,6},{8,9},{9,8},{10,11... | collective-permute-start | bytes 786440 | tf_op jit(solution)/shard_map/ppermute | solution.py:523
  90.5 5.9 %collective-permute-start.18 = (f32[1,264,128]{2,1,0:T(8,128)S(1)}, f32[1,264,128]{2,1,0:T(8,128)S(1)}, u32[]{:S(2)}, u32[]{:S(2)}) collective-permute-start(f32[1,264,128]{2,1,0:T(8,128)S(1)} %bitcast.22), channel_id=1, source_target_pairs={{0,2},{1,3},{2,0},{3,1},{4,6},{5,7},{6,4},{7,5},{8,10},{9,11},{10,... | collective-permute-start | bytes 405512 | tf_op jit(solution)/shard_map/ppermute | solution.py:523
  96.5 1.6 %collective-permute-start.19 = (f32[2,264,128]{2,1,0:T(8,128)S(1)}, f32[2,264,128]{2,1,0:T(8,128)S(1)}, u32[]{:S(2)}, u32[]{:S(2)}) collective-permute-start(f32[2,264,128]{2,1,0:T(8,128)S(1)} %pad_maximum_fusion.5), channel_id=1, source_target_pairs={{0,1},{1,0},{2,3},{3,2},{4,5},{5,4},{6,7},{7,6},{8,9},{9,8},{10,11... | collective-permute-start | bytes 811016 | tf_op jit(solution)/shard_map/ppermute | solution.py:523

commit v3 on v2

--- a/solution.py
+++ b/solution.py
@@ -27,11 +27,13 @@
 A, B, E, W, HB, HE, BASE, FA, BA, REST = range(10)
 TABLE = 10
 CHUNKS = 2
-BLOCKS = 2
+BLOCKS = 4
+PAD = 8
 
 
 SMEM = pl.BlockSpec(memory_space=pltpu.SMEM)
 VMEM = pl.BlockSpec(memory_space=pltpu.VMEM)
+HBM = pl.BlockSpec(memory_space=pltpu.HBM)
 PARAMS = pltpu.CompilerParams(vmem_limit_bytes=16 * 1024 * 1024)
 
 
@@ -74,7 +76,7 @@
             return add_moments(acc, state_at(x, rows), t_ref, table_rows)
 
         acc = tuple(acc_ref[k, x] for k in range(13))
-        acc = lax.fori_loop(0, groups, step, acc, unroll=4)
+        acc = lax.fori_loop(0, groups, step, acc, unroll=min(16, groups))
         for k, value in enumerate(acc):
             acc_ref[k, x] = value
 
@@ -85,52 +87,61 @@
         m_ref[k * width : (k + 1) * width, :] = jnp.sum(acc_ref[k], axis=1)
 
 
-def first_kernel(
-    extent, steps, v_ref, w_ref, collision_ref, solid_ref, dist_ref, m_ref, t_ref, rate_ref, wall_ref, vw_ref, acc_ref
-):
-    block, width = dist_ref.shape[0], dist_ref.shape[1]
-    i = pl.program_id(0)
-    start = pl.multiple_of(i * block, block)
-
-    @pl.when(i == 0)
-    def _():
-        wall = solid_ref[...].astype(jnp.float32)
-        wall_ref[...] = wall
-        rate_ref[...] = collision_ref[...] + wall_rate * wall
-        acc_ref[...] = jnp.zeros_like(acc_ref)
-        vw_ref[0:3, :] = v_ref[...]
-        vw_ref[3:4, :] = w_ref[...]
-        vw_ref[4:8, :] = jnp.zeros((4, vw_ref.shape[1]), jnp.float32)
-        lines = vw_ref.shape[1] // LANES
-        for k in range(4):
-            for j in range(lines):
-                row = 13 * width + k * lines + j
-                m_ref[row : row + 1, :] = vw_ref[k : k + 1, j * LANES : (j + 1) * LANES]
-
-    part = max(block, LANES)
-
-    @pl.when(start % part == 0)
-    def _():
-        here = pl.ds(pl.multiple_of(start, part), part)
-        columns = vw_ref[:, here].T
-
-        def wide(k):
-            return jnp.broadcast_to(columns[:, k : k + 1], (part, LANES))
-
-        a, b, e = wide(0), wide(1), wide(2)
-        t_ref[A, here], t_ref[B, here], t_ref[E, here], t_ref[W, here] = a, b, e, wide(3)
-        hb, he = 0.5 * jnp.abs(b), 0.5 * jnp.abs(e)
-        t_ref[HB, here], t_ref[HE, here] = hb, he
-        t_ref[BASE, here] = pseudo_rate + (hb + he) + jnp.abs(a) * extent
-        t_ref[FA, here] = jnp.maximum(a, 0.0) * extent
-        t_ref[BA, here] = jnp.maximum(-a, 0.0) * extent
-        t_ref[REST, here] = (box_volume * (2.0 * math.pi) ** (-1.5)) * jnp.exp(-0.5 * (a * a + b * b + e * e))
-
-    moments_loop(acc_ref, t_ref, start, block // SUB, lambda x, rows: dist_ref[rows, x, :])
-
-    @pl.when(i == steps - 1)
-    def _():
-        write_moments(m_ref, acc_ref)
+def first_kernel(extent, *refs):
+    sources, (m_ref, t_ref, rate_ref, wall_ref), rest = refs[:5], refs[5:9], refs[9:]
+    v_ref, w_ref, collision_ref, solid_ref, dist_ref, vw_ref, acc_ref, sem = rest
+    count, width = dist_ref.shape[0], dist_ref.shape[1]
+    block = count // BLOCKS
+    small = [
+        pltpu.make_async_copy(source, target, sem.at[k])
+        for k, (source, target) in enumerate(zip(sources[:4], (v_ref, w_ref, collision_ref, solid_ref)))
+    ]
+    large = [
+        pltpu.make_async_copy(
+            sources[4].at[pl.ds(k * block, block)], dist_ref.at[pl.ds(k * block, block)], sem.at[4 + k]
+        )
+        for k in range(BLOCKS)
+    ]
+    for copy in small + large:
+        copy.start()
+    for copy in small:
+        copy.wait()
+    wall = solid_ref[...].astype(jnp.float32)
+    wall_ref[...] = wall
+    rate_ref[...] = collision_ref[...] + wall_rate * wall
+    acc_ref[...] = jnp.zeros_like(acc_ref)
+    vw_ref[0:3, :] = v_ref[...]
+    vw_ref[3:4, :] = w_ref[...]
+    vw_ref[4:8, :] = jnp.zeros((4, count), jnp.float32)
+    lines = count // LANES
+    for k in range(4):
+        for j in range(lines):
+            row = 13 * width + k * lines + j
+            m_ref[row : row + 1, :] = vw_ref[k : k + 1, j * LANES : (j + 1) * LANES]
+    columns = vw_ref[...].T
+
+    def wide(k):
+        return jnp.broadcast_to(columns[:, k : k + 1], (count, LANES))
+
+    here = slice(0, count)
+    a, b, e = wide(0), wide(1), wide(2)
+    t_ref[A, here], t_ref[B, here], t_ref[E, here], t_ref[W, here] = a, b, e, wide(3)
+    hb, he = 0.5 * jnp.abs(b), 0.5 * jnp.abs(e)
+    t_ref[HB, here], t_ref[HE, here] = hb, he
+    t_ref[BASE, here] = pseudo_rate + (hb + he) + jnp.abs(a) * extent
+    t_ref[FA, here] = jnp.maximum(a, 0.0) * extent
+    t_ref[BA, here] = jnp.maximum(-a, 0.0) * extent
+    t_ref[REST, here] = (box_volume * (2.0 * math.pi) ** (-1.5)) * jnp.exp(-0.5 * (a * a + b * b + e * e))
+    for k, copy in enumerate(large):
+        copy.wait()
+        moments_loop(
+            acc_ref,
+            t_ref,
+            k * block,
+            block // SUB,
+            lambda x, rows, k=k: dist_ref[pl.ds(pl.multiple_of(k * block + rows.start, SUB), SUB), x, :],
+        )
+    write_moments(m_ref, acc_ref)
 
 
 def gains_kernel(t_ref, rate_ref, rden_ref, p_ref):
@@ -294,30 +305,46 @@
     return delta
 
 
-def transport_kernel(first, raw, t_ref, s_ref, drive_ref):
+def transport_kernel(first, t_ref, s_ref, drive_ref):
+    transport(first, 0, drive_ref.shape[1], t_ref, lambda x, rows: s_ref[x, rows, :], drive_ref)
+
+
+def first_transport_kernel(first, t_ref, dist_ref, drive_ref, held_ref, sem):
+    block = drive_ref.shape[1] // BLOCKS
+    copies = [
+        pltpu.make_async_copy(
+            dist_ref.at[pl.ds(first + k * block, block)], held_ref.at[pl.ds(k * block, block)], sem.at[k]
+        )
+        for k in range(BLOCKS)
+    ]
+    for copy in copies:
+        copy.start()
+    for k, copy in enumerate(copies):
+        copy.wait()
+        transport(first, k * block, block, t_ref, lambda x, rows: held_ref[rows, x, :], drive_ref)
+
+
+def transport(first, start, count, t_ref, state_at, drive_ref):
     width = drive_ref.shape[0]
-    count = s_ref.shape[0] if raw else s_ref.shape[1]
-    start = pl.program_id(0) * count
     lane = lax.broadcasted_iota(jnp.int32, (SUB, LANES), 1)
     z = lane % NZ
     y_down, y_up = (lane + LANES - NZ) % LANES, (lane + NZ) % LANES
     z_down, z_up = lane - z + (z + NZ - 1) % NZ, lane - z + (z + 1) % NZ
 
     def step(g, carry):
-        rows = pl.ds(pl.multiple_of(g * SUB, SUB), SUB)
-        out = pl.ds(pl.multiple_of(start + g * SUB, SUB), SUB)
+        rows = pl.ds(pl.multiple_of(start + g * SUB, SUB), SUB)
         table_rows = pl.ds(pl.multiple_of(first + start + g * SUB, SUB), SUB)
         hb, he = t_ref[HB, table_rows, :], t_ref[HE, table_rows, :]
         from_y = jnp.where(t_ref[B, table_rows, :] > 0.0, y_down, y_up)
         from_z = jnp.where(t_ref[E, table_rows, :] > 0.0, z_down, z_up)
         for x in range(width):
-            s = s_ref[rows, x, :] if raw else s_ref[x, rows, :]
+            s = state_at(x, rows)
             sy = jnp.take_along_axis(s, from_y, axis=1, mode="promise_in_bounds")
             sz = jnp.take_along_axis(s, from_z, axis=1, mode="promise_in_bounds")
-            drive_ref[x, out, :] = pseudo_rate * s + hb * sy + he * sz
+            drive_ref[x, rows, :] = pseudo_rate * s + hb * sy + he * sz
         return carry
 
-    lax.fori_loop(0, count // SUB, step, 0, unroll=8)
+    lax.fori_loop(0, count // SUB, step, 0, unroll=min(8, count // SUB))
 
 
 def kinetic_kernel(
@@ -412,7 +439,7 @@
             s_ref[x, rows, :] = value
             return carry
 
-        lax.fori_loop(0, count // SUB, ahead, 0, unroll=16)
+        lax.fori_loop(0, count // SUB, ahead, 0, unroll=min(32, count // SUB))
 
     def back(g, carry):
         rows, wide = both(g)
@@ -540,24 +567,28 @@
 
 def iteration(repeat, m, states, table, rate, wall, me, inflow, kept):
     width, cells = rate.shape
-    count, peers = table.shape[1], lax.axis_size("gx")
+    count, peers = table.shape[1] - PAD, lax.axis_size("gx")
     chunk = count // len(states)
-    block = chunk // BLOCKS
+    block = chunk // 2
     if repeat == 0:
         kept["gains"] = run(gains_kernel, (f32(width, count, cells),) * 2, (table, rate), scalar=False)
     rden, prefix = kept["gains"]
     drives = []
     for k, state in enumerate(states):
-        kernel = functools.partial(transport_kernel, k * chunk, repeat == 0)
-        at = (lambda i, k=k: (k * BLOCKS + i, 0, 0)) if repeat == 0 else None
-        source = pl.BlockSpec((block, width, cells), at) if repeat == 0 else VMEM
+        if repeat:
+            kernel = functools.partial(transport_kernel, k * chunk)
+            drives.append(run(kernel, f32(width, chunk, cells), (table, state), scalar=False))
+            continue
         drives.append(
             pl.pallas_call(
-                kernel,
-                grid=(BLOCKS if repeat == 0 else 1,),
+                functools.partial(first_transport_kernel, k * chunk),
                 out_shape=f32(width, chunk, cells),
-                in_specs=[VMEM, source],
+                in_specs=[VMEM, HBM],
                 out_specs=VMEM,
+                scratch_shapes=[
+                    pltpu.VMEM((chunk, width, cells), jnp.float32),
+                    pltpu.SemaphoreType.DMA((BLOCKS,)),
+                ],
                 compiler_params=PARAMS,
             )(table, state)
         )
@@ -611,10 +642,10 @@
             rest = [] if k == 0 else [states]
             states = pl.pallas_call(
                 functools.partial(last_kernel, peers, k * chunk),
-                grid=(BLOCKS,),
+                grid=(2,),
                 out_shape=f32(count, width, cells),
                 in_specs=[SMEM] + [VMEM] * 6 + [pl.BlockSpec(memory_space=pl.ANY)] * len(rest),
-                out_specs=pl.BlockSpec((block, width, cells), lambda i, k=k: (k * BLOCKS + i, 0, 0)),
+                out_specs=pl.BlockSpec((block, width, cells), lambda i, k=k: (k * 2 + i, 0, 0)),
                 input_output_aliases={len(args): 0} if rest else {},
                 compiler_params=PARAMS,
             )(*args, *rest)
@@ -625,22 +656,28 @@
     count, width, cells = distribution.shape
     peers = lax.axis_size("gx")
     me = lax.axis_index("gx").astype(jnp.int32).reshape(1)
-    chunk = count // CHUNKS
-    block = chunk // BLOCKS
-    distribution = pltpu.with_memory_space_constraint(distribution, pltpu.HBM)
     lines = 4 * count // LANES
-    outs = (f32(13 * width + lines, cells), f32(TABLE, count, cells))
-    outs += (f32(width, cells), f32(width, cells))
+    far = functools.partial(pltpu.with_memory_space_constraint, memory_space=pltpu.HBM)
+    given = tuple(far(x) for x in (velocity, weights.reshape(1, count), collision, solid, distribution))
     m, table, rate, wall = pl.pallas_call(
-        functools.partial(first_kernel, float(width * peers), count // block),
-        grid=(count // block,),
-        out_shape=outs,
-        in_specs=[VMEM] * 4 + [pl.BlockSpec((block, width, cells), lambda i: (i, 0, 0))],
-        out_specs=(VMEM,) * len(outs),
-        scratch_shapes=(pltpu.VMEM((8, count), jnp.float32), pltpu.VMEM((13, width, SUB, cells), jnp.float32)),
+        functools.partial(first_kernel, float(width * peers)),
+        out_shape=(
+            f32(13 * width + lines, cells),
+            f32(TABLE, count + PAD, cells),
+            f32(width, cells),
+            f32(width, cells),
+        ),
+        in_specs=[HBM] * len(given),
+        out_specs=(VMEM,) * 4,
+        scratch_shapes=[pltpu.VMEM(x.shape, x.dtype) for x in given]
+        + [
+            pltpu.VMEM((SUB, count), jnp.float32),
+            pltpu.VMEM((13, width, SUB, cells), jnp.float32),
+            pltpu.SemaphoreType.DMA((4 + BLOCKS,)),
+        ],
         compiler_params=PARAMS,
-    )(velocity, weights.reshape(1, count), collision, solid, distribution)
-    kept, states = {}, (distribution,) * CHUNKS
+    )(*given)
+    kept, states = {}, given[-1:] * CHUNKS
     for repeat in range(ITERS):
         m, states, macro = iteration(repeat, m, states, table, rate, wall, me, inflow, kept)
     return states, macro

time: 102 us -> 96.5 us (0.946)
  Pallas kernels: 37.7 us -> 34.9 us
  local copies, waits for them, and re-layouts: 4.8 us -> 2.05 us
    pallas_call x7 -> x5, Pallas kernels: 17.7 us -> 13.2 us  [the longest x2 5.15 us: iteration(): pl.pallas_call(functools.partial(first_transport_kernel, k * chunk), out_...]
    unnamed x22 -> x14, local copies, waits for them, and re-layouts: 4.71 us -> 1.96 us
    pallas_call x9 -> x11, Pallas kernels: 20 us -> 21.7 us  [run(): pl.pallas_call(kernel, out_shape=out_shape, in_specs=([SMEM] if scalar el...]
where the time goes in v3:
time: 96.5 us; the launch traced here: 96.2 us
  Pallas kernels  34.9 us (36%)
  waiting for transfers between devices  33.6 us (35%)
  starting transfers between devices  24.2 us (25%)
  local copies, waits for them, and re-layouts  2.05 us (2%)
  between operations  1.04 us (1%)
    ppermute x8, waiting for transfers between devices, gather_over(): got = lax.ppermute(blocks, axis, [(i, i ^ bit) for i in range(size)])  22.1 us
    pallas_call x11, Pallas kernels, run(): pl.pallas_call(kernel, out_shape=out_shape, in_specs=([SMEM] if scalar el...  21.7 us
    ppermute x8, starting transfers between devices, reduce_over(): got.append(lax.ppermute(sent, axis, pairs))  12.9 us
    ppermute x8, waiting for transfers between devices, reduce_over(): got.append(lax.ppermute(sent, axis, pairs))  11.6 us
    ppermute x8, starting transfers between devices, gather_over(): got = lax.ppermute(blocks, axis, [(i, i ^ bit) for i in range(size)])  9.7 us
    pallas_call x2, Pallas kernels, iteration(): pl.pallas_call(functools.partial(first_transport_kernel, k * chunk), out_...  5.15 us
    pallas_call x1, Pallas kernels, per_device(): pl.pallas_call(functools.partial(first_kernel, float(width * peers)), out...  4.3 us
    pallas_call x2, Pallas kernels, iteration(): pl.pallas_call(functools.partial(last_kernel, peers, k * chunk), grid=(2,...  3.71 us
  transfers between devices with their start and end apart: 20, of which 12 were waited for; matrix products, arithmetic and copies ran while one was open for 0% of the time, Pallas kernels for 10%

profile of v3, /device:TPU:0, one launch (start us, length us, event | category | flops | bytes accessed | tf_op | source)
XLA Modules:
  0.0 96.2 jit_solution(2696204089208683093)
XLA Ops:
  0.6 4.3 %shard_map.77 = (f32[120,128]{1,0:T(8,128)S(1)}, f32[10,520,128]{2,1,0:T(8,128)S(1)}, f32[8,128]{1,0:T(8,128)S(1)}, f32[8,128]{1,0:T(8,128)S(1)}) custom-call(f32[3,512]{1,0:T(4,128)} %refs_0_.1, f32[1,512]{1,0:T(1,128)} %bitcast.38, f32[8,128]{1,0:T(8,128)} %refs_2_.1, s32[8,128]{1,0:T(8,128)} %refs_3_.1, f32[512,8,128]{2,1,0:T(8,128)} %dist_ref.3), custom_call_target="tpu_custom_call" | custom-call | tf_op jit(solution)/shard_map/pallas_call | solution.py:662
  4.9 3.1 %collective-permute-start = (f32[120,128]{1,0:T(8,128)S(1)}, f32[120,128]{1,0:T(8,128)S(1)}, u32[]{:S(2)}, u32[]{:S(2)}) collective-permute-start(f32[120,128]{1,0:T(8,128)S(1)} %get-tuple-element.24), channel_id=1, source_target_pairs={{0,4},{4,0},{8,12},{12,8},{16,20},{20,16},{24,28},{28,24},{1,5},{5... | collective-permute-start | bytes 184328 | tf_op jit(solution)/shard_map/ppermute | solution.py:534
  8.0 2.6 %shard_map.79.drive_ref = f32[8,256,128]{2,1,0:T(8,128)S(1)} custom-call(f32[10,520,128]{2,1,0:T(8,128)S(1)} %get-tuple-element.23.t_ref, f32[512,8,128]{2,1,0:T(8,128)} %dist_ref.3), custom_call_target="tpu_custom_call" | custom-call | tf_op jit(solution)/shard_map/pallas_call | solution.py:583
  10.6 0.0 copy-start.3
  10.6 1.0 copy-done.3
  11.6 2.6 %shard_map.82.drive_ref = f32[8,256,128]{2,1,0:T(8,128)S(1)} custom-call(f32[10,520,128]{2,1,0:T(8,128)S(1)} %get-tuple-element.23.t_ref, f32[512,8,128]{2,1,0:T(8,128)} %dist_ref.3), custom_call_target="tpu_custom_call" | custom-call | tf_op jit(solution)/shard_map/pallas_call | solution.py:583
  14.1 0.0 copy-start.1
  14.1 1.0 %copy-done.1 = f32[8,256,128]{2,1,0:T(8,128)} copy-done((f32[8,256,128]{2,1,0:T(8,128)}, f32[8,256,128]{2,1,0:T(8,128)S(1)}, u32[]{:S(2)}) %copy-start.1) | copy-done | bytes 1048600
  15.1 0.9 shard_map.80
  16.0 0.0 collective-permute-done
  16.0 1.6 %collective-permute-start.1 = (f32[136,128]{1,0:T(8,128)S(1)}, f32[136,128]{1,0:T(8,128)S(1)}, u32[]{:S(2)}, u32[]{:S(2)}) collective-permute-start(f32[136,128]{1,0:T(8,128)S(1)} %pad_maximum_fusion.8), channel_id=1, source_target_pairs={{0,8},{4,12},{8,16},{12,20},{16,24},{20,28},{24,0},{28,4},{1,9},{5... | collective-permute-start | bytes 208904 | tf_op jit(solution)/shard_map/ppermute | solution.py:534
  17.7 2.6 %collective-permute-start.2 = (f32[136,128]{1,0:T(8,128)S(1)}, f32[136,128]{1,0:T(8,128)S(1)}, u32[]{:S(2)}, u32[]{:S(2)}) collective-permute-start(f32[136,128]{1,0:T(8,128)S(1)} %pad_maximum_fusion.8), channel_id=1, source_target_pairs={{0,16},{4,20},{8,24},{12,28},{16,0},{20,4},{24,8},{28,12},{1,17},{... | collective-permute-start | bytes 208904 | tf_op jit(solution)/shard_map/ppermute | solution.py:534
  20.3 1.3 %collective-permute-start.3 = (f32[136,128]{1,0:T(8,128)S(1)}, f32[136,128]{1,0:T(8,128)S(1)}, u32[]{:S(2)}, u32[]{:S(2)}) collective-permute-start(f32[136,128]{1,0:T(8,128)S(1)} %pad_maximum_fusion.8), channel_id=1, source_target_pairs={{0,24},{4,28},{8,0},{12,4},{16,8},{20,12},{24,16},{28,20},{1,25},{... | collective-permute-start | bytes 208904 | tf_op jit(solution)/shard_map/ppermute | solution.py:534
  21.6 1.4 %collective-permute-done.1 = f32[136,128]{1,0:T(8,128)S(1)} collective-permute-done((f32[136,128]{1,0:T(8,128)S(1)}, f32[136,128]{1,0:T(8,128)S(1)}, u32[]{:S(2)}, u32[]{:S(2)}) %collective-permute-start.1) | collective-permute-done | bytes 69664 | tf_op jit(solution)/shard_map/ppermute | solution.py:534
  23.1 2.2 %collective-permute-done.2 = f32[136,128]{1,0:T(8,128)S(1)} collective-permute-done((f32[136,128]{1,0:T(8,128)S(1)}, f32[136,128]{1,0:T(8,128)S(1)}, u32[]{:S(2)}, u32[]{:S(2)}) %collective-permute-start.2) | collective-permute-done | bytes 69664 | tf_op jit(solution)/shard_map/ppermute | solution.py:534
  25.3 0.0 collective-permute-done.3
  25.3 0.1 collective-permute-start.4
  25.4 0.8 collective-permute-start.5
  26.3 1.2 %shard_map.78.f_ref = bf16[4096,32]{1,0:T(8,128)(2,1)S(1)} custom-call(f32[8,16,128]{2,1,0:T(8,128)S(1)} %constant_dynamic-update-slice_fusion.v_ref), custom_call_target="tpu_custom_call" | custom-call | tf_op jit(solution)/shard_map/pallas_call | solution.py:41
  27.5 0.0 collective-permute-done.4
  27.5 0.0 collective-permute-done.5
  27.6 0.0 copy-done.4
  27.6 0.0 copy-start.2
  27.6 5.1 %shard_map.81 = (f32[8,256,128]{2,1,0:T(8,128)S(1)}, f32[264,128]{1,0:T(8,128)S(1)}, f32[5,8,128]{2,1,0:T(8,128)}, f32[10,8,128]{2,1,0:T(8,128)S(1)}) custom-call(s32[1]{0:T(128)} %bitcast.me_ref, f32[13,3,128]{2,1,0:T(4,128)S(1)} %get-tuple-element.57.before_ref, f32[13,8,128]{2,1,0:T(8,128)S(1)} %fusion.m_ref, ...), custom_call_target="tpu_custom_call" | custom-call | tf_op jit(solution)/shard_map/pallas_call | solution.py:41
  32.7 0.0 copy-done.2
  32.7 1.2 %shard_map.83 = (f32[8,256,128]{2,1,0:T(8,128)S(1)}, f32[256,128]{1,0:T(8,128)S(1)}) custom-call(f32[10,520,128]{2,1,0:T(8,128)S(1)} %get-tuple-element.23.t_ref, f32[10,8,128]{2,1,0:T(8,128)S(1)} %get-tuple-element.28.field_ref, f32[8,256,128]{2,1,0:T(8,128)S(1)} %copy-done.2, f32[8,512,128]{2,1,0:T(8,128)S(1)} %get-tuple-element.27.rden_ref), custom_call_target="tpu_custom_call" | custom-call | tf_op jit(solution)/shard_map/pallas_call | solution.py:41
  33.9 4.6 %collective-permute-start.6 = (f32[1,256,128]{2,1,0:T(8,128)S(1)}, f32[1,256,128]{2,1,0:T(8,128)S(1)}, u32[]{:S(2)}, u32[]{:S(2)}) collective-permute-start(f32[1,256,128]{2,1,0:T(8,128)S(1)} %bitcast.31), channel_id=1, source_target_pairs={{0,2},{1,3},{2,0},{3,1},{4,6},{5,7},{6,4},{7,5},{8,10},{9,11},{10,... | collective-permute-start | bytes 393224 | tf_op jit(solution)/shard_map/ppermute | solution.py:550
  38.4 4.3 %collective-permute-done.6 = f32[1,256,128]{2,1,0:T(8,128)S(1)} collective-permute-done((f32[1,256,128]{2,1,0:T(8,128)S(1)}, f32[1,256,128]{2,1,0:T(8,128)S(1)}, u32[]{:S(2)}, u32[]{:S(2)}) %collective-permute-start.6) | collective-permute-done | bytes 131104 | tf_op jit(solution)/shard_map/ppermute | solution.py:550
  42.8 0.2 collective-permute-start.7
  43.0 0.6 collective-permute-start.8
  43.6 5.3 %collective-permute-done.8 = f32[1,264,128]{2,1,0:T(8,128)S(1)} collective-permute-done((f32[1,264,128]{2,1,0:T(8,128)S(1)}, f32[1,264,128]{2,1,0:T(8,128)S(1)}, u32[]{:S(2)}, u32[]{:S(2)}) %collective-permute-start.8) | collective-permute-done | bytes 135200 | tf_op jit(solution)/shard_map/ppermute | solution.py:550
  48.9 0.1 collective-permute-start.9
  48.9 0.0 collective-permute-done.7
  49.0 1.4 %collective-permute-done.9 = f32[2,264,128]{2,1,0:T(8,128)S(1)} collective-permute-done((f32[2,264,128]{2,1,0:T(8,128)S(1)}, f32[2,264,128]{2,1,0:T(8,128)S(1)}, u32[]{:S(2)}, u32[]{:S(2)}) %collective-permute-start.9) | collective-permute-done | bytes 270368 | tf_op jit(solution)/shard_map/ppermute | solution.py:550
  50.5 0.0 copy-start
  50.6 1.1 %shard_map.84.g_ref = f32[4,512,128]{2,1,0:T(8,128)S(1)} custom-call(s32[1]{0:T(128)} %bitcast.me_ref, f32[10,520,128]{2,1,0:T(8,128)S(1)} %get-tuple-element.23.t_ref, f32[4,264,128]{2,1,0:T(8,128)S(1)} %pad_maximum_fusion.c_ref), custom_call_target="tpu_custom_call" | custom-call | tf_op jit(solution)/shard_map/pallas_call | solution.py:41
  51.7 1.6 %shard_map.85 = (f32[104,128]{1,0:T(8,128)S(1)}, f32[8,256,128]{2,1,0:T(8,128)S(1)}) custom-call(s32[1]{0:T(128)} %bitcast.me_ref, f32[10,520,128]{2,1,0:T(8,128)S(1)} %get-tuple-element.23.t_ref, f32[4,264,128]{2,1,0:T(8,128)S(1)} %pad_maximum_fusion.c_ref, f32[4,512,128]{2,1,0:T(8,128)S(1)} %shard_map.84.g_ref, f32[2,512,128]{2,1,0:T(8,128)S(1)} %copy-done, ...), custom_call_target="tpu_custom_call" | custom-call | tf_op jit(solution)/shard_map/pallas_call | solution.py:41
  53.3 1.6 %shard_map.86 = (f32[104,128]{1,0:T(8,128)S(1)}, f32[8,256,128]{2,1,0:T(8,128)S(1)}) custom-call(s32[1]{0:T(128)} %bitcast.me_ref, f32[10,520,128]{2,1,0:T(8,128)S(1)} %get-tuple-element.23.t_ref, f32[4,256,128]{2,1,0:T(8,128)S(1)} %pad_maximum_fusion.2.c_ref, f32[4,512,128]{2,1,0:T(8,128)S(1)} %shard_map.84.g_ref, f32[2,512,128]{2,1,0:T(8,128)S(1)} %copy-done, ...), custom_call_target="tpu_custom_call" | custom-call | tf_op jit(solution)/shard_map/pallas_call | solution.py:41
  55.0 0.4 collective-permute-start.10
  55.3 3.8 %collective-permute-done.10 = f32[104,128]{1,0:T(8,128)S(1)} collective-permute-done((f32[104,128]{1,0:T(8,128)S(1)}, f32[104,128]{1,0:T(8,128)S(1)}, u32[]{:S(2)}, u32[]{:S(2)}) %collective-permute-start.10) | collective-permute-done | bytes 53280 | tf_op jit(solution)/shard_map/ppermute | solution.py:534
  59.2 1.4 %collective-permute-start.11 = (f32[104,128]{1,0:T(8,128)S(1)}, f32[104,128]{1,0:T(8,128)S(1)}, u32[]{:S(2)}, u32[]{:S(2)}) collective-permute-start(f32[104,128]{1,0:T(8,128)S(1)} %add.34), channel_id=1, source_target_pairs={{0,8},{4,12},{8,16},{12,20},{16,24},{20,28},{24,0},{28,4},{1,9},{5... | collective-permute-start | bytes 159752 | tf_op jit(solution)/shard_map/ppermute | solution.py:534
  60.6 2.0 %collective-permute-start.12 = (f32[104,128]{1,0:T(8,128)S(1)}, f32[104,128]{1,0:T(8,128)S(1)}, u32[]{:S(2)}, u32[]{:S(2)}) collective-permute-start(f32[104,128]{1,0:T(8,128)S(1)} %add.34), channel_id=1, source_target_pairs={{0,16},{4,20},{8,24},{12,28},{16,0},{20,4},{24,8},{28,12},{1,17},{... | collective-permute-start | bytes 159752 | tf_op jit(solution)/shard_map/ppermute | solution.py:534
  62.5 0.5 collective-permute-start.13
  63.0 2.2 %collective-permute-done.11 = f32[104,128]{1,0:T(8,128)S(1)} collective-permute-done((f32[104,128]{1,0:T(8,128)S(1)}, f32[104,128]{1,0:T(8,128)S(1)}, u32[]{:S(2)}, u32[]{:S(2)}) %collective-permute-start.11) | collective-permute-done | bytes 53280 | tf_op jit(solution)/shard_map/ppermute | solution.py:534
  65.3 1.4 %collective-permute-done.12 = f32[104,128]{1,0:T(8,128)S(1)} collective-permute-done((f32[104,128]{1,0:T(8,128)S(1)}, f32[104,128]{1,0:T(8,128)S(1)}, u32[]{:S(2)}, u32[]{:S(2)}) %collective-permute-start.12) | collective-permute-done | bytes 53280 | tf_op jit(solution)/shard_map/ppermute | solution.py:534
  66.7 0.4 collective-permute-done.13
  67.1 0.1 collective-permute-start.14
  67.2 0.7 collective-permute-start.15
  67.9 1.3 %shard_map.87.drive_ref = f32[8,256,128]{2,1,0:T(8,128)S(1)} custom-call(f32[10,520,128]{2,1,0:T(8,128)S(1)} %get-tuple-element.23.t_ref, f32[8,256,128]{2,1,0:T(8,128)S(1)} %get-tuple-element.36.s_ref), custom_call_target="tpu_custom_call" | custom-call | tf_op jit(solution)/shard_map/pallas_call | solution.py:41
  69.2 1.3 %shard_map.89.drive_ref = f32[8,256,128]{2,1,0:T(8,128)S(1)} custom-call(f32[10,520,128]{2,1,0:T(8,128)S(1)} %get-tuple-element.23.t_ref, f32[8,256,128]{2,1,0:T(8,128)S(1)} %get-tuple-element.38.s_ref), custom_call_target="tpu_custom_call" | custom-call | tf_op jit(solution)/shard_map/pallas_call | solution.py:41
  70.6 0.0 collective-permute-done.14
  70.6 0.0 collective-permute-done.15
  70.6 5.1 %shard_map.88 = (f32[8,256,128]{2,1,0:T(8,128)S(1)}, f32[264,128]{1,0:T(8,128)S(1)}, f32[5,8,128]{2,1,0:T(8,128)}, f32[10,8,128]{2,1,0:T(8,128)S(1)}) custom-call(s32[1]{0:T(128)} %bitcast.me_ref, f32[13,3,128]{2,1,0:T(4,128)S(1)} %get-tuple-element.53.before_ref, f32[13,8,128]{2,1,0:T(8,128)S(1)} %add_bitcast_fusion.m_ref, ...), custom_call_target="tpu_custom_call" | custom-call | tf_op jit(solution)/shard_map/pallas_call | solution.py:41
  75.7 1.2 %shard_map.90 = (f32[8,256,128]{2,1,0:T(8,128)S(1)}, f32[256,128]{1,0:T(8,128)S(1)}) custom-call(f32[10,520,128]{2,1,0:T(8,128)S(1)} %get-tuple-element.23.t_ref, f32[10,8,128]{2,1,0:T(8,128)S(1)} %get-tuple-element.37.field_ref, f32[8,256,128]{2,1,0:T(8,128)S(1)} %shard_map.89.drive_ref, f32[8,512,128]{2,1,0:T(8,128)S(1)} %get-tuple-element.27.rden_ref), custom_call_target="tpu_custom_call" | custom-call | tf_op jit(solution)/shard_map/pallas_call | solution.py:41
  77.0 3.4 %collective-permute-start.16 = (f32[1,256,128]{2,1,0:T(8,128)S(1)}, f32[1,256,128]{2,1,0:T(8,128)S(1)}, u32[]{:S(2)}, u32[]{:S(2)}) collective-permute-start(f32[1,256,128]{2,1,0:T(8,128)S(1)} %bitcast.28), channel_id=1, source_target_pairs={{0,2},{1,3},{2,0},{3,1},{4,6},{5,7},{6,4},{7,5},{8,10},{9,11},{10,... | collective-permute-start | bytes 393224 | tf_op jit(solution)/shard_map/ppermute | solution.py:550
  80.4 4.3 %collective-permute-done.16 = f32[1,256,128]{2,1,0:T(8,128)S(1)} collective-permute-done((f32[1,256,128]{2,1,0:T(8,128)S(1)}, f32[1,256,128]{2,1,0:T(8,128)S(1)}, u32[]{:S(2)}, u32[]{:S(2)}) %collective-permute-start.16) | collective-permute-done | bytes 131104 | tf_op jit(solution)/shard_map/ppermute | solution.py:550
  84.7 0.1 collective-permute-start.17
  84.9 0.7 collective-permute-start.18
  85.5 5.3 %collective-permute-done.18 = f32[1,264,128]{2,1,0:T(8,128)S(1)} collective-permute-done((f32[1,264,128]{2,1,0:T(8,128)S(1)}, f32[1,264,128]{2,1,0:T(8,128)S(1)}, u32[]{:S(2)}, u32[]{:S(2)}) %collective-permute-start.18) | collective-permute-done | bytes 135200 | tf_op jit(solution)/shard_map/ppermute | solution.py:550
  90.8 0.1 collective-permute-start.19
  90.9 0.0 collective-permute-done.17
  91.0 1.4 %collective-permute-done.19 = f32[2,264,128]{2,1,0:T(8,128)S(1)} collective-permute-done((f32[2,264,128]{2,1,0:T(8,128)S(1)}, f32[2,264,128]{2,1,0:T(8,128)S(1)}, u32[]{:S(2)}, u32[]{:S(2)}) %collective-permute-start.19) | collective-permute-done | bytes 270368 | tf_op jit(solution)/shard_map/ppermute | solution.py:550
  92.5 1.9 %shard_map.91.refs_0_ = f32[512,8,128]{2,1,0:T(8,128)} custom-call(s32[1]{0:T(128)} %bitcast.me_ref, f32[10,520,128]{2,1,0:T(8,128)S(1)} %get-tuple-element.23.t_ref, f32[4,264,128]{2,1,0:T(8,128)S(1)} %pad_maximum_fusion.1.c_ref, f32[4,512,128]{2,1,0:T(8,128)S(1)} %shard_map.84.g_ref, f32[2,512,128]{2,1,0:T(8,128)S(1)} %copy-done, ...), custom_call_target="tpu_custom_call" | custom-call | tf_op jit(solution)/shard_map/pallas_call | solution.py:643
  94.4 1.9 %shard_map.92 = f32[512,8,128]{2,1,0:T(8,128)} custom-call(s32[1]{0:T(128)} %bitcast.me_ref, f32[10,520,128]{2,1,0:T(8,128)S(1)} %get-tuple-element.23.t_ref, f32[4,256,128]{2,1,0:T(8,128)S(1)} %pad_maximum_fusion.3.c_ref, f32[4,512,128]{2,1,0:T(8,128)S(1)} %shard_map.84.g_ref, f32[2,512,128]{2,1,0:T(8,128)S(1)} %copy-done, ...), custom_call_target="tpu_custom_call", output_to_operand_aliasing={{}: (7, {})} | custom-call | tf_op jit(solution)/shard_map/pallas_call | solution.py:643
  (34 shorter events, 0.5 us)
Async XLA Ops:
  4.9 11.0 %collective-permute-start = (f32[120,128]{1,0:T(8,128)S(1)}, f32[120,128]{1,0:T(8,128)S(1)}, u32[]{:S(2)}, u32[]{:S(2)}) collective-permute-start(f32[120,128]{1,0:T(8,128)S(1)} %get-tuple-element.24), channel_id=1, source_target_pairs={{0,4},{4,0},{8,12},{12,8},{16,20},{20,16},{24,28},{28,24},{1,5},{5... | collective-permute-start | bytes 184328 | tf_op jit(solution)/shard_map/ppermute | solution.py:534
  10.6 1.0 %copy-start.3 = (f32[8,256,128]{2,1,0:T(8,128)}, f32[8,256,128]{2,1,0:T(8,128)S(1)}, u32[]{:S(2)}) copy-start(f32[8,256,128]{2,1,0:T(8,128)S(1)} %shard_map.79.drive_ref) | copy-start | bytes 3145732
  14.1 1.0 %copy-start.1 = (f32[8,256,128]{2,1,0:T(8,128)}, f32[8,256,128]{2,1,0:T(8,128)S(1)}, u32[]{:S(2)}) copy-start(f32[8,256,128]{2,1,0:T(8,128)S(1)} %shard_map.82.drive_ref) | copy-start | bytes 3145732
  15.1 12.5 %copy-start.4 = (f32[8,256,128]{2,1,0:T(8,128)S(1)}, f32[8,256,128]{2,1,0:T(8,128)}, u32[]{:S(2)}) copy-start(f32[8,256,128]{2,1,0:T(8,128)} %copy-done.3) | copy-start | bytes 3145732
  16.0 7.0 %collective-permute-start.1 = (f32[136,128]{1,0:T(8,128)S(1)}, f32[136,128]{1,0:T(8,128)S(1)}, u32[]{:S(2)}, u32[]{:S(2)}) collective-permute-start(f32[136,128]{1,0:T(8,128)S(1)} %pad_maximum_fusion.8), channel_id=1, source_target_pairs={{0,8},{4,12},{8,16},{12,20},{16,24},{20,28},{24,0},{28,4},{1,9},{5... | collective-permute-start | bytes 208904 | tf_op jit(solution)/shard_map/ppermute | solution.py:534
  17.7 7.6 %collective-permute-start.2 = (f32[136,128]{1,0:T(8,128)S(1)}, f32[136,128]{1,0:T(8,128)S(1)}, u32[]{:S(2)}, u32[]{:S(2)}) collective-permute-start(f32[136,128]{1,0:T(8,128)S(1)} %pad_maximum_fusion.8), channel_id=1, source_target_pairs={{0,16},{4,20},{8,24},{12,28},{16,0},{20,4},{24,8},{28,12},{1,17},{... | collective-permute-start | bytes 208904 | tf_op jit(solution)/shard_map/ppermute | solution.py:534
  20.3 5.0 %collective-permute-start.3 = (f32[136,128]{1,0:T(8,128)S(1)}, f32[136,128]{1,0:T(8,128)S(1)}, u32[]{:S(2)}, u32[]{:S(2)}) collective-permute-start(f32[136,128]{1,0:T(8,128)S(1)} %pad_maximum_fusion.8), channel_id=1, source_target_pairs={{0,24},{4,28},{8,0},{12,4},{16,8},{20,12},{24,16},{28,20},{1,25},{... | collective-permute-start | bytes 208904 | tf_op jit(solution)/shard_map/ppermute | solution.py:534
  25.3 2.2 %collective-permute-start.4 = (f32[13,3,128]{2,1,0:T(4,128)S(1)}, f32[13,3,128]{2,1,0:T(4,128)S(1)}, u32[]{:S(2)}, u32[]{:S(2)}) collective-permute-start(f32[13,3,128]{2,1,0:T(4,128)S(1)} %get-tuple-element.59), channel_id=1, source_target_pairs={{0,1},{1,0},{2,3},{3,2},{4,5},{5,4},{6,7},{7,6},{8,9},{9,8},{10,11... | collective-permute-start | bytes 59912 | tf_op jit(solution)/shard_map/ppermute | solution.py:564
  25.4 2.1 %collective-permute-start.5 = (f32[13,3,128]{2,1,0:T(4,128)S(1)}, f32[13,3,128]{2,1,0:T(4,128)S(1)}, u32[]{:S(2)}, u32[]{:S(2)}) collective-permute-start(f32[13,3,128]{2,1,0:T(4,128)S(1)} %get-tuple-element.58), channel_id=1, source_target_pairs={{1,2},{2,1},{5,6},{6,5},{9,10},{10,9},{13,14},{14,13},{17,18},{18,... | collective-permute-start | bytes 59912 | tf_op jit(solution)/shard_map/ppermute | solution.py:563
  27.6 5.1 %copy-start.2 = (f32[8,256,128]{2,1,0:T(8,128)S(1)}, f32[8,256,128]{2,1,0:T(8,128)}, u32[]{:S(2)}) copy-start(f32[8,256,128]{2,1,0:T(8,128)} %copy-done.1) | copy-start | bytes 3145732
  33.9 8.9 %collective-permute-start.6 = (f32[1,256,128]{2,1,0:T(8,128)S(1)}, f32[1,256,128]{2,1,0:T(8,128)S(1)}, u32[]{:S(2)}, u32[]{:S(2)}) collective-permute-start(f32[1,256,128]{2,1,0:T(8,128)S(1)} %bitcast.31), channel_id=1, source_target_pairs={{0,2},{1,3},{2,0},{3,1},{4,6},{5,7},{6,4},{7,5},{8,10},{9,11},{10,... | collective-permute-start | bytes 393224 | tf_op jit(solution)/shard_map/ppermute | solution.py:550
  42.8 6.2 %collective-permute-start.7 = (f32[2,256,128]{2,1,0:T(8,128)S(1)}, f32[2,256,128]{2,1,0:T(8,128)S(1)}, u32[]{:S(2)}, u32[]{:S(2)}) collective-permute-start(f32[2,256,128]{2,1,0:T(8,128)S(1)} %pad_maximum_fusion.6), channel_id=1, source_target_pairs={{0,1},{1,0},{2,3},{3,2},{4,5},{5,4},{6,7},{7,6},{8,9},{9,8},{10,11... | collective-permute-start | bytes 786440 | tf_op jit(solution)/shard_map/ppermute | solution.py:550
  43.0 5.9 %collective-permute-start.8 = (f32[1,264,128]{2,1,0:T(8,128)S(1)}, f32[1,264,128]{2,1,0:T(8,128)S(1)}, u32[]{:S(2)}, u32[]{:S(2)}) collective-permute-start(f32[1,264,128]{2,1,0:T(8,128)S(1)} %bitcast.25), channel_id=1, source_target_pairs={{0,2},{1,3},{2,0},{3,1},{4,6},{5,7},{6,4},{7,5},{8,10},{9,11},{10,... | collective-permute-start | bytes 405512 | tf_op jit(solution)/shard_map/ppermute | solution.py:550
  48.9 1.6 %collective-permute-start.9 = (f32[2,264,128]{2,1,0:T(8,128)S(1)}, f32[2,264,128]{2,1,0:T(8,128)S(1)}, u32[]{:S(2)}, u32[]{:S(2)}) collective-permute-start(f32[2,264,128]{2,1,0:T(8,128)S(1)} %pad_maximum_fusion.4), channel_id=1, source_target_pairs={{0,1},{1,0},{2,3},{3,2},{4,5},{5,4},{6,7},{7,6},{8,9},{9,8},{10,11... | collective-permute-start | bytes 811016 | tf_op jit(solution)/shard_map/ppermute | solution.py:550
  50.5 1.2 %copy-start = (f32[2,512,128]{2,1,0:T(8,128)S(1)}, f32[2,512,128]{2,1,0:T(8,128)}, u32[]{:S(2)}) copy-start(f32[2,512,128]{2,1,0:T(8,128)} %flow_ref.7) | copy-start | bytes 1572868
  55.0 4.2 %collective-permute-start.10 = (f32[104,128]{1,0:T(8,128)S(1)}, f32[104,128]{1,0:T(8,128)S(1)}, u32[]{:S(2)}, u32[]{:S(2)}) collective-permute-start(f32[104,128]{1,0:T(8,128)S(1)} %get-tuple-element.35), channel_id=1, source_target_pairs={{0,4},{4,0},{8,12},{12,8},{16,20},{20,16},{24,28},{28,24},{1,5},{5... | collective-permute-start | bytes 159752 | tf_op jit(solution)/shard_map/ppermute | solution.py:534
  59.2 6.1 %collective-permute-start.11 = (f32[104,128]{1,0:T(8,128)S(1)}, f32[104,128]{1,0:T(8,128)S(1)}, u32[]{:S(2)}, u32[]{:S(2)}) collective-permute-start(f32[104,128]{1,0:T(8,128)S(1)} %add.34), channel_id=1, source_target_pairs={{0,8},{4,12},{8,16},{12,20},{16,24},{20,28},{24,0},{28,4},{1,9},{5... | collective-permute-start | bytes 159752 | tf_op jit(solution)/shard_map/ppermute | solution.py:534
  60.6 6.1 %collective-permute-start.12 = (f32[104,128]{1,0:T(8,128)S(1)}, f32[104,128]{1,0:T(8,128)S(1)}, u32[]{:S(2)}, u32[]{:S(2)}) collective-permute-start(f32[104,128]{1,0:T(8,128)S(1)} %add.34), channel_id=1, source_target_pairs={{0,16},{4,20},{8,24},{12,28},{16,0},{20,4},{24,8},{28,12},{1,17},{... | collective-permute-start | bytes 159752 | tf_op jit(solution)/shard_map/ppermute | solution.py:534
  62.5 4.6 %collective-permute-start.13 = (f32[104,128]{1,0:T(8,128)S(1)}, f32[104,128]{1,0:T(8,128)S(1)}, u32[]{:S(2)}, u32[]{:S(2)}) collective-permute-start(f32[104,128]{1,0:T(8,128)S(1)} %add.34), channel_id=1, source_target_pairs={{0,24},{4,28},{8,0},{12,4},{16,8},{20,12},{24,16},{28,20},{1,25},{... | collective-permute-start | bytes 159752 | tf_op jit(solution)/shard_map/ppermute | solution.py:534
  67.1 3.4 %collective-permute-start.14 = (f32[13,3,128]{2,1,0:T(4,128)S(1)}, f32[13,3,128]{2,1,0:T(4,128)S(1)}, u32[]{:S(2)}, u32[]{:S(2)}) collective-permute-start(f32[13,3,128]{2,1,0:T(4,128)S(1)} %get-tuple-element.55), channel_id=1, source_target_pairs={{0,1},{1,0},{2,3},{3,2},{4,5},{5,4},{6,7},{7,6},{8,9},{9,8},{10,11... | collective-permute-start | bytes 59912 | tf_op jit(solution)/shard_map/ppermute | solution.py:564
  67.2 3.4 %collective-permute-start.15 = (f32[13,3,128]{2,1,0:T(4,128)S(1)}, f32[13,3,128]{2,1,0:T(4,128)S(1)}, u32[]{:S(2)}, u32[]{:S(2)}) collective-permute-start(f32[13,3,128]{2,1,0:T(4,128)S(1)} %get-tuple-element.54), channel_id=1, source_target_pairs={{1,2},{2,1},{5,6},{6,5},{9,10},{10,9},{13,14},{14,13},{17,18},{18,... | collective-permute-start | bytes 59912 | tf_op jit(solution)/shard_map/ppermute | solution.py:563
  77.0 7.7 %collective-permute-start.16 = (f32[1,256,128]{2,1,0:T(8,128)S(1)}, f32[1,256,128]{2,1,0:T(8,128)S(1)}, u32[]{:S(2)}, u32[]{:S(2)}) collective-permute-start(f32[1,256,128]{2,1,0:T(8,128)S(1)} %bitcast.28), channel_id=1, source_target_pairs={{0,2},{1,3},{2,0},{3,1},{4,6},{5,7},{6,4},{7,5},{8,10},{9,11},{10,... | collective-permute-start | bytes 393224 | tf_op jit(solution)/shard_map/ppermute | solution.py:550
  84.7 6.2 %collective-permute-start.17 = (f32[2,256,128]{2,1,0:T(8,128)S(1)}, f32[2,256,128]{2,1,0:T(8,128)S(1)}, u32[]{:S(2)}, u32[]{:S(2)}) collective-permute-start(f32[2,256,128]{2,1,0:T(8,128)S(1)} %pad_maximum_fusion.7), channel_id=1, source_target_pairs={{0,1},{1,0},{2,3},{3,2},{4,5},{5,4},{6,7},{7,6},{8,9},{9,8},{10,11... | collective-permute-start | bytes 786440 | tf_op jit(solution)/shard_map/ppermute | solution.py:550
  84.9 5.9 %collective-permute-start.18 = (f32[1,264,128]{2,1,0:T(8,128)S(1)}, f32[1,264,128]{2,1,0:T(8,128)S(1)}, u32[]{:S(2)}, u32[]{:S(2)}) collective-permute-start(f32[1,264,128]{2,1,0:T(8,128)S(1)} %bitcast.22), channel_id=1, source_target_pairs={{0,2},{1,3},{2,0},{3,1},{4,6},{5,7},{6,4},{7,5},{8,10},{9,11},{10,... | collective-permute-start | bytes 405512 | tf_op jit(solution)/shard_map/ppermute | solution.py:550
  90.8 1.6 %collective-permute-start.19 = (f32[2,264,128]{2,1,0:T(8,128)S(1)}, f32[2,264,128]{2,1,0:T(8,128)S(1)}, u32[]{:S(2)}, u32[]{:S(2)}) collective-permute-start(f32[2,264,128]{2,1,0:T(8,128)S(1)} %pad_maximum_fusion.5), channel_id=1, source_target_pairs={{0,1},{1,0},{2,3},{3,2},{4,5},{5,4},{6,7},{7,6},{8,9},{9,8},{10,11... | collective-permute-start | bytes 811016 | tf_op jit(solution)/shard_map/ppermute | solution.py:550

commit v4 on v3

--- a/solution.py
+++ b/solution.py
@@ -177,19 +177,21 @@
         rows = pl.ds(pl.multiple_of(g * SUB, SUB), SUB)
         base = t_ref[BASE, rows, :]
         gain = t_ref[FA, rows, :] + t_ref[BA, rows, :]
-        for d in range(peers):
-            slab = jnp.ones_like(gain)
-            for x in range(0, width, 2):
-                product = base + c_ref[d ^ me, below + x : below + x + 1, :]
-                power = gain
-                if x + 1 < width:
-                    product = product * (base + c_ref[d ^ me, below + x + 1 : below + x + 2, :])
-                    power = power * gain
-                slab = slab * (power / product)
-            g_ref[d, rows, :] = slab
+        for other in range(1, peers):
+            products, powers = [], []
+            for x in range(width):
+                products.append(base + c_ref[other, below + x : below + x + 1, :])
+                powers.append(gain)
+            g_ref[other ^ me, rows, :] = times(powers) / times(products)
         return carry
 
     lax.fori_loop(0, count // SUB, step, 0, unroll=2)
+
+
+def times(values):
+    while len(values) > 1:
+        values = [a * b for a, b in zip(values[::2], values[1::2])] + values[len(values) // 2 * 2 :]
+    return values[0]
 
 
 def features_kernel(v_ref, f_ref, row_ref):
@@ -491,21 +493,30 @@
 
 
 def last_kernel(peers, first, me_ref, t_ref, c_ref, g_ref, flow_ref, s_ref, p_ref, *refs):
-    out_ref = refs[-1]
-    width, block = out_ref.shape[1], out_ref.shape[0]
+    out_ref, held_ref, sem = refs[-3:]
+    count, width = held_ref.shape[0], held_ref.shape[1]
+    block = count // BLOCKS
     me = me_ref[0]
-    start = pl.program_id(0) * block
-
-    def step(g, carry):
-        rows = pl.ds(pl.multiple_of(start + g * SUB, SUB), SUB)
-        wide = pl.ds(pl.multiple_of(first + start + g * SUB, SUB), SUB)
-        out = pl.ds(pl.multiple_of(g * SUB, SUB), SUB)
-        enter = entering(peers, me, first, rows, t_ref, c_ref, g_ref, flow_ref)
-        for x in range(width):
-            out_ref[out, x, :] = s_ref[x, rows, :] + p_ref[x, wide, :] * enter
-        return carry
-
-    lax.fori_loop(0, block // SUB, step, 0, unroll=2)
+    copies = [
+        pltpu.make_async_copy(
+            held_ref.at[pl.ds(k * block, block)], out_ref.at[pl.ds(first + k * block, block)], sem.at[k]
+        )
+        for k in range(BLOCKS)
+    ]
+    for k, copy in enumerate(copies):
+
+        def step(g, carry, k=k):
+            rows = pl.ds(pl.multiple_of(k * block + g * SUB, SUB), SUB)
+            wide = pl.ds(pl.multiple_of(first + k * block + g * SUB, SUB), SUB)
+            enter = entering(peers, me, first, rows, t_ref, c_ref, g_ref, flow_ref)
+            for x in range(width):
+                held_ref[rows, x, :] = s_ref[x, rows, :] + p_ref[x, wide, :] * enter
+            return carry
+
+        lax.fori_loop(0, block // SUB, step, 0, unroll=4)
+        copy.start()
+    for copy in copies:
+        copy.wait()
 
 
 def stages(size):
@@ -569,7 +580,6 @@
     width, cells = rate.shape
     count, peers = table.shape[1] - PAD, lax.axis_size("gx")
     chunk = count // len(states)
-    block = chunk // 2
     if repeat == 0:
         kept["gains"] = run(gains_kernel, (f32(width, count, cells),) * 2, (table, rate), scalar=False)
     rden, prefix = kept["gains"]
@@ -642,10 +652,13 @@
             rest = [] if k == 0 else [states]
             states = pl.pallas_call(
                 functools.partial(last_kernel, peers, k * chunk),
-                grid=(2,),
                 out_shape=f32(count, width, cells),
-                in_specs=[SMEM] + [VMEM] * 6 + [pl.BlockSpec(memory_space=pl.ANY)] * len(rest),
-                out_specs=pl.BlockSpec((block, width, cells), lambda i, k=k: (k * 2 + i, 0, 0)),
+                in_specs=[SMEM] + [VMEM] * 6 + [HBM] * len(rest),
+                out_specs=HBM,
+                scratch_shapes=[
+                    pltpu.VMEM((chunk, width, cells), jnp.float32),
+                    pltpu.SemaphoreType.DMA((BLOCKS,)),
+                ],
                 input_output_aliases={len(args): 0} if rest else {},
                 compiler_params=PARAMS,
             )(*args, *rest)

time: 96.5 us -> 96 us (level)
  no operation moved by 1% of the time
where the time goes in v4:
time: 96 us; the launch traced here: 95.7 us
  Pallas kernels  34 us (35%)
  waiting for transfers between devices  33.6 us (35%)
  starting transfers between devices  24.2 us (25%)
  local copies, waits for them, and re-layouts  2.22 us (2%)
  between operations  1.2 us (1%)
    ppermute x8, waiting for transfers between devices, gather_over(): got = lax.ppermute(blocks, axis, [(i, i ^ bit) for i in range(size)])  22.1 us
    pallas_call x11, Pallas kernels, run(): pl.pallas_call(kernel, out_shape=out_shape, in_specs=([SMEM] if scalar el...  21.4 us
    ppermute x8, starting transfers between devices, reduce_over(): got.append(lax.ppermute(sent, axis, pairs))  12.9 us
    ppermute x8, waiting for transfers between devices, reduce_over(): got.append(lax.ppermute(sent, axis, pairs))  11.6 us
    ppermute x8, starting transfers between devices, gather_over(): got = lax.ppermute(blocks, axis, [(i, i ^ bit) for i in range(size)])  9.71 us
    pallas_call x2, Pallas kernels, iteration(): pl.pallas_call(functools.partial(first_transport_kernel, k * chunk), out_...  5.15 us
    pallas_call x1, Pallas kernels, per_device(): pl.pallas_call(functools.partial(first_kernel, float(width * peers)), out...  4.3 us
    pallas_call x2, Pallas kernels, iteration(): pl.pallas_call(functools.partial(last_kernel, peers, k * chunk), out_shap...  3.17 us
  transfers between devices with their start and end apart: 20, of which 12 were waited for; matrix products, arithmetic and copies ran while one was open for 0% of the time, Pallas kernels for 10%

profile of v4, /device:TPU:0, one launch (start us, length us, event | category | flops | bytes accessed | tf_op | source)
XLA Modules:
  0.0 95.7 jit_solution(16706904722135744247)
XLA Ops:
  0.6 4.3 %shard_map.77 = (f32[120,128]{1,0:T(8,128)S(1)}, f32[10,520,128]{2,1,0:T(8,128)S(1)}, f32[8,128]{1,0:T(8,128)S(1)}, f32[8,128]{1,0:T(8,128)S(1)}) custom-call(f32[3,512]{1,0:T(4,128)} %refs_0_.1, f32[1,512]{1,0:T(1,128)} %bitcast.38, f32[8,128]{1,0:T(8,128)} %refs_2_.1, s32[8,128]{1,0:T(8,128)} %refs_3_.1, f32[512,8,128]{2,1,0:T(8,128)} %dist_ref.3), custom_call_target="tpu_custom_call" | custom-call | tf_op jit(solution)/shard_map/pallas_call | solution.py:675
  4.9 3.1 %collective-permute-start = (f32[120,128]{1,0:T(8,128)S(1)}, f32[120,128]{1,0:T(8,128)S(1)}, u32[]{:S(2)}, u32[]{:S(2)}) collective-permute-start(f32[120,128]{1,0:T(8,128)S(1)} %get-tuple-element.24), channel_id=1, source_target_pairs={{0,4},{4,0},{8,12},{12,8},{16,20},{20,16},{24,28},{28,24},{1,5},{5... | collective-permute-start | bytes 184328 | tf_op jit(solution)/shard_map/ppermute | solution.py:545
  8.0 2.6 %shard_map.79.drive_ref = f32[8,256,128]{2,1,0:T(8,128)S(1)} custom-call(f32[10,520,128]{2,1,0:T(8,128)S(1)} %get-tuple-element.23.t_ref, f32[512,8,128]{2,1,0:T(8,128)} %dist_ref.3), custom_call_target="tpu_custom_call" | custom-call | tf_op jit(solution)/shard_map/pallas_call | solution.py:593
  10.6 0.0 copy-start.3
  10.6 1.0 %copy-done.3 = f32[8,256,128]{2,1,0:T(8,128)} copy-done((f32[8,256,128]{2,1,0:T(8,128)}, f32[8,256,128]{2,1,0:T(8,128)S(1)}, u32[]{:S(2)}) %copy-start.3) | copy-done | bytes 1048600
  11.6 2.6 %shard_map.82.drive_ref = f32[8,256,128]{2,1,0:T(8,128)S(1)} custom-call(f32[10,520,128]{2,1,0:T(8,128)S(1)} %get-tuple-element.23.t_ref, f32[512,8,128]{2,1,0:T(8,128)} %dist_ref.3), custom_call_target="tpu_custom_call" | custom-call | tf_op jit(solution)/shard_map/pallas_call | solution.py:593
  14.1 0.0 copy-start.1
  14.1 1.0 %copy-done.1 = f32[8,256,128]{2,1,0:T(8,128)} copy-done((f32[8,256,128]{2,1,0:T(8,128)}, f32[8,256,128]{2,1,0:T(8,128)S(1)}, u32[]{:S(2)}) %copy-start.1) | copy-done | bytes 1048600
  15.1 0.9 shard_map.80
  16.0 0.0 collective-permute-done
  16.0 1.6 %collective-permute-start.1 = (f32[136,128]{1,0:T(8,128)S(1)}, f32[136,128]{1,0:T(8,128)S(1)}, u32[]{:S(2)}, u32[]{:S(2)}) collective-permute-start(f32[136,128]{1,0:T(8,128)S(1)} %pad_maximum_fusion.8), channel_id=1, source_target_pairs={{0,8},{4,12},{8,16},{12,20},{16,24},{20,28},{24,0},{28,4},{1,9},{5... | collective-permute-start | bytes 208904 | tf_op jit(solution)/shard_map/ppermute | solution.py:545
  17.7 2.6 %collective-permute-start.2 = (f32[136,128]{1,0:T(8,128)S(1)}, f32[136,128]{1,0:T(8,128)S(1)}, u32[]{:S(2)}, u32[]{:S(2)}) collective-permute-start(f32[136,128]{1,0:T(8,128)S(1)} %pad_maximum_fusion.8), channel_id=1, source_target_pairs={{0,16},{4,20},{8,24},{12,28},{16,0},{20,4},{24,8},{28,12},{1,17},{... | collective-permute-start | bytes 208904 | tf_op jit(solution)/shard_map/ppermute | solution.py:545
  20.3 1.3 %collective-permute-start.3 = (f32[136,128]{1,0:T(8,128)S(1)}, f32[136,128]{1,0:T(8,128)S(1)}, u32[]{:S(2)}, u32[]{:S(2)}) collective-permute-start(f32[136,128]{1,0:T(8,128)S(1)} %pad_maximum_fusion.8), channel_id=1, source_target_pairs={{0,24},{4,28},{8,0},{12,4},{16,8},{20,12},{24,16},{28,20},{1,25},{... | collective-permute-start | bytes 208904 | tf_op jit(solution)/shard_map/ppermute | solution.py:545
  21.6 1.4 %collective-permute-done.1 = f32[136,128]{1,0:T(8,128)S(1)} collective-permute-done((f32[136,128]{1,0:T(8,128)S(1)}, f32[136,128]{1,0:T(8,128)S(1)}, u32[]{:S(2)}, u32[]{:S(2)}) %collective-permute-start.1) | collective-permute-done | bytes 69664 | tf_op jit(solution)/shard_map/ppermute | solution.py:545
  23.1 2.2 %collective-permute-done.2 = f32[136,128]{1,0:T(8,128)S(1)} collective-permute-done((f32[136,128]{1,0:T(8,128)S(1)}, f32[136,128]{1,0:T(8,128)S(1)}, u32[]{:S(2)}, u32[]{:S(2)}) %collective-permute-start.2) | collective-permute-done | bytes 69664 | tf_op jit(solution)/shard_map/ppermute | solution.py:545
  25.3 0.0 collective-permute-done.3
  25.3 0.1 collective-permute-start.4
  25.4 0.8 collective-permute-start.5
  26.3 1.2 %shard_map.78.f_ref = bf16[4096,32]{1,0:T(8,128)(2,1)S(1)} custom-call(f32[8,16,128]{2,1,0:T(8,128)S(1)} %constant_dynamic-update-slice_fusion.v_ref), custom_call_target="tpu_custom_call" | custom-call | tf_op jit(solution)/shard_map/pallas_call | solution.py:41
  27.5 0.0 collective-permute-done.4
  27.5 0.0 collective-permute-done.5
  27.6 0.0 copy-done.4
  27.6 0.0 copy-start.2
  27.6 5.1 %shard_map.81 = (f32[8,256,128]{2,1,0:T(8,128)S(1)}, f32[264,128]{1,0:T(8,128)S(1)}, f32[5,8,128]{2,1,0:T(8,128)}, f32[10,8,128]{2,1,0:T(8,128)S(1)}) custom-call(s32[1]{0:T(128)} %bitcast.me_ref, f32[13,3,128]{2,1,0:T(4,128)S(1)} %get-tuple-element.57.before_ref, f32[13,8,128]{2,1,0:T(8,128)S(1)} %fusion.m_ref, ...), custom_call_target="tpu_custom_call" | custom-call | tf_op jit(solution)/shard_map/pallas_call | solution.py:41
  32.7 1.2 %shard_map.83 = (f32[8,256,128]{2,1,0:T(8,128)S(1)}, f32[256,128]{1,0:T(8,128)S(1)}) custom-call(f32[10,520,128]{2,1,0:T(8,128)S(1)} %get-tuple-element.23.t_ref, f32[10,8,128]{2,1,0:T(8,128)S(1)} %get-tuple-element.28.field_ref, f32[8,256,128]{2,1,0:T(8,128)S(1)} %copy-done.2, f32[8,512,128]{2,1,0:T(8,128)S(1)} %get-tuple-element.27.rden_ref), custom_call_target="tpu_custom_call" | custom-call | tf_op jit(solution)/shard_map/pallas_call | solution.py:41
  33.9 4.6 %collective-permute-start.6 = (f32[1,256,128]{2,1,0:T(8,128)S(1)}, f32[1,256,128]{2,1,0:T(8,128)S(1)}, u32[]{:S(2)}, u32[]{:S(2)}) collective-permute-start(f32[1,256,128]{2,1,0:T(8,128)S(1)} %bitcast.31), channel_id=1, source_target_pairs={{0,2},{1,3},{2,0},{3,1},{4,6},{5,7},{6,4},{7,5},{8,10},{9,11},{10,... | collective-permute-start | bytes 393224 | tf_op jit(solution)/shard_map/ppermute | solution.py:561
  38.4 4.3 %collective-permute-done.6 = f32[1,256,128]{2,1,0:T(8,128)S(1)} collective-permute-done((f32[1,256,128]{2,1,0:T(8,128)S(1)}, f32[1,256,128]{2,1,0:T(8,128)S(1)}, u32[]{:S(2)}, u32[]{:S(2)}) %collective-permute-start.6) | collective-permute-done | bytes 131104 | tf_op jit(solution)/shard_map/ppermute | solution.py:561
  42.8 0.2 collective-permute-start.7
  43.0 0.6 collective-permute-start.8
  43.6 5.3 %collective-permute-done.8 = f32[1,264,128]{2,1,0:T(8,128)S(1)} collective-permute-done((f32[1,264,128]{2,1,0:T(8,128)S(1)}, f32[1,264,128]{2,1,0:T(8,128)S(1)}, u32[]{:S(2)}, u32[]{:S(2)}) %collective-permute-start.8) | collective-permute-done | bytes 135200 | tf_op jit(solution)/shard_map/ppermute | solution.py:561
  48.9 0.1 collective-permute-start.9
  48.9 0.0 collective-permute-done.7
  49.0 1.4 %collective-permute-done.9 = f32[2,264,128]{2,1,0:T(8,128)S(1)} collective-permute-done((f32[2,264,128]{2,1,0:T(8,128)S(1)}, f32[2,264,128]{2,1,0:T(8,128)S(1)}, u32[]{:S(2)}, u32[]{:S(2)}) %collective-permute-start.9) | collective-permute-done | bytes 270368 | tf_op jit(solution)/shard_map/ppermute | solution.py:561
  50.5 0.0 copy-start
  50.6 0.9 shard_map.84.g_ref
  51.4 0.2 copy-done
  51.6 1.6 %shard_map.85 = (f32[104,128]{1,0:T(8,128)S(1)}, f32[8,256,128]{2,1,0:T(8,128)S(1)}) custom-call(s32[1]{0:T(128)} %bitcast.me_ref, f32[10,520,128]{2,1,0:T(8,128)S(1)} %get-tuple-element.23.t_ref, f32[4,264,128]{2,1,0:T(8,128)S(1)} %pad_maximum_fusion.c_ref, f32[4,512,128]{2,1,0:T(8,128)S(1)} %shard_map.84.g_ref, f32[2,512,128]{2,1,0:T(8,128)S(1)} %copy-done, ...), custom_call_target="tpu_custom_call" | custom-call | tf_op jit(solution)/shard_map/pallas_call | solution.py:41
  53.2 1.6 %shard_map.86 = (f32[104,128]{1,0:T(8,128)S(1)}, f32[8,256,128]{2,1,0:T(8,128)S(1)}) custom-call(s32[1]{0:T(128)} %bitcast.me_ref, f32[10,520,128]{2,1,0:T(8,128)S(1)} %get-tuple-element.23.t_ref, f32[4,256,128]{2,1,0:T(8,128)S(1)} %pad_maximum_fusion.2.c_ref, f32[4,512,128]{2,1,0:T(8,128)S(1)} %shard_map.84.g_ref, f32[2,512,128]{2,1,0:T(8,128)S(1)} %copy-done, ...), custom_call_target="tpu_custom_call" | custom-call | tf_op jit(solution)/shard_map/pallas_call | solution.py:41
  54.8 0.4 collective-permute-start.10
  55.2 3.8 %collective-permute-done.10 = f32[104,128]{1,0:T(8,128)S(1)} collective-permute-done((f32[104,128]{1,0:T(8,128)S(1)}, f32[104,128]{1,0:T(8,128)S(1)}, u32[]{:S(2)}, u32[]{:S(2)}) %collective-permute-start.10) | collective-permute-done | bytes 53280 | tf_op jit(solution)/shard_map/ppermute | solution.py:545
  59.0 1.4 %collective-permute-start.11 = (f32[104,128]{1,0:T(8,128)S(1)}, f32[104,128]{1,0:T(8,128)S(1)}, u32[]{:S(2)}, u32[]{:S(2)}) collective-permute-start(f32[104,128]{1,0:T(8,128)S(1)} %add.34), channel_id=1, source_target_pairs={{0,8},{4,12},{8,16},{12,20},{16,24},{20,28},{24,0},{28,4},{1,9},{5... | collective-permute-start | bytes 159752 | tf_op jit(solution)/shard_map/ppermute | solution.py:545
  60.4 2.0 %collective-permute-start.12 = (f32[104,128]{1,0:T(8,128)S(1)}, f32[104,128]{1,0:T(8,128)S(1)}, u32[]{:S(2)}, u32[]{:S(2)}) collective-permute-start(f32[104,128]{1,0:T(8,128)S(1)} %add.34), channel_id=1, source_target_pairs={{0,16},{4,20},{8,24},{12,28},{16,0},{20,4},{24,8},{28,12},{1,17},{... | collective-permute-start | bytes 159752 | tf_op jit(solution)/shard_map/ppermute | solution.py:545
  62.4 0.5 collective-permute-start.13
  62.9 2.2 %collective-permute-done.11 = f32[104,128]{1,0:T(8,128)S(1)} collective-permute-done((f32[104,128]{1,0:T(8,128)S(1)}, f32[104,128]{1,0:T(8,128)S(1)}, u32[]{:S(2)}, u32[]{:S(2)}) %collective-permute-start.11) | collective-permute-done | bytes 53280 | tf_op jit(solution)/shard_map/ppermute | solution.py:545
  65.1 1.4 %collective-permute-done.12 = f32[104,128]{1,0:T(8,128)S(1)} collective-permute-done((f32[104,128]{1,0:T(8,128)S(1)}, f32[104,128]{1,0:T(8,128)S(1)}, u32[]{:S(2)}, u32[]{:S(2)}) %collective-permute-start.12) | collective-permute-done | bytes 53280 | tf_op jit(solution)/shard_map/ppermute | solution.py:545
  66.6 0.4 collective-permute-done.13
  67.0 0.1 collective-permute-start.14
  67.1 0.7 collective-permute-start.15
  67.8 1.3 %shard_map.87.drive_ref = f32[8,256,128]{2,1,0:T(8,128)S(1)} custom-call(f32[10,520,128]{2,1,0:T(8,128)S(1)} %get-tuple-element.23.t_ref, f32[8,256,128]{2,1,0:T(8,128)S(1)} %get-tuple-element.36.s_ref), custom_call_target="tpu_custom_call" | custom-call | tf_op jit(solution)/shard_map/pallas_call | solution.py:41
  69.1 1.3 %shard_map.89.drive_ref = f32[8,256,128]{2,1,0:T(8,128)S(1)} custom-call(f32[10,520,128]{2,1,0:T(8,128)S(1)} %get-tuple-element.23.t_ref, f32[8,256,128]{2,1,0:T(8,128)S(1)} %get-tuple-element.38.s_ref), custom_call_target="tpu_custom_call" | custom-call | tf_op jit(solution)/shard_map/pallas_call | solution.py:41
  70.4 0.0 collective-permute-done.14
  70.4 0.0 collective-permute-done.15
  70.5 5.1 %shard_map.88 = (f32[8,256,128]{2,1,0:T(8,128)S(1)}, f32[264,128]{1,0:T(8,128)S(1)}, f32[5,8,128]{2,1,0:T(8,128)}, f32[10,8,128]{2,1,0:T(8,128)S(1)}) custom-call(s32[1]{0:T(128)} %bitcast.me_ref, f32[13,3,128]{2,1,0:T(4,128)S(1)} %get-tuple-element.53.before_ref, f32[13,8,128]{2,1,0:T(8,128)S(1)} %add_bitcast_fusion.m_ref, ...), custom_call_target="tpu_custom_call" | custom-call | tf_op jit(solution)/shard_map/pallas_call | solution.py:41
  75.6 1.2 %shard_map.90 = (f32[8,256,128]{2,1,0:T(8,128)S(1)}, f32[256,128]{1,0:T(8,128)S(1)}) custom-call(f32[10,520,128]{2,1,0:T(8,128)S(1)} %get-tuple-element.23.t_ref, f32[10,8,128]{2,1,0:T(8,128)S(1)} %get-tuple-element.37.field_ref, f32[8,256,128]{2,1,0:T(8,128)S(1)} %shard_map.89.drive_ref, f32[8,512,128]{2,1,0:T(8,128)S(1)} %get-tuple-element.27.rden_ref), custom_call_target="tpu_custom_call" | custom-call | tf_op jit(solution)/shard_map/pallas_call | solution.py:41
  76.8 3.4 %collective-permute-start.16 = (f32[1,256,128]{2,1,0:T(8,128)S(1)}, f32[1,256,128]{2,1,0:T(8,128)S(1)}, u32[]{:S(2)}, u32[]{:S(2)}) collective-permute-start(f32[1,256,128]{2,1,0:T(8,128)S(1)} %bitcast.28), channel_id=1, source_target_pairs={{0,2},{1,3},{2,0},{3,1},{4,6},{5,7},{6,4},{7,5},{8,10},{9,11},{10,... | collective-permute-start | bytes 393224 | tf_op jit(solution)/shard_map/ppermute | solution.py:561
  80.3 4.3 %collective-permute-done.16 = f32[1,256,128]{2,1,0:T(8,128)S(1)} collective-permute-done((f32[1,256,128]{2,1,0:T(8,128)S(1)}, f32[1,256,128]{2,1,0:T(8,128)S(1)}, u32[]{:S(2)}, u32[]{:S(2)}) %collective-permute-start.16) | collective-permute-done | bytes 131104 | tf_op jit(solution)/shard_map/ppermute | solution.py:561
  84.6 0.1 collective-permute-start.17
  84.7 0.7 collective-permute-start.18
  85.4 5.3 %collective-permute-done.18 = f32[1,264,128]{2,1,0:T(8,128)S(1)} collective-permute-done((f32[1,264,128]{2,1,0:T(8,128)S(1)}, f32[1,264,128]{2,1,0:T(8,128)S(1)}, u32[]{:S(2)}, u32[]{:S(2)}) %collective-permute-start.18) | collective-permute-done | bytes 135200 | tf_op jit(solution)/shard_map/ppermute | solution.py:561
  90.7 0.1 collective-permute-start.19
  90.8 0.0 collective-permute-done.17
  90.9 1.4 %collective-permute-done.19 = f32[2,264,128]{2,1,0:T(8,128)S(1)} collective-permute-done((f32[2,264,128]{2,1,0:T(8,128)S(1)}, f32[2,264,128]{2,1,0:T(8,128)S(1)}, u32[]{:S(2)}, u32[]{:S(2)}) %collective-permute-start.19) | collective-permute-done | bytes 270368 | tf_op jit(solution)/shard_map/ppermute | solution.py:561
  92.4 1.6 %shard_map.91.refs_0_ = f32[512,8,128]{2,1,0:T(8,128)} custom-call(s32[1]{0:T(128)} %bitcast.me_ref, f32[10,520,128]{2,1,0:T(8,128)S(1)} %get-tuple-element.23.t_ref, f32[4,264,128]{2,1,0:T(8,128)S(1)} %pad_maximum_fusion.1.c_ref, f32[4,512,128]{2,1,0:T(8,128)S(1)} %shard_map.84.g_ref, f32[2,512,128]{2,1,0:T(8,128)S(1)} %copy-done, ...), custom_call_target="tpu_custom_call" | custom-call | tf_op jit(solution)/shard_map/pallas_call | solution.py:653
  94.0 1.6 %shard_map.92 = f32[512,8,128]{2,1,0:T(8,128)} custom-call(s32[1]{0:T(128)} %bitcast.me_ref, f32[10,520,128]{2,1,0:T(8,128)S(1)} %get-tuple-element.23.t_ref, f32[4,256,128]{2,1,0:T(8,128)S(1)} %pad_maximum_fusion.3.c_ref, f32[4,512,128]{2,1,0:T(8,128)S(1)} %shard_map.84.g_ref, f32[2,512,128]{2,1,0:T(8,128)S(1)} %copy-done, ...), custom_call_target="tpu_custom_call", output_to_operand_aliasing={{}: (7, {})} | custom-call | tf_op jit(solution)/shard_map/pallas_call | solution.py:653
  (34 shorter events, 0.5 us)
Async XLA Ops:
  4.9 11.0 %collective-permute-start = (f32[120,128]{1,0:T(8,128)S(1)}, f32[120,128]{1,0:T(8,128)S(1)}, u32[]{:S(2)}, u32[]{:S(2)}) collective-permute-start(f32[120,128]{1,0:T(8,128)S(1)} %get-tuple-element.24), channel_id=1, source_target_pairs={{0,4},{4,0},{8,12},{12,8},{16,20},{20,16},{24,28},{28,24},{1,5},{5... | collective-permute-start | bytes 184328 | tf_op jit(solution)/shard_map/ppermute | solution.py:545
  10.6 1.0 %copy-start.3 = (f32[8,256,128]{2,1,0:T(8,128)}, f32[8,256,128]{2,1,0:T(8,128)S(1)}, u32[]{:S(2)}) copy-start(f32[8,256,128]{2,1,0:T(8,128)S(1)} %shard_map.79.drive_ref) | copy-start | bytes 3145732
  14.1 1.0 %copy-start.1 = (f32[8,256,128]{2,1,0:T(8,128)}, f32[8,256,128]{2,1,0:T(8,128)S(1)}, u32[]{:S(2)}) copy-start(f32[8,256,128]{2,1,0:T(8,128)S(1)} %shard_map.82.drive_ref) | copy-start | bytes 3145732
  15.1 12.5 %copy-start.4 = (f32[8,256,128]{2,1,0:T(8,128)S(1)}, f32[8,256,128]{2,1,0:T(8,128)}, u32[]{:S(2)}) copy-start(f32[8,256,128]{2,1,0:T(8,128)} %copy-done.3) | copy-start | bytes 3145732
  16.0 7.0 %collective-permute-start.1 = (f32[136,128]{1,0:T(8,128)S(1)}, f32[136,128]{1,0:T(8,128)S(1)}, u32[]{:S(2)}, u32[]{:S(2)}) collective-permute-start(f32[136,128]{1,0:T(8,128)S(1)} %pad_maximum_fusion.8), channel_id=1, source_target_pairs={{0,8},{4,12},{8,16},{12,20},{16,24},{20,28},{24,0},{28,4},{1,9},{5... | collective-permute-start | bytes 208904 | tf_op jit(solution)/shard_map/ppermute | solution.py:545
  17.7 7.6 %collective-permute-start.2 = (f32[136,128]{1,0:T(8,128)S(1)}, f32[136,128]{1,0:T(8,128)S(1)}, u32[]{:S(2)}, u32[]{:S(2)}) collective-permute-start(f32[136,128]{1,0:T(8,128)S(1)} %pad_maximum_fusion.8), channel_id=1, source_target_pairs={{0,16},{4,20},{8,24},{12,28},{16,0},{20,4},{24,8},{28,12},{1,17},{... | collective-permute-start | bytes 208904 | tf_op jit(solution)/shard_map/ppermute | solution.py:545
  20.3 5.0 %collective-permute-start.3 = (f32[136,128]{1,0:T(8,128)S(1)}, f32[136,128]{1,0:T(8,128)S(1)}, u32[]{:S(2)}, u32[]{:S(2)}) collective-permute-start(f32[136,128]{1,0:T(8,128)S(1)} %pad_maximum_fusion.8), channel_id=1, source_target_pairs={{0,24},{4,28},{8,0},{12,4},{16,8},{20,12},{24,16},{28,20},{1,25},{... | collective-permute-start | bytes 208904 | tf_op jit(solution)/shard_map/ppermute | solution.py:545
  25.3 2.2 %collective-permute-start.4 = (f32[13,3,128]{2,1,0:T(4,128)S(1)}, f32[13,3,128]{2,1,0:T(4,128)S(1)}, u32[]{:S(2)}, u32[]{:S(2)}) collective-permute-start(f32[13,3,128]{2,1,0:T(4,128)S(1)} %get-tuple-element.59), channel_id=1, source_target_pairs={{0,1},{1,0},{2,3},{3,2},{4,5},{5,4},{6,7},{7,6},{8,9},{9,8},{10,11... | collective-permute-start | bytes 59912 | tf_op jit(solution)/shard_map/ppermute | solution.py:575
  25.4 2.1 %collective-permute-start.5 = (f32[13,3,128]{2,1,0:T(4,128)S(1)}, f32[13,3,128]{2,1,0:T(4,128)S(1)}, u32[]{:S(2)}, u32[]{:S(2)}) collective-permute-start(f32[13,3,128]{2,1,0:T(4,128)S(1)} %get-tuple-element.58), channel_id=1, source_target_pairs={{1,2},{2,1},{5,6},{6,5},{9,10},{10,9},{13,14},{14,13},{17,18},{18,... | collective-permute-start | bytes 59912 | tf_op jit(solution)/shard_map/ppermute | solution.py:574
  27.6 5.1 %copy-start.2 = (f32[8,256,128]{2,1,0:T(8,128)S(1)}, f32[8,256,128]{2,1,0:T(8,128)}, u32[]{:S(2)}) copy-start(f32[8,256,128]{2,1,0:T(8,128)} %copy-done.1) | copy-start | bytes 3145732
  33.9 8.9 %collective-permute-start.6 = (f32[1,256,128]{2,1,0:T(8,128)S(1)}, f32[1,256,128]{2,1,0:T(8,128)S(1)}, u32[]{:S(2)}, u32[]{:S(2)}) collective-permute-start(f32[1,256,128]{2,1,0:T(8,128)S(1)} %bitcast.31), channel_id=1, source_target_pairs={{0,2},{1,3},{2,0},{3,1},{4,6},{5,7},{6,4},{7,5},{8,10},{9,11},{10,... | collective-permute-start | bytes 393224 | tf_op jit(solution)/shard_map/ppermute | solution.py:561
  42.8 6.2 %collective-permute-start.7 = (f32[2,256,128]{2,1,0:T(8,128)S(1)}, f32[2,256,128]{2,1,0:T(8,128)S(1)}, u32[]{:S(2)}, u32[]{:S(2)}) collective-permute-start(f32[2,256,128]{2,1,0:T(8,128)S(1)} %pad_maximum_fusion.6), channel_id=1, source_target_pairs={{0,1},{1,0},{2,3},{3,2},{4,5},{5,4},{6,7},{7,6},{8,9},{9,8},{10,11... | collective-permute-start | bytes 786440 | tf_op jit(solution)/shard_map/ppermute | solution.py:561
  43.0 5.9 %collective-permute-start.8 = (f32[1,264,128]{2,1,0:T(8,128)S(1)}, f32[1,264,128]{2,1,0:T(8,128)S(1)}, u32[]{:S(2)}, u32[]{:S(2)}) collective-permute-start(f32[1,264,128]{2,1,0:T(8,128)S(1)} %bitcast.25), channel_id=1, source_target_pairs={{0,2},{1,3},{2,0},{3,1},{4,6},{5,7},{6,4},{7,5},{8,10},{9,11},{10,... | collective-permute-start | bytes 405512 | tf_op jit(solution)/shard_map/ppermute | solution.py:561
  48.9 1.6 %collective-permute-start.9 = (f32[2,264,128]{2,1,0:T(8,128)S(1)}, f32[2,264,128]{2,1,0:T(8,128)S(1)}, u32[]{:S(2)}, u32[]{:S(2)}) collective-permute-start(f32[2,264,128]{2,1,0:T(8,128)S(1)} %pad_maximum_fusion.4), channel_id=1, source_target_pairs={{0,1},{1,0},{2,3},{3,2},{4,5},{5,4},{6,7},{7,6},{8,9},{9,8},{10,11... | collective-permute-start | bytes 811016 | tf_op jit(solution)/shard_map/ppermute | solution.py:561
  50.5 1.0 %copy-start = (f32[2,512,128]{2,1,0:T(8,128)S(1)}, f32[2,512,128]{2,1,0:T(8,128)}, u32[]{:S(2)}) copy-start(f32[2,512,128]{2,1,0:T(8,128)} %flow_ref.7) | copy-start | bytes 1572868
  54.8 4.2 %collective-permute-start.10 = (f32[104,128]{1,0:T(8,128)S(1)}, f32[104,128]{1,0:T(8,128)S(1)}, u32[]{:S(2)}, u32[]{:S(2)}) collective-permute-start(f32[104,128]{1,0:T(8,128)S(1)} %get-tuple-element.35), channel_id=1, source_target_pairs={{0,4},{4,0},{8,12},{12,8},{16,20},{20,16},{24,28},{28,24},{1,5},{5... | collective-permute-start | bytes 159752 | tf_op jit(solution)/shard_map/ppermute | solution.py:545
  59.0 6.1 %collective-permute-start.11 = (f32[104,128]{1,0:T(8,128)S(1)}, f32[104,128]{1,0:T(8,128)S(1)}, u32[]{:S(2)}, u32[]{:S(2)}) collective-permute-start(f32[104,128]{1,0:T(8,128)S(1)} %add.34), channel_id=1, source_target_pairs={{0,8},{4,12},{8,16},{12,20},{16,24},{20,28},{24,0},{28,4},{1,9},{5... | collective-permute-start | bytes 159752 | tf_op jit(solution)/shard_map/ppermute | solution.py:545
  60.4 6.1 %collective-permute-start.12 = (f32[104,128]{1,0:T(8,128)S(1)}, f32[104,128]{1,0:T(8,128)S(1)}, u32[]{:S(2)}, u32[]{:S(2)}) collective-permute-start(f32[104,128]{1,0:T(8,128)S(1)} %add.34), channel_id=1, source_target_pairs={{0,16},{4,20},{8,24},{12,28},{16,0},{20,4},{24,8},{28,12},{1,17},{... | collective-permute-start | bytes 159752 | tf_op jit(solution)/shard_map/ppermute | solution.py:545
  62.4 4.6 %collective-permute-start.13 = (f32[104,128]{1,0:T(8,128)S(1)}, f32[104,128]{1,0:T(8,128)S(1)}, u32[]{:S(2)}, u32[]{:S(2)}) collective-permute-start(f32[104,128]{1,0:T(8,128)S(1)} %add.34), channel_id=1, source_target_pairs={{0,24},{4,28},{8,0},{12,4},{16,8},{20,12},{24,16},{28,20},{1,25},{... | collective-permute-start | bytes 159752 | tf_op jit(solution)/shard_map/ppermute | solution.py:545
  67.0 3.4 %collective-permute-start.14 = (f32[13,3,128]{2,1,0:T(4,128)S(1)}, f32[13,3,128]{2,1,0:T(4,128)S(1)}, u32[]{:S(2)}, u32[]{:S(2)}) collective-permute-start(f32[13,3,128]{2,1,0:T(4,128)S(1)} %get-tuple-element.55), channel_id=1, source_target_pairs={{0,1},{1,0},{2,3},{3,2},{4,5},{5,4},{6,7},{7,6},{8,9},{9,8},{10,11... | collective-permute-start | bytes 59912 | tf_op jit(solution)/shard_map/ppermute | solution.py:575
  67.1 3.4 %collective-permute-start.15 = (f32[13,3,128]{2,1,0:T(4,128)S(1)}, f32[13,3,128]{2,1,0:T(4,128)S(1)}, u32[]{:S(2)}, u32[]{:S(2)}) collective-permute-start(f32[13,3,128]{2,1,0:T(4,128)S(1)} %get-tuple-element.54), channel_id=1, source_target_pairs={{1,2},{2,1},{5,6},{6,5},{9,10},{10,9},{13,14},{14,13},{17,18},{18,... | collective-permute-start | bytes 59912 | tf_op jit(solution)/shard_map/ppermute | solution.py:574
  76.8 7.7 %collective-permute-start.16 = (f32[1,256,128]{2,1,0:T(8,128)S(1)}, f32[1,256,128]{2,1,0:T(8,128)S(1)}, u32[]{:S(2)}, u32[]{:S(2)}) collective-permute-start(f32[1,256,128]{2,1,0:T(8,128)S(1)} %bitcast.28), channel_id=1, source_target_pairs={{0,2},{1,3},{2,0},{3,1},{4,6},{5,7},{6,4},{7,5},{8,10},{9,11},{10,... | collective-permute-start | bytes 393224 | tf_op jit(solution)/shard_map/ppermute | solution.py:561
  84.6 6.2 %collective-permute-start.17 = (f32[2,256,128]{2,1,0:T(8,128)S(1)}, f32[2,256,128]{2,1,0:T(8,128)S(1)}, u32[]{:S(2)}, u32[]{:S(2)}) collective-permute-start(f32[2,256,128]{2,1,0:T(8,128)S(1)} %pad_maximum_fusion.7), channel_id=1, source_target_pairs={{0,1},{1,0},{2,3},{3,2},{4,5},{5,4},{6,7},{7,6},{8,9},{9,8},{10,11... | collective-permute-start | bytes 786440 | tf_op jit(solution)/shard_map/ppermute | solution.py:561
  84.7 5.9 %collective-permute-start.18 = (f32[1,264,128]{2,1,0:T(8,128)S(1)}, f32[1,264,128]{2,1,0:T(8,128)S(1)}, u32[]{:S(2)}, u32[]{:S(2)}) collective-permute-start(f32[1,264,128]{2,1,0:T(8,128)S(1)} %bitcast.22), channel_id=1, source_target_pairs={{0,2},{1,3},{2,0},{3,1},{4,6},{5,7},{6,4},{7,5},{8,10},{9,11},{10,... | collective-permute-start | bytes 405512 | tf_op jit(solution)/shard_map/ppermute | solution.py:561
  90.7 1.6 %collective-permute-start.19 = (f32[2,264,128]{2,1,0:T(8,128)S(1)}, f32[2,264,128]{2,1,0:T(8,128)S(1)}, u32[]{:S(2)}, u32[]{:S(2)}) collective-permute-start(f32[2,264,128]{2,1,0:T(8,128)S(1)} %pad_maximum_fusion.5), channel_id=1, source_target_pairs={{0,1},{1,0},{2,3},{3,2},{4,5},{5,4},{6,7},{7,6},{8,9},{9,8},{10,11... | collective-permute-start | bytes 811016 | tf_op jit(solution)/shard_map/ppermute | solution.py:561

commit v5 on v4

--- a/solution.py
+++ b/solution.py
@@ -24,9 +24,11 @@
 SUB = 8
 PAIRS = ((0, 0), (0, 1), (1, 0), (0, 2), (2, 0), (1, 1))
 FEATURES = 32
-A, B, E, W, HB, HE, BASE, FA, BA, REST = range(10)
-TABLE = 10
+A, B, E, W, BASE, FA, BA, REST = range(8)
+BASIC = 4
+TABLE = 8
 CHUNKS = 2
+FIRST = 4
 BLOCKS = 4
 PAD = 8
 
@@ -48,6 +50,10 @@
     )(*args)
 
 
+def fit(trips, most):
+    return max(u for u in range(1, most + 1) if trips % u == 0)
+
+
 def f32(*shape):
     return jax.ShapeDtypeStruct(shape, jnp.float32)
 
@@ -76,7 +82,7 @@
             return add_moments(acc, state_at(x, rows), t_ref, table_rows)
 
         acc = tuple(acc_ref[k, x] for k in range(13))
-        acc = lax.fori_loop(0, groups, step, acc, unroll=min(16, groups))
+        acc = lax.fori_loop(0, groups, step, acc, unroll=fit(groups, 16))
         for k, value in enumerate(acc):
             acc_ref[k, x] = value
 
@@ -87,7 +93,7 @@
         m_ref[k * width : (k + 1) * width, :] = jnp.sum(acc_ref[k], axis=1)
 
 
-def first_kernel(extent, *refs):
+def first_kernel(*refs):
     sources, (m_ref, t_ref, rate_ref, wall_ref), rest = refs[:5], refs[5:9], refs[9:]
     v_ref, w_ref, collision_ref, solid_ref, dist_ref, vw_ref, acc_ref, sem = rest
     count, width = dist_ref.shape[0], dist_ref.shape[1]
@@ -126,12 +132,6 @@
     here = slice(0, count)
     a, b, e = wide(0), wide(1), wide(2)
     t_ref[A, here], t_ref[B, here], t_ref[E, here], t_ref[W, here] = a, b, e, wide(3)
-    hb, he = 0.5 * jnp.abs(b), 0.5 * jnp.abs(e)
-    t_ref[HB, here], t_ref[HE, here] = hb, he
-    t_ref[BASE, here] = pseudo_rate + (hb + he) + jnp.abs(a) * extent
-    t_ref[FA, here] = jnp.maximum(a, 0.0) * extent
-    t_ref[BA, here] = jnp.maximum(-a, 0.0) * extent
-    t_ref[REST, here] = (box_volume * (2.0 * math.pi) ** (-1.5)) * jnp.exp(-0.5 * (a * a + b * b + e * e))
     for k, copy in enumerate(large):
         copy.wait()
         moments_loop(
@@ -144,14 +144,19 @@
     write_moments(m_ref, acc_ref)
 
 
-def gains_kernel(t_ref, rate_ref, rden_ref, p_ref):
+def gains_kernel(extent, v_ref, rate_ref, t_ref, rden_ref, p_ref):
     width, count = rden_ref.shape[0], rden_ref.shape[1]
 
     def step(g, carry):
         rows = pl.ds(pl.multiple_of(g * SUB, SUB), SUB)
-        base = t_ref[BASE, rows, :]
-        gain = t_ref[FA, rows, :] + t_ref[BA, rows, :]
-        ahead = t_ref[A, rows, :] >= 0.0
+        a, b, e, w = (v_ref[k, rows, :] for k in (A, B, E, W))
+        base = pseudo_rate + (0.5 * jnp.abs(b) + 0.5 * jnp.abs(e)) + jnp.abs(a) * extent
+        gain = jnp.abs(a) * extent
+        ahead = a >= 0.0
+        rest = (box_volume * (2.0 * math.pi) ** (-1.5)) * jnp.exp(-0.5 * (a * a + b * b + e * e))
+        whole = (a, b, e, w, base, jnp.maximum(a, 0.0) * extent, jnp.maximum(-a, 0.0) * extent, rest)
+        for k, value in enumerate(whole):
+            t_ref[k, rows, :] = value
         steps = []
         for x in range(width):
             rden = 1.0 / (base + rate_ref[x : x + 1, :])
@@ -336,9 +341,10 @@
     def step(g, carry):
         rows = pl.ds(pl.multiple_of(start + g * SUB, SUB), SUB)
         table_rows = pl.ds(pl.multiple_of(first + start + g * SUB, SUB), SUB)
-        hb, he = t_ref[HB, table_rows, :], t_ref[HE, table_rows, :]
-        from_y = jnp.where(t_ref[B, table_rows, :] > 0.0, y_down, y_up)
-        from_z = jnp.where(t_ref[E, table_rows, :] > 0.0, z_down, z_up)
+        b, e = t_ref[B, table_rows, :], t_ref[E, table_rows, :]
+        hb, he = 0.5 * jnp.abs(b), 0.5 * jnp.abs(e)
+        from_y = jnp.where(b > 0.0, y_down, y_up)
+        from_z = jnp.where(e > 0.0, z_down, z_up)
         for x in range(width):
             s = state_at(x, rows)
             sy = jnp.take_along_axis(s, from_y, axis=1, mode="promise_in_bounds")
@@ -346,7 +352,7 @@
             drive_ref[x, rows, :] = pseudo_rate * s + hb * sy + he * sz
         return carry
 
-    lax.fori_loop(0, count // SUB, step, 0, unroll=min(8, count // SUB))
+    lax.fori_loop(0, count // SUB, step, 0, unroll=fit(count // SUB, 8))
 
 
 def kinetic_kernel(
@@ -393,7 +399,7 @@
         weight = jnp.exp2(power)
         return acc + jnp.sum(weight.reshape(LANES // SUB, SUB, width * LANES), axis=0)
 
-    acc = lax.fori_loop(0, f_ref.shape[0] // LANES, mass, jnp.zeros((SUB, width * LANES), jnp.float32), unroll=8)
+    acc = lax.fori_loop(0, f_ref.shape[0] // LANES, mass, jnp.zeros((SUB, width * LANES), jnp.float32), unroll=fit(f_ref.shape[0] // LANES, 32))
     acc = jnp.sum(acc, axis=0, keepdims=True)
     for x in range(width):
         total_ref[x : x + 1, :] = acc[:, x * LANES : (x + 1) * LANES]
@@ -441,7 +447,7 @@
             s_ref[x, rows, :] = value
             return carry
 
-        lax.fori_loop(0, count // SUB, ahead, 0, unroll=min(32, count // SUB))
+        lax.fori_loop(0, count // SUB, ahead, 0, unroll=fit(count // SUB, 32))
 
     def back(g, carry):
         rows, wide = both(g)
@@ -454,7 +460,7 @@
         c_ref[rows, :] = jnp.where(t_ref[A, wide, :] >= 0.0, last, value)
         return carry
 
-    lax.fori_loop(0, count // SUB, back, 0, unroll=4)
+    lax.fori_loop(0, count // SUB, back, 0, unroll=fit(count // SUB, 4))
 
 
 def entering(peers, me, first, rows, t_ref, c_ref, g_ref, flow_ref):
@@ -513,7 +519,7 @@
                 held_ref[rows, x, :] = s_ref[x, rows, :] + p_ref[x, wide, :] * enter
             return carry
 
-        lax.fori_loop(0, block // SUB, step, 0, unroll=4)
+        lax.fori_loop(0, block // SUB, step, 0, unroll=fit(block // SUB, 4))
         copy.start()
     for copy in copies:
         copy.wait()
@@ -576,22 +582,28 @@
     return jnp.where(odd, near, far), jnp.where(odd, far, near)
 
 
-def iteration(repeat, m, states, table, rate, wall, me, inflow, kept):
+def iteration(repeat, m, states, basic, rate, wall, me, inflow, kept):
     width, cells = rate.shape
-    count, peers = table.shape[1] - PAD, lax.axis_size("gx")
-    chunk = count // len(states)
+    count, peers = basic.shape[1] - PAD, lax.axis_size("gx")
+    share = count * FIRST // 8
+    starts, sizes = (0, share), (share, count - share)
     if repeat == 0:
-        kept["gains"] = run(gains_kernel, (f32(width, count, cells),) * 2, (table, rate), scalar=False)
-    rden, prefix = kept["gains"]
+        kept["gains"] = run(
+            functools.partial(gains_kernel, float(width * peers)),
+            (f32(TABLE, count + PAD, cells),) + (f32(width, count, cells),) * 2,
+            (basic, rate),
+            scalar=False,
+        )
+    table, rden, prefix = kept["gains"]
     drives = []
-    for k, state in enumerate(states):
+    for state, start, chunk in zip(states, starts, sizes):
         if repeat:
-            kernel = functools.partial(transport_kernel, k * chunk)
-            drives.append(run(kernel, f32(width, chunk, cells), (table, state), scalar=False))
+            kernel = functools.partial(transport_kernel, start)
+            drives.append(run(kernel, f32(width, chunk, cells), (basic, state), scalar=False))
             continue
         drives.append(
             pl.pallas_call(
-                functools.partial(first_transport_kernel, k * chunk),
+                functools.partial(first_transport_kernel, start),
                 out_shape=f32(width, chunk, cells),
                 in_specs=[VMEM, HBM],
                 out_specs=VMEM,
@@ -600,7 +612,7 @@
                     pltpu.SemaphoreType.DMA((BLOCKS,)),
                 ],
                 compiler_params=PARAMS,
-            )(table, state)
+            )(basic, state)
         )
     m, extra = reduce_over("vel", m, 13 * width)
     m = m.reshape(13, width, cells)
@@ -614,6 +626,7 @@
             scratch=(pltpu.VMEM((total, FEATURES, LANES), jnp.float32),),
             scalar=False,
         )
+    chunk = sizes[0]
     local, carry, macro, fields = run(
         functools.partial(kinetic_kernel, peers),
         (f32(width, chunk, cells), f32(chunk + width, cells), f32(5, width, cells), f32(10, width, cells)),
@@ -626,8 +639,9 @@
     )
     locals_, carries = [local], [gather_over("gx", carry)]
     for k in range(1, len(states)):
+        chunk = sizes[k]
         local, carry = run(
-            functools.partial(sweep_kernel, k * chunk),
+            functools.partial(sweep_kernel, starts[k]),
             (f32(width, chunk, cells), f32(chunk, cells)),
             (table, fields, drives[k], rden),
             scalar=False,
@@ -638,11 +652,11 @@
         kernel = functools.partial(slabs_kernel, peers, width)
         kept["slabs"] = run(kernel, f32(peers, count, cells), (me, table, carries[0]))
     states, m, state = [], None, None
-    for k in range(len(locals_)):
+    for k, chunk in enumerate(sizes):
         args = (me, table, carries[k], kept["slabs"], inflow, locals_[k], prefix)
         if repeat < ITERS - 1:
             m, state = run(
-                functools.partial(next_kernel, peers, k * chunk),
+                functools.partial(next_kernel, peers, starts[k]),
                 (f32(13 * width, cells), f32(width, chunk, cells)),
                 args if m is None else args + (m,),
                 (pltpu.VMEM((chunk, cells), jnp.float32), pltpu.VMEM((13, width, SUB, cells), jnp.float32)),
@@ -651,7 +665,7 @@
         else:
             rest = [] if k == 0 else [states]
             states = pl.pallas_call(
-                functools.partial(last_kernel, peers, k * chunk),
+                functools.partial(last_kernel, peers, starts[k]),
                 out_shape=f32(count, width, cells),
                 in_specs=[SMEM] + [VMEM] * 6 + [HBM] * len(rest),
                 out_specs=HBM,
@@ -667,16 +681,15 @@
 
 def per_device(distribution, velocity, weights, collision, solid, inflow):
     count, width, cells = distribution.shape
-    peers = lax.axis_size("gx")
     me = lax.axis_index("gx").astype(jnp.int32).reshape(1)
     lines = 4 * count // LANES
     far = functools.partial(pltpu.with_memory_space_constraint, memory_space=pltpu.HBM)
     given = tuple(far(x) for x in (velocity, weights.reshape(1, count), collision, solid, distribution))
     m, table, rate, wall = pl.pallas_call(
-        functools.partial(first_kernel, float(width * peers)),
+        first_kernel,
         out_shape=(
             f32(13 * width + lines, cells),
-            f32(TABLE, count + PAD, cells),
+            f32(BASIC, count + PAD, cells),
             f32(width, cells),
             f32(width, cells),
         ),

time: 96 us -> 93.2 us (0.971)
  local copies, waits for them, and re-layouts: 2.22 us -> 0.29 us
    unnamed x14 -> x6, local copies, waits for them, and re-layouts: 2.12 us -> 0.2 us
  transfers between devices with their start and end apart: 20 -> 20, of which waited for: 12 -> 12; matrix products, arithmetic and copies ran while one was open for 0% -> 0% of each run, Pallas kernels for 10% -> 11%
where the time goes in v5:
time: 93.2 us; the launch traced here: 92.9 us
  Pallas kernels  33.2 us (36%)
  waiting for transfers between devices  33.2 us (36%)
  starting transfers between devices  24.7 us (27%)
  between operations  1.21 us (1%)
    ppermute x8, waiting for transfers between devices, gather_over(): got = lax.ppermute(blocks, axis, [(i, i ^ bit) for i in range(size)])  21.6 us
    pallas_call x11, Pallas kernels, run(): pl.pallas_call(kernel, out_shape=out_shape, in_specs=([SMEM] if scalar el...  20.6 us
    ppermute x8, starting transfers between devices, reduce_over(): got.append(lax.ppermute(sent, axis, pairs))  12.9 us
    ppermute x8, waiting for transfers between devices, reduce_over(): got.append(lax.ppermute(sent, axis, pairs))  11.6 us
    ppermute x8, starting transfers between devices, gather_over(): got = lax.ppermute(blocks, axis, [(i, i ^ bit) for i in range(size)])  9.95 us
    pallas_call x2, Pallas kernels, iteration(): pl.pallas_call(functools.partial(first_transport_kernel, start), out_shap...  5.18 us
    pallas_call x1, Pallas kernels, per_device(): pl.pallas_call(first_kernel, out_shape=(f32(13 * width + lines, cells), f...  4.28 us
    pallas_call x2, Pallas kernels, iteration(): pl.pallas_call(functools.partial(last_kernel, peers, starts[k]), out_shap...  3.18 us
  transfers between devices with their start and end apart: 20, of which 12 were waited for; matrix products, arithmetic and copies ran while one was open for 0% of the time, Pallas kernels for 11%

profile of v5, /device:TPU:0, one launch (start us, length us, event | category | flops | bytes accessed | tf_op | source)
XLA Modules:
  0.0 92.9 jit_solution(4136324747855597008)
XLA Ops:
  0.6 4.3 %shard_map.77 = (f32[120,128]{1,0:T(8,128)S(1)}, f32[4,520,128]{2,1,0:T(8,128)S(1)}, f32[8,128]{1,0:T(8,128)S(1)}, f32[8,128]{1,0:T(8,128)S(1)}) custom-call(f32[3,512]{1,0:T(4,128)} %refs_0_.1, f32[1,512]{1,0:T(1,128)} %bitcast.38, f32[8,128]{1,0:T(8,128)} %refs_2_.1, s32[8,128]{1,0:T(8,128)} %refs_3_.1, f32[512,8,128]{2,1,0:T(8,128)} %dist_ref.3), custom_call_target="tpu_custom_call" | custom-call | tf_op jit(solution)/shard_map/pallas_call | solution.py:688
  4.9 3.1 %collective-permute-start = (f32[120,128]{1,0:T(8,128)S(1)}, f32[120,128]{1,0:T(8,128)S(1)}, u32[]{:S(2)}, u32[]{:S(2)}) collective-permute-start(f32[120,128]{1,0:T(8,128)S(1)} %get-tuple-element.27), channel_id=1, source_target_pairs={{0,4},{4,0},{8,12},{12,8},{16,20},{20,16},{24,28},{28,24},{1,5},{5... | collective-permute-start | bytes 184328 | tf_op jit(solution)/shard_map/ppermute | solution.py:551
  8.0 2.6 %shard_map.80.drive_ref = f32[8,256,128]{2,1,0:T(8,128)S(1)} custom-call(f32[4,520,128]{2,1,0:T(8,128)S(1)} %get-tuple-element.24.v_ref.t_ref, f32[512,8,128]{2,1,0:T(8,128)} %dist_ref.3), custom_call_target="tpu_custom_call" | custom-call | tf_op jit(solution)/shard_map/pallas_call | solution.py:605
  10.6 2.6 %shard_map.82.drive_ref = f32[8,256,128]{2,1,0:T(8,128)S(1)} custom-call(f32[4,520,128]{2,1,0:T(8,128)S(1)} %get-tuple-element.24.v_ref.t_ref, f32[512,8,128]{2,1,0:T(8,128)} %dist_ref.3), custom_call_target="tpu_custom_call" | custom-call | tf_op jit(solution)/shard_map/pallas_call | solution.py:605
  13.2 1.0 %shard_map.78 = (f32[8,520,128]{2,1,0:T(8,128)S(1)}, f32[8,512,128]{2,1,0:T(8,128)S(1)}, f32[8,512,128]{2,1,0:T(8,128)S(1)}) custom-call(f32[4,520,128]{2,1,0:T(8,128)S(1)} %get-tuple-element.24.v_ref.t_ref, f32[8,128]{1,0:T(8,128)S(1)} %get-tuple-element.25.rate_ref), custom_call_target="tpu_custom_call" | custom-call | tf_op jit(solution)/shard_map/pallas_call | solution.py:43
  14.2 0.0 collective-permute-done
  14.3 1.6 %collective-permute-start.1 = (f32[136,128]{1,0:T(8,128)S(1)}, f32[136,128]{1,0:T(8,128)S(1)}, u32[]{:S(2)}, u32[]{:S(2)}) collective-permute-start(f32[136,128]{1,0:T(8,128)S(1)} %pad_maximum_fusion.8), channel_id=1, source_target_pairs={{0,8},{4,12},{8,16},{12,20},{16,24},{20,28},{24,0},{28,4},{1,9},{5... | collective-permute-start | bytes 208904 | tf_op jit(solution)/shard_map/ppermute | solution.py:551
  15.9 2.6 %collective-permute-start.2 = (f32[136,128]{1,0:T(8,128)S(1)}, f32[136,128]{1,0:T(8,128)S(1)}, u32[]{:S(2)}, u32[]{:S(2)}) collective-permute-start(f32[136,128]{1,0:T(8,128)S(1)} %pad_maximum_fusion.8), channel_id=1, source_target_pairs={{0,16},{4,20},{8,24},{12,28},{16,0},{20,4},{24,8},{28,12},{1,17},{... | collective-permute-start | bytes 208904 | tf_op jit(solution)/shard_map/ppermute | solution.py:551
  18.5 1.3 %collective-permute-start.3 = (f32[136,128]{1,0:T(8,128)S(1)}, f32[136,128]{1,0:T(8,128)S(1)}, u32[]{:S(2)}, u32[]{:S(2)}) collective-permute-start(f32[136,128]{1,0:T(8,128)S(1)} %pad_maximum_fusion.8), channel_id=1, source_target_pairs={{0,24},{4,28},{8,0},{12,4},{16,8},{20,12},{24,16},{28,20},{1,25},{... | collective-permute-start | bytes 208904 | tf_op jit(solution)/shard_map/ppermute | solution.py:551
  19.9 1.4 %collective-permute-done.1 = f32[136,128]{1,0:T(8,128)S(1)} collective-permute-done((f32[136,128]{1,0:T(8,128)S(1)}, f32[136,128]{1,0:T(8,128)S(1)}, u32[]{:S(2)}, u32[]{:S(2)}) %collective-permute-start.1) | collective-permute-done | bytes 69664 | tf_op jit(solution)/shard_map/ppermute | solution.py:551
  21.3 2.2 %collective-permute-done.2 = f32[136,128]{1,0:T(8,128)S(1)} collective-permute-done((f32[136,128]{1,0:T(8,128)S(1)}, f32[136,128]{1,0:T(8,128)S(1)}, u32[]{:S(2)}, u32[]{:S(2)}) %collective-permute-start.2) | collective-permute-done | bytes 69664 | tf_op jit(solution)/shard_map/ppermute | solution.py:551
  23.5 0.0 collective-permute-done.3
  23.6 0.1 collective-permute-start.4
  23.7 0.8 collective-permute-start.5
  24.6 1.2 %shard_map.79.f_ref = bf16[4096,32]{1,0:T(8,128)(2,1)S(1)} custom-call(f32[8,16,128]{2,1,0:T(8,128)S(1)} %constant_dynamic-update-slice_fusion.v_ref), custom_call_target="tpu_custom_call" | custom-call | tf_op jit(solution)/shard_map/pallas_call | solution.py:43
  25.8 0.0 collective-permute-done.4
  25.8 0.0 collective-permute-done.5
  25.8 4.6 %shard_map.81 = (f32[8,256,128]{2,1,0:T(8,128)S(1)}, f32[264,128]{1,0:T(8,128)S(1)}, f32[5,8,128]{2,1,0:T(8,128)}, f32[10,8,128]{2,1,0:T(8,128)S(1)}) custom-call(s32[1]{0:T(128)} %bitcast.me_ref, f32[13,3,128]{2,1,0:T(4,128)S(1)} %get-tuple-element.59.before_ref, f32[13,8,128]{2,1,0:T(8,128)S(1)} %fusion.m_ref, ...), custom_call_target="tpu_custom_call" | custom-call | tf_op jit(solution)/shard_map/pallas_call | solution.py:43
  30.4 1.3 %shard_map.83 = (f32[8,256,128]{2,1,0:T(8,128)S(1)}, f32[256,128]{1,0:T(8,128)S(1)}) custom-call(f32[8,520,128]{2,1,0:T(8,128)S(1)} %get-tuple-element.26.t_ref, f32[10,8,128]{2,1,0:T(8,128)S(1)} %get-tuple-element.30.field_ref, f32[8,256,128]{2,1,0:T(8,128)S(1)} %shard_map.82.drive_ref, f32[8,512,128]{2,1,0:T(8,128)S(1)} %get-tuple-element.29.rden_ref), custom_call_target="tpu_custom_call" | custom-call | tf_op jit(solution)/shard_map/pallas_call | solution.py:43
  31.7 4.6 %collective-permute-start.6 = (f32[1,256,128]{2,1,0:T(8,128)S(1)}, f32[1,256,128]{2,1,0:T(8,128)S(1)}, u32[]{:S(2)}, u32[]{:S(2)}) collective-permute-start(f32[1,256,128]{2,1,0:T(8,128)S(1)} %bitcast.31), channel_id=1, source_target_pairs={{0,2},{1,3},{2,0},{3,1},{4,6},{5,7},{6,4},{7,5},{8,10},{9,11},{10,... | collective-permute-start | bytes 393224 | tf_op jit(solution)/shard_map/ppermute | solution.py:567
  36.2 4.3 %collective-permute-done.6 = f32[1,256,128]{2,1,0:T(8,128)S(1)} collective-permute-done((f32[1,256,128]{2,1,0:T(8,128)S(1)}, f32[1,256,128]{2,1,0:T(8,128)S(1)}, u32[]{:S(2)}, u32[]{:S(2)}) %collective-permute-start.6) | collective-permute-done | bytes 131104 | tf_op jit(solution)/shard_map/ppermute | solution.py:567
  40.6 0.2 collective-permute-start.7
  40.7 0.6 collective-permute-start.8
  41.4 5.3 %collective-permute-done.8 = f32[1,264,128]{2,1,0:T(8,128)S(1)} collective-permute-done((f32[1,264,128]{2,1,0:T(8,128)S(1)}, f32[1,264,128]{2,1,0:T(8,128)S(1)}, u32[]{:S(2)}, u32[]{:S(2)}) %collective-permute-start.8) | collective-permute-done | bytes 135200 | tf_op jit(solution)/shard_map/ppermute | solution.py:567
  46.7 0.1 collective-permute-start.9
  46.7 0.0 collective-permute-done.7
  46.8 1.5 %collective-permute-done.9 = f32[2,264,128]{2,1,0:T(8,128)S(1)} collective-permute-done((f32[2,264,128]{2,1,0:T(8,128)S(1)}, f32[2,264,128]{2,1,0:T(8,128)S(1)}, u32[]{:S(2)}, u32[]{:S(2)}) %collective-permute-start.9) | collective-permute-done | bytes 270368 | tf_op jit(solution)/shard_map/ppermute | solution.py:567
  48.3 0.1 pad_maximum_fusion.c_ref
  48.4 0.0 copy-start
  48.4 0.8 shard_map.84.g_ref
  49.2 0.2 copy-done
  49.4 1.6 %shard_map.85 = (f32[104,128]{1,0:T(8,128)S(1)}, f32[8,256,128]{2,1,0:T(8,128)S(1)}) custom-call(s32[1]{0:T(128)} %bitcast.me_ref, f32[8,520,128]{2,1,0:T(8,128)S(1)} %get-tuple-element.26.t_ref, f32[4,264,128]{2,1,0:T(8,128)S(1)} %pad_maximum_fusion.c_ref, f32[4,512,128]{2,1,0:T(8,128)S(1)} %shard_map.84.g_ref, f32[2,512,128]{2,1,0:T(8,128)S(1)} %copy-done, ...), custom_call_target="tpu_custom_call" | custom-call | tf_op jit(solution)/shard_map/pallas_call | solution.py:43
  51.0 1.6 %shard_map.86 = (f32[104,128]{1,0:T(8,128)S(1)}, f32[8,256,128]{2,1,0:T(8,128)S(1)}) custom-call(s32[1]{0:T(128)} %bitcast.me_ref, f32[8,520,128]{2,1,0:T(8,128)S(1)} %get-tuple-element.26.t_ref, f32[4,256,128]{2,1,0:T(8,128)S(1)} %pad_maximum_fusion.2.c_ref, f32[4,512,128]{2,1,0:T(8,128)S(1)} %shard_map.84.g_ref, f32[2,512,128]{2,1,0:T(8,128)S(1)} %copy-done, ...), custom_call_target="tpu_custom_call" | custom-call | tf_op jit(solution)/shard_map/pallas_call | solution.py:43
  52.6 0.3 collective-permute-start.10
  53.0 3.9 %collective-permute-done.10 = f32[104,128]{1,0:T(8,128)S(1)} collective-permute-done((f32[104,128]{1,0:T(8,128)S(1)}, f32[104,128]{1,0:T(8,128)S(1)}, u32[]{:S(2)}, u32[]{:S(2)}) %collective-permute-start.10) | collective-permute-done | bytes 53280 | tf_op jit(solution)/shard_map/ppermute | solution.py:551
  56.8 1.4 %collective-permute-start.11 = (f32[104,128]{1,0:T(8,128)S(1)}, f32[104,128]{1,0:T(8,128)S(1)}, u32[]{:S(2)}, u32[]{:S(2)}) collective-permute-start(f32[104,128]{1,0:T(8,128)S(1)} %add.34), channel_id=1, source_target_pairs={{0,8},{4,12},{8,16},{12,20},{16,24},{20,28},{24,0},{28,4},{1,9},{5... | collective-permute-start | bytes 159752 | tf_op jit(solution)/shard_map/ppermute | solution.py:551
  58.2 2.0 %collective-permute-start.12 = (f32[104,128]{1,0:T(8,128)S(1)}, f32[104,128]{1,0:T(8,128)S(1)}, u32[]{:S(2)}, u32[]{:S(2)}) collective-permute-start(f32[104,128]{1,0:T(8,128)S(1)} %add.34), channel_id=1, source_target_pairs={{0,16},{4,20},{8,24},{12,28},{16,0},{20,4},{24,8},{28,12},{1,17},{... | collective-permute-start | bytes 159752 | tf_op jit(solution)/shard_map/ppermute | solution.py:551
  60.2 0.5 collective-permute-start.13
  60.7 2.2 %collective-permute-done.11 = f32[104,128]{1,0:T(8,128)S(1)} collective-permute-done((f32[104,128]{1,0:T(8,128)S(1)}, f32[104,128]{1,0:T(8,128)S(1)}, u32[]{:S(2)}, u32[]{:S(2)}) %collective-permute-start.11) | collective-permute-done | bytes 53280 | tf_op jit(solution)/shard_map/ppermute | solution.py:551
  62.9 1.4 %collective-permute-done.12 = f32[104,128]{1,0:T(8,128)S(1)} collective-permute-done((f32[104,128]{1,0:T(8,128)S(1)}, f32[104,128]{1,0:T(8,128)S(1)}, u32[]{:S(2)}, u32[]{:S(2)}) %collective-permute-start.12) | collective-permute-done | bytes 53280 | tf_op jit(solution)/shard_map/ppermute | solution.py:551
  64.4 0.4 collective-permute-done.13
  64.8 0.1 collective-permute-start.14
  64.9 0.9 collective-permute-start.15
  65.8 1.3 %shard_map.87.drive_ref = f32[8,256,128]{2,1,0:T(8,128)S(1)} custom-call(f32[4,520,128]{2,1,0:T(8,128)S(1)} %get-tuple-element.24.v_ref.t_ref, f32[8,256,128]{2,1,0:T(8,128)S(1)} %get-tuple-element.38.s_ref), custom_call_target="tpu_custom_call" | custom-call | tf_op jit(solution)/shard_map/pallas_call | solution.py:43
  67.1 1.3 %shard_map.89.drive_ref = f32[8,256,128]{2,1,0:T(8,128)S(1)} custom-call(f32[4,520,128]{2,1,0:T(8,128)S(1)} %get-tuple-element.24.v_ref.t_ref, f32[8,256,128]{2,1,0:T(8,128)S(1)} %get-tuple-element.40.s_ref), custom_call_target="tpu_custom_call" | custom-call | tf_op jit(solution)/shard_map/pallas_call | solution.py:43
  68.5 0.0 collective-permute-done.14
  68.5 0.0 collective-permute-done.15
  68.5 4.5 %shard_map.88 = (f32[8,256,128]{2,1,0:T(8,128)S(1)}, f32[264,128]{1,0:T(8,128)S(1)}, f32[5,8,128]{2,1,0:T(8,128)}, f32[10,8,128]{2,1,0:T(8,128)S(1)}) custom-call(s32[1]{0:T(128)} %bitcast.me_ref, f32[13,3,128]{2,1,0:T(4,128)S(1)} %get-tuple-element.55.before_ref, f32[13,8,128]{2,1,0:T(8,128)S(1)} %add_bitcast_fusion.m_ref, ...), custom_call_target="tpu_custom_call" | custom-call | tf_op jit(solution)/shard_map/pallas_call | solution.py:43
  73.0 1.3 %shard_map.90 = (f32[8,256,128]{2,1,0:T(8,128)S(1)}, f32[256,128]{1,0:T(8,128)S(1)}) custom-call(f32[8,520,128]{2,1,0:T(8,128)S(1)} %get-tuple-element.26.t_ref, f32[10,8,128]{2,1,0:T(8,128)S(1)} %get-tuple-element.39.field_ref, f32[8,256,128]{2,1,0:T(8,128)S(1)} %shard_map.89.drive_ref, f32[8,512,128]{2,1,0:T(8,128)S(1)} %get-tuple-element.29.rden_ref), custom_call_target="tpu_custom_call" | custom-call | tf_op jit(solution)/shard_map/pallas_call | solution.py:43
  74.3 3.4 %collective-permute-start.16 = (f32[1,256,128]{2,1,0:T(8,128)S(1)}, f32[1,256,128]{2,1,0:T(8,128)S(1)}, u32[]{:S(2)}, u32[]{:S(2)}) collective-permute-start(f32[1,256,128]{2,1,0:T(8,128)S(1)} %bitcast.28), channel_id=1, source_target_pairs={{0,2},{1,3},{2,0},{3,1},{4,6},{5,7},{6,4},{7,5},{8,10},{9,11},{10,... | collective-permute-start | bytes 393224 | tf_op jit(solution)/shard_map/ppermute | solution.py:567
  77.7 4.1 %collective-permute-done.16 = f32[1,256,128]{2,1,0:T(8,128)S(1)} collective-permute-done((f32[1,256,128]{2,1,0:T(8,128)S(1)}, f32[1,256,128]{2,1,0:T(8,128)S(1)}, u32[]{:S(2)}, u32[]{:S(2)}) %collective-permute-start.16) | collective-permute-done | bytes 131104 | tf_op jit(solution)/shard_map/ppermute | solution.py:567
  81.8 0.1 collective-permute-start.17
  81.9 1.0 %collective-permute-start.18 = (f32[1,264,128]{2,1,0:T(8,128)S(1)}, f32[1,264,128]{2,1,0:T(8,128)S(1)}, u32[]{:S(2)}, u32[]{:S(2)}) collective-permute-start(f32[1,264,128]{2,1,0:T(8,128)S(1)} %bitcast.22), channel_id=1, source_target_pairs={{0,2},{1,3},{2,0},{3,1},{4,6},{5,7},{6,4},{7,5},{8,10},{9,11},{10,... | collective-permute-start | bytes 405512 | tf_op jit(solution)/shard_map/ppermute | solution.py:567
  82.8 5.0 %collective-permute-done.18 = f32[1,264,128]{2,1,0:T(8,128)S(1)} collective-permute-done((f32[1,264,128]{2,1,0:T(8,128)S(1)}, f32[1,264,128]{2,1,0:T(8,128)S(1)}, u32[]{:S(2)}, u32[]{:S(2)}) %collective-permute-start.18) | collective-permute-done | bytes 135200 | tf_op jit(solution)/shard_map/ppermute | solution.py:567
  87.9 0.1 collective-permute-start.19
  88.0 0.0 collective-permute-done.17
  88.0 0.1 pad_maximum_fusion.3.c_ref
  88.1 1.4 %collective-permute-done.19 = f32[2,264,128]{2,1,0:T(8,128)S(1)} collective-permute-done((f32[2,264,128]{2,1,0:T(8,128)S(1)}, f32[2,264,128]{2,1,0:T(8,128)S(1)}, u32[]{:S(2)}, u32[]{:S(2)}) %collective-permute-start.19) | collective-permute-done | bytes 270368 | tf_op jit(solution)/shard_map/ppermute | solution.py:567
  89.6 1.6 %shard_map.91.refs_0_ = f32[512,8,128]{2,1,0:T(8,128)} custom-call(s32[1]{0:T(128)} %bitcast.me_ref, f32[8,520,128]{2,1,0:T(8,128)S(1)} %get-tuple-element.26.t_ref, f32[4,264,128]{2,1,0:T(8,128)S(1)} %pad_maximum_fusion.1.c_ref, f32[4,512,128]{2,1,0:T(8,128)S(1)} %shard_map.84.g_ref, f32[2,512,128]{2,1,0:T(8,128)S(1)} %copy-done, ...), custom_call_target="tpu_custom_call" | custom-call | tf_op jit(solution)/shard_map/pallas_call | solution.py:667
  91.2 1.6 %shard_map.92 = f32[512,8,128]{2,1,0:T(8,128)} custom-call(s32[1]{0:T(128)} %bitcast.me_ref, f32[8,520,128]{2,1,0:T(8,128)S(1)} %get-tuple-element.26.t_ref, f32[4,256,128]{2,1,0:T(8,128)S(1)} %pad_maximum_fusion.3.c_ref, f32[4,512,128]{2,1,0:T(8,128)S(1)} %shard_map.84.g_ref, f32[2,512,128]{2,1,0:T(8,128)S(1)} %copy-done, ...), custom_call_target="tpu_custom_call", output_to_operand_aliasing={{}: (7, {})} | custom-call | tf_op jit(solution)/shard_map/pallas_call | solution.py:667
  (30 shorter events, 0.4 us)
Async XLA Ops:
  4.9 9.3 %collective-permute-start = (f32[120,128]{1,0:T(8,128)S(1)}, f32[120,128]{1,0:T(8,128)S(1)}, u32[]{:S(2)}, u32[]{:S(2)}) collective-permute-start(f32[120,128]{1,0:T(8,128)S(1)} %get-tuple-element.27), channel_id=1, source_target_pairs={{0,4},{4,0},{8,12},{12,8},{16,20},{20,16},{24,28},{28,24},{1,5},{5... | collective-permute-start | bytes 184328 | tf_op jit(solution)/shard_map/ppermute | solution.py:551
  14.3 7.0 %collective-permute-start.1 = (f32[136,128]{1,0:T(8,128)S(1)}, f32[136,128]{1,0:T(8,128)S(1)}, u32[]{:S(2)}, u32[]{:S(2)}) collective-permute-start(f32[136,128]{1,0:T(8,128)S(1)} %pad_maximum_fusion.8), channel_id=1, source_target_pairs={{0,8},{4,12},{8,16},{12,20},{16,24},{20,28},{24,0},{28,4},{1,9},{5... | collective-permute-start | bytes 208904 | tf_op jit(solution)/shard_map/ppermute | solution.py:551
  15.9 7.6 %collective-permute-start.2 = (f32[136,128]{1,0:T(8,128)S(1)}, f32[136,128]{1,0:T(8,128)S(1)}, u32[]{:S(2)}, u32[]{:S(2)}) collective-permute-start(f32[136,128]{1,0:T(8,128)S(1)} %pad_maximum_fusion.8), channel_id=1, source_target_pairs={{0,16},{4,20},{8,24},{12,28},{16,0},{20,4},{24,8},{28,12},{1,17},{... | collective-permute-start | bytes 208904 | tf_op jit(solution)/shard_map/ppermute | solution.py:551
  18.5 5.0 %collective-permute-start.3 = (f32[136,128]{1,0:T(8,128)S(1)}, f32[136,128]{1,0:T(8,128)S(1)}, u32[]{:S(2)}, u32[]{:S(2)}) collective-permute-start(f32[136,128]{1,0:T(8,128)S(1)} %pad_maximum_fusion.8), channel_id=1, source_target_pairs={{0,24},{4,28},{8,0},{12,4},{16,8},{20,12},{24,16},{28,20},{1,25},{... | collective-permute-start | bytes 208904 | tf_op jit(solution)/shard_map/ppermute | solution.py:551
  23.6 2.2 %collective-permute-start.4 = (f32[13,3,128]{2,1,0:T(4,128)S(1)}, f32[13,3,128]{2,1,0:T(4,128)S(1)}, u32[]{:S(2)}, u32[]{:S(2)}) collective-permute-start(f32[13,3,128]{2,1,0:T(4,128)S(1)} %get-tuple-element.61), channel_id=1, source_target_pairs={{0,1},{1,0},{2,3},{3,2},{4,5},{5,4},{6,7},{7,6},{8,9},{9,8},{10,11... | collective-permute-start | bytes 59912 | tf_op jit(solution)/shard_map/ppermute | solution.py:581
  23.7 2.1 %collective-permute-start.5 = (f32[13,3,128]{2,1,0:T(4,128)S(1)}, f32[13,3,128]{2,1,0:T(4,128)S(1)}, u32[]{:S(2)}, u32[]{:S(2)}) collective-permute-start(f32[13,3,128]{2,1,0:T(4,128)S(1)} %get-tuple-element.60), channel_id=1, source_target_pairs={{1,2},{2,1},{5,6},{6,5},{9,10},{10,9},{13,14},{14,13},{17,18},{18,... | collective-permute-start | bytes 59912 | tf_op jit(solution)/shard_map/ppermute | solution.py:580
  31.7 8.9 %collective-permute-start.6 = (f32[1,256,128]{2,1,0:T(8,128)S(1)}, f32[1,256,128]{2,1,0:T(8,128)S(1)}, u32[]{:S(2)}, u32[]{:S(2)}) collective-permute-start(f32[1,256,128]{2,1,0:T(8,128)S(1)} %bitcast.31), channel_id=1, source_target_pairs={{0,2},{1,3},{2,0},{3,1},{4,6},{5,7},{6,4},{7,5},{8,10},{9,11},{10,... | collective-permute-start | bytes 393224 | tf_op jit(solution)/shard_map/ppermute | solution.py:567
  40.6 6.2 %collective-permute-start.7 = (f32[2,256,128]{2,1,0:T(8,128)S(1)}, f32[2,256,128]{2,1,0:T(8,128)S(1)}, u32[]{:S(2)}, u32[]{:S(2)}) collective-permute-start(f32[2,256,128]{2,1,0:T(8,128)S(1)} %pad_maximum_fusion.6), channel_id=1, source_target_pairs={{0,1},{1,0},{2,3},{3,2},{4,5},{5,4},{6,7},{7,6},{8,9},{9,8},{10,11... | collective-permute-start | bytes 786440 | tf_op jit(solution)/shard_map/ppermute | solution.py:567
  40.7 5.9 %collective-permute-start.8 = (f32[1,264,128]{2,1,0:T(8,128)S(1)}, f32[1,264,128]{2,1,0:T(8,128)S(1)}, u32[]{:S(2)}, u32[]{:S(2)}) collective-permute-start(f32[1,264,128]{2,1,0:T(8,128)S(1)} %bitcast.25), channel_id=1, source_target_pairs={{0,2},{1,3},{2,0},{3,1},{4,6},{5,7},{6,4},{7,5},{8,10},{9,11},{10,... | collective-permute-start | bytes 405512 | tf_op jit(solution)/shard_map/ppermute | solution.py:567
  46.7 1.6 %collective-permute-start.9 = (f32[2,264,128]{2,1,0:T(8,128)S(1)}, f32[2,264,128]{2,1,0:T(8,128)S(1)}, u32[]{:S(2)}, u32[]{:S(2)}) collective-permute-start(f32[2,264,128]{2,1,0:T(8,128)S(1)} %pad_maximum_fusion.4), channel_id=1, source_target_pairs={{0,1},{1,0},{2,3},{3,2},{4,5},{5,4},{6,7},{7,6},{8,9},{9,8},{10,11... | collective-permute-start | bytes 811016 | tf_op jit(solution)/shard_map/ppermute | solution.py:567
  48.4 1.0 %copy-start = (f32[2,512,128]{2,1,0:T(8,128)S(1)}, f32[2,512,128]{2,1,0:T(8,128)}, u32[]{:S(2)}) copy-start(f32[2,512,128]{2,1,0:T(8,128)} %flow_ref.7) | copy-start | bytes 1572868
  52.6 4.2 %collective-permute-start.10 = (f32[104,128]{1,0:T(8,128)S(1)}, f32[104,128]{1,0:T(8,128)S(1)}, u32[]{:S(2)}, u32[]{:S(2)}) collective-permute-start(f32[104,128]{1,0:T(8,128)S(1)} %get-tuple-element.37), channel_id=1, source_target_pairs={{0,4},{4,0},{8,12},{12,8},{16,20},{20,16},{24,28},{28,24},{1,5},{5... | collective-permute-start | bytes 159752 | tf_op jit(solution)/shard_map/ppermute | solution.py:551
  56.8 6.1 %collective-permute-start.11 = (f32[104,128]{1,0:T(8,128)S(1)}, f32[104,128]{1,0:T(8,128)S(1)}, u32[]{:S(2)}, u32[]{:S(2)}) collective-permute-start(f32[104,128]{1,0:T(8,128)S(1)} %add.34), channel_id=1, source_target_pairs={{0,8},{4,12},{8,16},{12,20},{16,24},{20,28},{24,0},{28,4},{1,9},{5... | collective-permute-start | bytes 159752 | tf_op jit(solution)/shard_map/ppermute | solution.py:551
  58.2 6.1 %collective-permute-start.12 = (f32[104,128]{1,0:T(8,128)S(1)}, f32[104,128]{1,0:T(8,128)S(1)}, u32[]{:S(2)}, u32[]{:S(2)}) collective-permute-start(f32[104,128]{1,0:T(8,128)S(1)} %add.34), channel_id=1, source_target_pairs={{0,16},{4,20},{8,24},{12,28},{16,0},{20,4},{24,8},{28,12},{1,17},{... | collective-permute-start | bytes 159752 | tf_op jit(solution)/shard_map/ppermute | solution.py:551
  60.2 4.6 %collective-permute-start.13 = (f32[104,128]{1,0:T(8,128)S(1)}, f32[104,128]{1,0:T(8,128)S(1)}, u32[]{:S(2)}, u32[]{:S(2)}) collective-permute-start(f32[104,128]{1,0:T(8,128)S(1)} %add.34), channel_id=1, source_target_pairs={{0,24},{4,28},{8,0},{12,4},{16,8},{20,12},{24,16},{28,20},{1,25},{... | collective-permute-start | bytes 159752 | tf_op jit(solution)/shard_map/ppermute | solution.py:551
  64.8 3.7 %collective-permute-start.14 = (f32[13,3,128]{2,1,0:T(4,128)S(1)}, f32[13,3,128]{2,1,0:T(4,128)S(1)}, u32[]{:S(2)}, u32[]{:S(2)}) collective-permute-start(f32[13,3,128]{2,1,0:T(4,128)S(1)} %get-tuple-element.57), channel_id=1, source_target_pairs={{0,1},{1,0},{2,3},{3,2},{4,5},{5,4},{6,7},{7,6},{8,9},{9,8},{10,11... | collective-permute-start | bytes 59912 | tf_op jit(solution)/shard_map/ppermute | solution.py:581
  64.9 3.6 %collective-permute-start.15 = (f32[13,3,128]{2,1,0:T(4,128)S(1)}, f32[13,3,128]{2,1,0:T(4,128)S(1)}, u32[]{:S(2)}, u32[]{:S(2)}) collective-permute-start(f32[13,3,128]{2,1,0:T(4,128)S(1)} %get-tuple-element.56), channel_id=1, source_target_pairs={{1,2},{2,1},{5,6},{6,5},{9,10},{10,9},{13,14},{14,13},{17,18},{18,... | collective-permute-start | bytes 59912 | tf_op jit(solution)/shard_map/ppermute | solution.py:580
  74.3 7.5 %collective-permute-start.16 = (f32[1,256,128]{2,1,0:T(8,128)S(1)}, f32[1,256,128]{2,1,0:T(8,128)S(1)}, u32[]{:S(2)}, u32[]{:S(2)}) collective-permute-start(f32[1,256,128]{2,1,0:T(8,128)S(1)} %bitcast.28), channel_id=1, source_target_pairs={{0,2},{1,3},{2,0},{3,1},{4,6},{5,7},{6,4},{7,5},{8,10},{9,11},{10,... | collective-permute-start | bytes 393224 | tf_op jit(solution)/shard_map/ppermute | solution.py:567
  81.8 6.2 %collective-permute-start.17 = (f32[2,256,128]{2,1,0:T(8,128)S(1)}, f32[2,256,128]{2,1,0:T(8,128)S(1)}, u32[]{:S(2)}, u32[]{:S(2)}) collective-permute-start(f32[2,256,128]{2,1,0:T(8,128)S(1)} %pad_maximum_fusion.7), channel_id=1, source_target_pairs={{0,1},{1,0},{2,3},{3,2},{4,5},{5,4},{6,7},{7,6},{8,9},{9,8},{10,11... | collective-permute-start | bytes 786440 | tf_op jit(solution)/shard_map/ppermute | solution.py:567
  81.9 6.0 %collective-permute-start.18 = (f32[1,264,128]{2,1,0:T(8,128)S(1)}, f32[1,264,128]{2,1,0:T(8,128)S(1)}, u32[]{:S(2)}, u32[]{:S(2)}) collective-permute-start(f32[1,264,128]{2,1,0:T(8,128)S(1)} %bitcast.22), channel_id=1, source_target_pairs={{0,2},{1,3},{2,0},{3,1},{4,6},{5,7},{6,4},{7,5},{8,10},{9,11},{10,... | collective-permute-start | bytes 405512 | tf_op jit(solution)/shard_map/ppermute | solution.py:567
  87.9 1.6 %collective-permute-start.19 = (f32[2,264,128]{2,1,0:T(8,128)S(1)}, f32[2,264,128]{2,1,0:T(8,128)S(1)}, u32[]{:S(2)}, u32[]{:S(2)}) collective-permute-start(f32[2,264,128]{2,1,0:T(8,128)S(1)} %pad_maximum_fusion.5), channel_id=1, source_target_pairs={{0,1},{1,0},{2,3},{3,2},{4,5},{5,4},{6,7},{7,6},{8,9},{9,8},{10,11... | collective-permute-start | bytes 811016 | tf_op jit(solution)/shard_map/ppermute | solution.py:567

commit v6 on v5

--- a/solution.py
+++ b/solution.py
@@ -199,11 +199,17 @@
     return values[0]
 
 
-def features_kernel(v_ref, f_ref, row_ref):
+def features_kernel(v_ref, f_ref, center_ref, row_ref):
     blocks = v_ref.shape[0]
     part = v_ref.shape[1] // 4
+    centers = []
+    for i in range(3):
+        total = sum(v_ref[k, i * part : (i + 1) * part, :] for k in range(blocks))
+        centers.append(jnp.sum(total, keepdims=True) * (1.0 / (blocks * part * LANES)))
+        center_ref[i : i + 1, :] = jnp.broadcast_to(centers[i], (1, LANES))
     for k in range(blocks):
         a, b, e, w = (v_ref[k, i * part : (i + 1) * part, :] for i in range(4))
+        a, b, e = (value - center for value, center in zip((a, b, e), centers))
         sides = [split(value) for value in (a, b, e, a * a + b * b + e * e)]
         one, zero = jnp.ones_like(a), jnp.zeros_like(a)
         rows = [side[i] for side in sides for i, _ in PAIRS] + [one] * 3 + split(jnp.log2(w))
@@ -356,7 +362,7 @@
 
 
 def kinetic_kernel(
-    peers, me_ref, before_ref, m_ref, after_ref, f_ref, t_ref, rate_ref, wall_ref, drive_ref, rden_ref,
+    peers, me_ref, before_ref, m_ref, after_ref, f_ref, center_ref, t_ref, rate_ref, wall_ref, drive_ref, rden_ref,
     s_ref, c_ref, macro_ref, field_ref, pad_ref, cell_ref, total_ref,
 ):
     width, count = s_ref.shape[0], s_ref.shape[1]
@@ -383,8 +389,9 @@
     q = [pad_ref[5 + k, own, :] for k in range(3)]
     cold = 1.0 / T
     beta = (-0.5 * LOG2E) * cold
-    alpha = [(LOG2E * cold) * U[k] for k in range(3)]
-    gamma = beta * (U[0] * U[0] + U[1] * U[1] + U[2] * U[2])
+    V = [U[k] - center_ref[k : k + 1, :] for k in range(3)]
+    alpha = [(LOG2E * cold) * V[k] for k in range(3)]
+    gamma = beta * (V[0] * V[0] + V[1] * V[1] + V[2] * V[2])
     rows = [side[j] for side in (split(v) for v in (*alpha, beta)) for _, j in PAIRS]
     rows = rows + split(gamma) + [jnp.ones_like(T)] * 3
     rows = rows + [jnp.zeros_like(T)] * (FEATURES - len(rows))
@@ -621,7 +628,7 @@
         total = extra.shape[0] * extra.shape[1] // 4
         kept["features"] = run(
             features_kernel,
-            jax.ShapeDtypeStruct((total * LANES, FEATURES), jnp.bfloat16),
+            (jax.ShapeDtypeStruct((total * LANES, FEATURES), jnp.bfloat16), f32(3, cells)),
             (extra,),
             scratch=(pltpu.VMEM((total, FEATURES, LANES), jnp.float32),),
             scalar=False,
@@ -630,7 +637,7 @@
     local, carry, macro, fields = run(
         functools.partial(kinetic_kernel, peers),
         (f32(width, chunk, cells), f32(chunk + width, cells), f32(5, width, cells), f32(10, width, cells)),
-        (me, before, m, after, kept["features"], table, rate, wall, drives[0], rden),
+        (me, before, m, after, *kept["features"], table, rate, wall, drives[0], rden),
         scratch=(
             pltpu.VMEM((13, width + 2 * SUB, cells), jnp.float32),
             pltpu.VMEM((FEATURES, width * cells), jnp.float32),

time: 93.2 us -> 93.1 us (level)
  no operation moved by 1% of the time
where the time goes in v6:
time: 93.1 us; the launch traced here: 92.9 us
  Pallas kernels  33.2 us (36%)
  waiting for transfers between devices  33.1 us (36%)
  starting transfers between devices  24.6 us (26%)
  between operations  1.21 us (1%)
    ppermute x8, waiting for transfers between devices, gather_over(): got = lax.ppermute(blocks, axis, [(i, i ^ bit) for i in range(size)])  21.6 us
    pallas_call x11, Pallas kernels, run(): pl.pallas_call(kernel, out_shape=out_shape, in_specs=([SMEM] if scalar el...  20.6 us
    ppermute x8, starting transfers between devices, reduce_over(): got.append(lax.ppermute(sent, axis, pairs))  12.9 us
    ppermute x8, waiting for transfers between devices, reduce_over(): got.append(lax.ppermute(sent, axis, pairs))  11.6 us
    ppermute x8, starting transfers between devices, gather_over(): got = lax.ppermute(blocks, axis, [(i, i ^ bit) for i in range(size)])  9.9 us
    pallas_call x2, Pallas kernels, iteration(): pl.pallas_call(functools.partial(first_transport_kernel, start), out_shap...  5.18 us
    pallas_call x1, Pallas kernels, per_device(): pl.pallas_call(first_kernel, out_shape=(f32(13 * width + lines, cells), f...  4.28 us
    pallas_call x2, Pallas kernels, iteration(): pl.pallas_call(functools.partial(last_kernel, peers, starts[k]), out_shap...  3.18 us
  transfers between devices with their start and end apart: 20, of which 12 were waited for; matrix products, arithmetic and copies ran while one was open for 0% of the time, Pallas kernels for 11%

profile of v6, /device:TPU:0, one launch (start us, length us, event | category | flops | bytes accessed | tf_op | source)
XLA Modules:
  0.0 92.9 jit_solution(9503691507030664021)
XLA Ops:
  0.6 4.3 %shard_map.77 = (f32[120,128]{1,0:T(8,128)S(1)}, f32[4,520,128]{2,1,0:T(8,128)S(1)}, f32[8,128]{1,0:T(8,128)S(1)}, f32[8,128]{1,0:T(8,128)S(1)}) custom-call(f32[3,512]{1,0:T(4,128)} %refs_0_.1, f32[1,512]{1,0:T(1,128)} %bitcast.38, f32[8,128]{1,0:T(8,128)} %refs_2_.1, s32[8,128]{1,0:T(8,128)} %refs_3_.1, f32[512,8,128]{2,1,0:T(8,128)} %dist_ref.3), custom_call_target="tpu_custom_call" | custom-call | tf_op jit(solution)/shard_map/pallas_call | solution.py:695
  4.9 3.1 %collective-permute-start = (f32[120,128]{1,0:T(8,128)S(1)}, f32[120,128]{1,0:T(8,128)S(1)}, u32[]{:S(2)}, u32[]{:S(2)}) collective-permute-start(f32[120,128]{1,0:T(8,128)S(1)} %get-tuple-element.29), channel_id=1, source_target_pairs={{0,4},{4,0},{8,12},{12,8},{16,20},{20,16},{24,28},{28,24},{1,5},{5... | collective-permute-start | bytes 184328 | tf_op jit(solution)/shard_map/ppermute | solution.py:558
  8.0 2.6 %shard_map.80.drive_ref = f32[8,256,128]{2,1,0:T(8,128)S(1)} custom-call(f32[4,520,128]{2,1,0:T(8,128)S(1)} %get-tuple-element.26.v_ref.t_ref, f32[512,8,128]{2,1,0:T(8,128)} %dist_ref.3), custom_call_target="tpu_custom_call" | custom-call | tf_op jit(solution)/shard_map/pallas_call | solution.py:612
  10.6 2.6 %shard_map.82.drive_ref = f32[8,256,128]{2,1,0:T(8,128)S(1)} custom-call(f32[4,520,128]{2,1,0:T(8,128)S(1)} %get-tuple-element.26.v_ref.t_ref, f32[512,8,128]{2,1,0:T(8,128)} %dist_ref.3), custom_call_target="tpu_custom_call" | custom-call | tf_op jit(solution)/shard_map/pallas_call | solution.py:612
  13.2 1.0 %shard_map.78 = (f32[8,520,128]{2,1,0:T(8,128)S(1)}, f32[8,512,128]{2,1,0:T(8,128)S(1)}, f32[8,512,128]{2,1,0:T(8,128)S(1)}) custom-call(f32[4,520,128]{2,1,0:T(8,128)S(1)} %get-tuple-element.26.v_ref.t_ref, f32[8,128]{1,0:T(8,128)S(1)} %get-tuple-element.27.rate_ref), custom_call_target="tpu_custom_call" | custom-call | tf_op jit(solution)/shard_map/pallas_call | solution.py:43
  14.2 0.0 collective-permute-done
  14.3 1.6 %collective-permute-start.1 = (f32[136,128]{1,0:T(8,128)S(1)}, f32[136,128]{1,0:T(8,128)S(1)}, u32[]{:S(2)}, u32[]{:S(2)}) collective-permute-start(f32[136,128]{1,0:T(8,128)S(1)} %pad_maximum_fusion.8), channel_id=1, source_target_pairs={{0,8},{4,12},{8,16},{12,20},{16,24},{20,28},{24,0},{28,4},{1,9},{5... | collective-permute-start | bytes 208904 | tf_op jit(solution)/shard_map/ppermute | solution.py:558
  15.9 2.6 %collective-permute-start.2 = (f32[136,128]{1,0:T(8,128)S(1)}, f32[136,128]{1,0:T(8,128)S(1)}, u32[]{:S(2)}, u32[]{:S(2)}) collective-permute-start(f32[136,128]{1,0:T(8,128)S(1)} %pad_maximum_fusion.8), channel_id=1, source_target_pairs={{0,16},{4,20},{8,24},{12,28},{16,0},{20,4},{24,8},{28,12},{1,17},{... | collective-permute-start | bytes 208904 | tf_op jit(solution)/shard_map/ppermute | solution.py:558
  18.5 1.3 %collective-permute-start.3 = (f32[136,128]{1,0:T(8,128)S(1)}, f32[136,128]{1,0:T(8,128)S(1)}, u32[]{:S(2)}, u32[]{:S(2)}) collective-permute-start(f32[136,128]{1,0:T(8,128)S(1)} %pad_maximum_fusion.8), channel_id=1, source_target_pairs={{0,24},{4,28},{8,0},{12,4},{16,8},{20,12},{24,16},{28,20},{1,25},{... | collective-permute-start | bytes 208904 | tf_op jit(solution)/shard_map/ppermute | solution.py:558
  19.9 1.4 %collective-permute-done.1 = f32[136,128]{1,0:T(8,128)S(1)} collective-permute-done((f32[136,128]{1,0:T(8,128)S(1)}, f32[136,128]{1,0:T(8,128)S(1)}, u32[]{:S(2)}, u32[]{:S(2)}) %collective-permute-start.1) | collective-permute-done | bytes 69664 | tf_op jit(solution)/shard_map/ppermute | solution.py:558
  21.3 2.2 %collective-permute-done.2 = f32[136,128]{1,0:T(8,128)S(1)} collective-permute-done((f32[136,128]{1,0:T(8,128)S(1)}, f32[136,128]{1,0:T(8,128)S(1)}, u32[]{:S(2)}, u32[]{:S(2)}) %collective-permute-start.2) | collective-permute-done | bytes 69664 | tf_op jit(solution)/shard_map/ppermute | solution.py:558
  23.5 0.0 collective-permute-done.3
  23.6 0.1 collective-permute-start.4
  23.7 0.8 collective-permute-start.5
  24.6 1.3 %shard_map.79 = (bf16[4096,32]{1,0:T(8,128)(2,1)S(1)}, f32[3,128]{1,0:T(4,128)S(1)}) custom-call(f32[8,16,128]{2,1,0:T(8,128)S(1)} %constant_dynamic-update-slice_fusion.v_ref), custom_call_target="tpu_custom_call" | custom-call | tf_op jit(solution)/shard_map/pallas_call | solution.py:43
  25.8 0.0 collective-permute-done.4
  25.9 0.0 collective-permute-done.5
  25.9 4.5 %shard_map.81 = (f32[8,256,128]{2,1,0:T(8,128)S(1)}, f32[264,128]{1,0:T(8,128)S(1)}, f32[5,8,128]{2,1,0:T(8,128)}, f32[10,8,128]{2,1,0:T(8,128)S(1)}) custom-call(s32[1]{0:T(128)} %bitcast.me_ref, f32[13,3,128]{2,1,0:T(4,128)S(1)} %get-tuple-element.63.before_ref, f32[13,8,128]{2,1,0:T(8,128)S(1)} %fusion.m_ref, ...), custom_call_target="tpu_custom_call" | custom-call | tf_op jit(solution)/shard_map/pallas_call | solution.py:43
  30.4 1.3 %shard_map.83 = (f32[8,256,128]{2,1,0:T(8,128)S(1)}, f32[256,128]{1,0:T(8,128)S(1)}) custom-call(f32[8,520,128]{2,1,0:T(8,128)S(1)} %get-tuple-element.28.t_ref, f32[10,8,128]{2,1,0:T(8,128)S(1)} %get-tuple-element.34.field_ref, f32[8,256,128]{2,1,0:T(8,128)S(1)} %shard_map.82.drive_ref, f32[8,512,128]{2,1,0:T(8,128)S(1)} %get-tuple-element.33.rden_ref), custom_call_target="tpu_custom_call" | custom-call | tf_op jit(solution)/shard_map/pallas_call | solution.py:43
  31.6 4.5 %collective-permute-start.6 = (f32[1,256,128]{2,1,0:T(8,128)S(1)}, f32[1,256,128]{2,1,0:T(8,128)S(1)}, u32[]{:S(2)}, u32[]{:S(2)}) collective-permute-start(f32[1,256,128]{2,1,0:T(8,128)S(1)} %bitcast.31), channel_id=1, source_target_pairs={{0,2},{1,3},{2,0},{3,1},{4,6},{5,7},{6,4},{7,5},{8,10},{9,11},{10,... | collective-permute-start | bytes 393224 | tf_op jit(solution)/shard_map/ppermute | solution.py:574
  36.1 4.3 %collective-permute-done.6 = f32[1,256,128]{2,1,0:T(8,128)S(1)} collective-permute-done((f32[1,256,128]{2,1,0:T(8,128)S(1)}, f32[1,256,128]{2,1,0:T(8,128)S(1)}, u32[]{:S(2)}, u32[]{:S(2)}) %collective-permute-start.6) | collective-permute-done | bytes 131104 | tf_op jit(solution)/shard_map/ppermute | solution.py:574
  40.5 0.2 collective-permute-start.7
  40.7 0.6 collective-permute-start.8
  41.3 5.3 %collective-permute-done.8 = f32[1,264,128]{2,1,0:T(8,128)S(1)} collective-permute-done((f32[1,264,128]{2,1,0:T(8,128)S(1)}, f32[1,264,128]{2,1,0:T(8,128)S(1)}, u32[]{:S(2)}, u32[]{:S(2)}) %collective-permute-start.8) | collective-permute-done | bytes 135200 | tf_op jit(solution)/shard_map/ppermute | solution.py:574
  46.6 0.1 collective-permute-start.9
  46.7 0.0 collective-permute-done.7
  46.7 0.1 pad_maximum_fusion.2.c_ref
  46.7 1.4 %collective-permute-done.9 = f32[2,264,128]{2,1,0:T(8,128)S(1)} collective-permute-done((f32[2,264,128]{2,1,0:T(8,128)S(1)}, f32[2,264,128]{2,1,0:T(8,128)S(1)}, u32[]{:S(2)}, u32[]{:S(2)}) %collective-permute-start.9) | collective-permute-done | bytes 270368 | tf_op jit(solution)/shard_map/ppermute | solution.py:574
  48.3 0.0 copy-start
  48.3 0.9 shard_map.84.g_ref
  49.1 0.2 copy-done
  49.3 1.6 %shard_map.85 = (f32[104,128]{1,0:T(8,128)S(1)}, f32[8,256,128]{2,1,0:T(8,128)S(1)}) custom-call(s32[1]{0:T(128)} %bitcast.me_ref, f32[8,520,128]{2,1,0:T(8,128)S(1)} %get-tuple-element.28.t_ref, f32[4,264,128]{2,1,0:T(8,128)S(1)} %pad_maximum_fusion.c_ref, f32[4,512,128]{2,1,0:T(8,128)S(1)} %shard_map.84.g_ref, f32[2,512,128]{2,1,0:T(8,128)S(1)} %copy-done, ...), custom_call_target="tpu_custom_call" | custom-call | tf_op jit(solution)/shard_map/pallas_call | solution.py:43
  50.9 1.6 %shard_map.86 = (f32[104,128]{1,0:T(8,128)S(1)}, f32[8,256,128]{2,1,0:T(8,128)S(1)}) custom-call(s32[1]{0:T(128)} %bitcast.me_ref, f32[8,520,128]{2,1,0:T(8,128)S(1)} %get-tuple-element.28.t_ref, f32[4,256,128]{2,1,0:T(8,128)S(1)} %pad_maximum_fusion.2.c_ref, f32[4,512,128]{2,1,0:T(8,128)S(1)} %shard_map.84.g_ref, f32[2,512,128]{2,1,0:T(8,128)S(1)} %copy-done, ...), custom_call_target="tpu_custom_call" | custom-call | tf_op jit(solution)/shard_map/pallas_call | solution.py:43
  52.5 0.4 collective-permute-start.10
  52.9 3.8 %collective-permute-done.10 = f32[104,128]{1,0:T(8,128)S(1)} collective-permute-done((f32[104,128]{1,0:T(8,128)S(1)}, f32[104,128]{1,0:T(8,128)S(1)}, u32[]{:S(2)}, u32[]{:S(2)}) %collective-permute-start.10) | collective-permute-done | bytes 53280 | tf_op jit(solution)/shard_map/ppermute | solution.py:558
  56.7 1.4 %collective-permute-start.11 = (f32[104,128]{1,0:T(8,128)S(1)}, f32[104,128]{1,0:T(8,128)S(1)}, u32[]{:S(2)}, u32[]{:S(2)}) collective-permute-start(f32[104,128]{1,0:T(8,128)S(1)} %add.34), channel_id=1, source_target_pairs={{0,8},{4,12},{8,16},{12,20},{16,24},{20,28},{24,0},{28,4},{1,9},{5... | collective-permute-start | bytes 159752 | tf_op jit(solution)/shard_map/ppermute | solution.py:558
  58.1 2.0 %collective-permute-start.12 = (f32[104,128]{1,0:T(8,128)S(1)}, f32[104,128]{1,0:T(8,128)S(1)}, u32[]{:S(2)}, u32[]{:S(2)}) collective-permute-start(f32[104,128]{1,0:T(8,128)S(1)} %add.34), channel_id=1, source_target_pairs={{0,16},{4,20},{8,24},{12,28},{16,0},{20,4},{24,8},{28,12},{1,17},{... | collective-permute-start | bytes 159752 | tf_op jit(solution)/shard_map/ppermute | solution.py:558
  60.1 0.5 collective-permute-start.13
  60.6 2.2 %collective-permute-done.11 = f32[104,128]{1,0:T(8,128)S(1)} collective-permute-done((f32[104,128]{1,0:T(8,128)S(1)}, f32[104,128]{1,0:T(8,128)S(1)}, u32[]{:S(2)}, u32[]{:S(2)}) %collective-permute-start.11) | collective-permute-done | bytes 53280 | tf_op jit(solution)/shard_map/ppermute | solution.py:558
  62.8 1.4 %collective-permute-done.12 = f32[104,128]{1,0:T(8,128)S(1)} collective-permute-done((f32[104,128]{1,0:T(8,128)S(1)}, f32[104,128]{1,0:T(8,128)S(1)}, u32[]{:S(2)}, u32[]{:S(2)}) %collective-permute-start.12) | collective-permute-done | bytes 53280 | tf_op jit(solution)/shard_map/ppermute | solution.py:558
  64.2 0.4 collective-permute-done.13
  64.7 0.1 collective-permute-start.14
  64.8 0.9 collective-permute-start.15
  65.7 1.3 %shard_map.87.drive_ref = f32[8,256,128]{2,1,0:T(8,128)S(1)} custom-call(f32[4,520,128]{2,1,0:T(8,128)S(1)} %get-tuple-element.26.v_ref.t_ref, f32[8,256,128]{2,1,0:T(8,128)S(1)} %get-tuple-element.42.s_ref), custom_call_target="tpu_custom_call" | custom-call | tf_op jit(solution)/shard_map/pallas_call | solution.py:43
  67.0 1.3 %shard_map.89.drive_ref = f32[8,256,128]{2,1,0:T(8,128)S(1)} custom-call(f32[4,520,128]{2,1,0:T(8,128)S(1)} %get-tuple-element.26.v_ref.t_ref, f32[8,256,128]{2,1,0:T(8,128)S(1)} %get-tuple-element.44.s_ref), custom_call_target="tpu_custom_call" | custom-call | tf_op jit(solution)/shard_map/pallas_call | solution.py:43
  68.4 0.0 collective-permute-done.14
  68.4 0.0 collective-permute-done.15
  68.4 4.5 %shard_map.88 = (f32[8,256,128]{2,1,0:T(8,128)S(1)}, f32[264,128]{1,0:T(8,128)S(1)}, f32[5,8,128]{2,1,0:T(8,128)}, f32[10,8,128]{2,1,0:T(8,128)S(1)}) custom-call(s32[1]{0:T(128)} %bitcast.me_ref, f32[13,3,128]{2,1,0:T(4,128)S(1)} %get-tuple-element.59.before_ref, f32[13,8,128]{2,1,0:T(8,128)S(1)} %add_bitcast_fusion.m_ref, ...), custom_call_target="tpu_custom_call" | custom-call | tf_op jit(solution)/shard_map/pallas_call | solution.py:43
  72.9 1.3 %shard_map.90 = (f32[8,256,128]{2,1,0:T(8,128)S(1)}, f32[256,128]{1,0:T(8,128)S(1)}) custom-call(f32[8,520,128]{2,1,0:T(8,128)S(1)} %get-tuple-element.28.t_ref, f32[10,8,128]{2,1,0:T(8,128)S(1)} %get-tuple-element.43.field_ref, f32[8,256,128]{2,1,0:T(8,128)S(1)} %shard_map.89.drive_ref, f32[8,512,128]{2,1,0:T(8,128)S(1)} %get-tuple-element.33.rden_ref), custom_call_target="tpu_custom_call" | custom-call | tf_op jit(solution)/shard_map/pallas_call | solution.py:43
  74.2 3.4 %collective-permute-start.16 = (f32[1,256,128]{2,1,0:T(8,128)S(1)}, f32[1,256,128]{2,1,0:T(8,128)S(1)}, u32[]{:S(2)}, u32[]{:S(2)}) collective-permute-start(f32[1,256,128]{2,1,0:T(8,128)S(1)} %bitcast.28), channel_id=1, source_target_pairs={{0,2},{1,3},{2,0},{3,1},{4,6},{5,7},{6,4},{7,5},{8,10},{9,11},{10,... | collective-permute-start | bytes 393224 | tf_op jit(solution)/shard_map/ppermute | solution.py:574
  77.6 4.1 %collective-permute-done.16 = f32[1,256,128]{2,1,0:T(8,128)S(1)} collective-permute-done((f32[1,256,128]{2,1,0:T(8,128)S(1)}, f32[1,256,128]{2,1,0:T(8,128)S(1)}, u32[]{:S(2)}, u32[]{:S(2)}) %collective-permute-start.16) | collective-permute-done | bytes 131104 | tf_op jit(solution)/shard_map/ppermute | solution.py:574
  81.7 0.1 collective-permute-start.17
  81.8 1.0 %collective-permute-start.18 = (f32[1,264,128]{2,1,0:T(8,128)S(1)}, f32[1,264,128]{2,1,0:T(8,128)S(1)}, u32[]{:S(2)}, u32[]{:S(2)}) collective-permute-start(f32[1,264,128]{2,1,0:T(8,128)S(1)} %bitcast.22), channel_id=1, source_target_pairs={{0,2},{1,3},{2,0},{3,1},{4,6},{5,7},{6,4},{7,5},{8,10},{9,11},{10,... | collective-permute-start | bytes 405512 | tf_op jit(solution)/shard_map/ppermute | solution.py:574
  82.7 5.0 %collective-permute-done.18 = f32[1,264,128]{2,1,0:T(8,128)S(1)} collective-permute-done((f32[1,264,128]{2,1,0:T(8,128)S(1)}, f32[1,264,128]{2,1,0:T(8,128)S(1)}, u32[]{:S(2)}, u32[]{:S(2)}) %collective-permute-start.18) | collective-permute-done | bytes 135200 | tf_op jit(solution)/shard_map/ppermute | solution.py:574
  87.8 0.1 collective-permute-start.19
  87.9 0.0 collective-permute-done.17
  88.0 1.5 %collective-permute-done.19 = f32[2,264,128]{2,1,0:T(8,128)S(1)} collective-permute-done((f32[2,264,128]{2,1,0:T(8,128)S(1)}, f32[2,264,128]{2,1,0:T(8,128)S(1)}, u32[]{:S(2)}, u32[]{:S(2)}) %collective-permute-start.19) | collective-permute-done | bytes 270368 | tf_op jit(solution)/shard_map/ppermute | solution.py:574
  89.5 1.6 %shard_map.91.refs_0_ = f32[512,8,128]{2,1,0:T(8,128)} custom-call(s32[1]{0:T(128)} %bitcast.me_ref, f32[8,520,128]{2,1,0:T(8,128)S(1)} %get-tuple-element.28.t_ref, f32[4,264,128]{2,1,0:T(8,128)S(1)} %pad_maximum_fusion.1.c_ref, f32[4,512,128]{2,1,0:T(8,128)S(1)} %shard_map.84.g_ref, f32[2,512,128]{2,1,0:T(8,128)S(1)} %copy-done, ...), custom_call_target="tpu_custom_call" | custom-call | tf_op jit(solution)/shard_map/pallas_call | solution.py:674
  91.1 1.6 %shard_map.92 = f32[512,8,128]{2,1,0:T(8,128)} custom-call(s32[1]{0:T(128)} %bitcast.me_ref, f32[8,520,128]{2,1,0:T(8,128)S(1)} %get-tuple-element.28.t_ref, f32[4,256,128]{2,1,0:T(8,128)S(1)} %pad_maximum_fusion.3.c_ref, f32[4,512,128]{2,1,0:T(8,128)S(1)} %shard_map.84.g_ref, f32[2,512,128]{2,1,0:T(8,128)S(1)} %copy-done, ...), custom_call_target="tpu_custom_call", output_to_operand_aliasing={{}: (7, {})} | custom-call | tf_op jit(solution)/shard_map/pallas_call | solution.py:674
  (31 shorter events, 0.5 us)
Async XLA Ops:
  4.9 9.3 %collective-permute-start = (f32[120,128]{1,0:T(8,128)S(1)}, f32[120,128]{1,0:T(8,128)S(1)}, u32[]{:S(2)}, u32[]{:S(2)}) collective-permute-start(f32[120,128]{1,0:T(8,128)S(1)} %get-tuple-element.29), channel_id=1, source_target_pairs={{0,4},{4,0},{8,12},{12,8},{16,20},{20,16},{24,28},{28,24},{1,5},{5... | collective-permute-start | bytes 184328 | tf_op jit(solution)/shard_map/ppermute | solution.py:558
  14.3 7.0 %collective-permute-start.1 = (f32[136,128]{1,0:T(8,128)S(1)}, f32[136,128]{1,0:T(8,128)S(1)}, u32[]{:S(2)}, u32[]{:S(2)}) collective-permute-start(f32[136,128]{1,0:T(8,128)S(1)} %pad_maximum_fusion.8), channel_id=1, source_target_pairs={{0,8},{4,12},{8,16},{12,20},{16,24},{20,28},{24,0},{28,4},{1,9},{5... | collective-permute-start | bytes 208904 | tf_op jit(solution)/shard_map/ppermute | solution.py:558
  15.9 7.6 %collective-permute-start.2 = (f32[136,128]{1,0:T(8,128)S(1)}, f32[136,128]{1,0:T(8,128)S(1)}, u32[]{:S(2)}, u32[]{:S(2)}) collective-permute-start(f32[136,128]{1,0:T(8,128)S(1)} %pad_maximum_fusion.8), channel_id=1, source_target_pairs={{0,16},{4,20},{8,24},{12,28},{16,0},{20,4},{24,8},{28,12},{1,17},{... | collective-permute-start | bytes 208904 | tf_op jit(solution)/shard_map/ppermute | solution.py:558
  18.5 5.0 %collective-permute-start.3 = (f32[136,128]{1,0:T(8,128)S(1)}, f32[136,128]{1,0:T(8,128)S(1)}, u32[]{:S(2)}, u32[]{:S(2)}) collective-permute-start(f32[136,128]{1,0:T(8,128)S(1)} %pad_maximum_fusion.8), channel_id=1, source_target_pairs={{0,24},{4,28},{8,0},{12,4},{16,8},{20,12},{24,16},{28,20},{1,25},{... | collective-permute-start | bytes 208904 | tf_op jit(solution)/shard_map/ppermute | solution.py:558
  23.6 2.3 %collective-permute-start.4 = (f32[13,3,128]{2,1,0:T(4,128)S(1)}, f32[13,3,128]{2,1,0:T(4,128)S(1)}, u32[]{:S(2)}, u32[]{:S(2)}) collective-permute-start(f32[13,3,128]{2,1,0:T(4,128)S(1)} %get-tuple-element.65), channel_id=1, source_target_pairs={{0,1},{1,0},{2,3},{3,2},{4,5},{5,4},{6,7},{7,6},{8,9},{9,8},{10,11... | collective-permute-start | bytes 59912 | tf_op jit(solution)/shard_map/ppermute | solution.py:588
  23.7 2.2 %collective-permute-start.5 = (f32[13,3,128]{2,1,0:T(4,128)S(1)}, f32[13,3,128]{2,1,0:T(4,128)S(1)}, u32[]{:S(2)}, u32[]{:S(2)}) collective-permute-start(f32[13,3,128]{2,1,0:T(4,128)S(1)} %get-tuple-element.64), channel_id=1, source_target_pairs={{1,2},{2,1},{5,6},{6,5},{9,10},{10,9},{13,14},{14,13},{17,18},{18,... | collective-permute-start | bytes 59912 | tf_op jit(solution)/shard_map/ppermute | solution.py:587
  31.6 8.8 %collective-permute-start.6 = (f32[1,256,128]{2,1,0:T(8,128)S(1)}, f32[1,256,128]{2,1,0:T(8,128)S(1)}, u32[]{:S(2)}, u32[]{:S(2)}) collective-permute-start(f32[1,256,128]{2,1,0:T(8,128)S(1)} %bitcast.31), channel_id=1, source_target_pairs={{0,2},{1,3},{2,0},{3,1},{4,6},{5,7},{6,4},{7,5},{8,10},{9,11},{10,... | collective-permute-start | bytes 393224 | tf_op jit(solution)/shard_map/ppermute | solution.py:574
  40.5 6.2 %collective-permute-start.7 = (f32[2,256,128]{2,1,0:T(8,128)S(1)}, f32[2,256,128]{2,1,0:T(8,128)S(1)}, u32[]{:S(2)}, u32[]{:S(2)}) collective-permute-start(f32[2,256,128]{2,1,0:T(8,128)S(1)} %pad_maximum_fusion.6), channel_id=1, source_target_pairs={{0,1},{1,0},{2,3},{3,2},{4,5},{5,4},{6,7},{7,6},{8,9},{9,8},{10,11... | collective-permute-start | bytes 786440 | tf_op jit(solution)/shard_map/ppermute | solution.py:574
  40.7 5.9 %collective-permute-start.8 = (f32[1,264,128]{2,1,0:T(8,128)S(1)}, f32[1,264,128]{2,1,0:T(8,128)S(1)}, u32[]{:S(2)}, u32[]{:S(2)}) collective-permute-start(f32[1,264,128]{2,1,0:T(8,128)S(1)} %bitcast.25), channel_id=1, source_target_pairs={{0,2},{1,3},{2,0},{3,1},{4,6},{5,7},{6,4},{7,5},{8,10},{9,11},{10,... | collective-permute-start | bytes 405512 | tf_op jit(solution)/shard_map/ppermute | solution.py:574
  46.6 1.6 %collective-permute-start.9 = (f32[2,264,128]{2,1,0:T(8,128)S(1)}, f32[2,264,128]{2,1,0:T(8,128)S(1)}, u32[]{:S(2)}, u32[]{:S(2)}) collective-permute-start(f32[2,264,128]{2,1,0:T(8,128)S(1)} %pad_maximum_fusion.4), channel_id=1, source_target_pairs={{0,1},{1,0},{2,3},{3,2},{4,5},{5,4},{6,7},{7,6},{8,9},{9,8},{10,11... | collective-permute-start | bytes 811016 | tf_op jit(solution)/shard_map/ppermute | solution.py:574
  48.3 1.0 %copy-start = (f32[2,512,128]{2,1,0:T(8,128)S(1)}, f32[2,512,128]{2,1,0:T(8,128)}, u32[]{:S(2)}) copy-start(f32[2,512,128]{2,1,0:T(8,128)} %flow_ref.7) | copy-start | bytes 1572868
  52.5 4.2 %collective-permute-start.10 = (f32[104,128]{1,0:T(8,128)S(1)}, f32[104,128]{1,0:T(8,128)S(1)}, u32[]{:S(2)}, u32[]{:S(2)}) collective-permute-start(f32[104,128]{1,0:T(8,128)S(1)} %get-tuple-element.41), channel_id=1, source_target_pairs={{0,4},{4,0},{8,12},{12,8},{16,20},{20,16},{24,28},{28,24},{1,5},{5... | collective-permute-start | bytes 159752 | tf_op jit(solution)/shard_map/ppermute | solution.py:558
  56.7 6.1 %collective-permute-start.11 = (f32[104,128]{1,0:T(8,128)S(1)}, f32[104,128]{1,0:T(8,128)S(1)}, u32[]{:S(2)}, u32[]{:S(2)}) collective-permute-start(f32[104,128]{1,0:T(8,128)S(1)} %add.34), channel_id=1, source_target_pairs={{0,8},{4,12},{8,16},{12,20},{16,24},{20,28},{24,0},{28,4},{1,9},{5... | collective-permute-start | bytes 159752 | tf_op jit(solution)/shard_map/ppermute | solution.py:558
  58.1 6.1 %collective-permute-start.12 = (f32[104,128]{1,0:T(8,128)S(1)}, f32[104,128]{1,0:T(8,128)S(1)}, u32[]{:S(2)}, u32[]{:S(2)}) collective-permute-start(f32[104,128]{1,0:T(8,128)S(1)} %add.34), channel_id=1, source_target_pairs={{0,16},{4,20},{8,24},{12,28},{16,0},{20,4},{24,8},{28,12},{1,17},{... | collective-permute-start | bytes 159752 | tf_op jit(solution)/shard_map/ppermute | solution.py:558
  60.1 4.6 %collective-permute-start.13 = (f32[104,128]{1,0:T(8,128)S(1)}, f32[104,128]{1,0:T(8,128)S(1)}, u32[]{:S(2)}, u32[]{:S(2)}) collective-permute-start(f32[104,128]{1,0:T(8,128)S(1)} %add.34), channel_id=1, source_target_pairs={{0,24},{4,28},{8,0},{12,4},{16,8},{20,12},{24,16},{28,20},{1,25},{... | collective-permute-start | bytes 159752 | tf_op jit(solution)/shard_map/ppermute | solution.py:558
  64.7 3.7 %collective-permute-start.14 = (f32[13,3,128]{2,1,0:T(4,128)S(1)}, f32[13,3,128]{2,1,0:T(4,128)S(1)}, u32[]{:S(2)}, u32[]{:S(2)}) collective-permute-start(f32[13,3,128]{2,1,0:T(4,128)S(1)} %get-tuple-element.61), channel_id=1, source_target_pairs={{0,1},{1,0},{2,3},{3,2},{4,5},{5,4},{6,7},{7,6},{8,9},{9,8},{10,11... | collective-permute-start | bytes 59912 | tf_op jit(solution)/shard_map/ppermute | solution.py:588
  64.8 3.6 %collective-permute-start.15 = (f32[13,3,128]{2,1,0:T(4,128)S(1)}, f32[13,3,128]{2,1,0:T(4,128)S(1)}, u32[]{:S(2)}, u32[]{:S(2)}) collective-permute-start(f32[13,3,128]{2,1,0:T(4,128)S(1)} %get-tuple-element.60), channel_id=1, source_target_pairs={{1,2},{2,1},{5,6},{6,5},{9,10},{10,9},{13,14},{14,13},{17,18},{18,... | collective-permute-start | bytes 59912 | tf_op jit(solution)/shard_map/ppermute | solution.py:587
  74.2 7.5 %collective-permute-start.16 = (f32[1,256,128]{2,1,0:T(8,128)S(1)}, f32[1,256,128]{2,1,0:T(8,128)S(1)}, u32[]{:S(2)}, u32[]{:S(2)}) collective-permute-start(f32[1,256,128]{2,1,0:T(8,128)S(1)} %bitcast.28), channel_id=1, source_target_pairs={{0,2},{1,3},{2,0},{3,1},{4,6},{5,7},{6,4},{7,5},{8,10},{9,11},{10,... | collective-permute-start | bytes 393224 | tf_op jit(solution)/shard_map/ppermute | solution.py:574
  81.7 6.2 %collective-permute-start.17 = (f32[2,256,128]{2,1,0:T(8,128)S(1)}, f32[2,256,128]{2,1,0:T(8,128)S(1)}, u32[]{:S(2)}, u32[]{:S(2)}) collective-permute-start(f32[2,256,128]{2,1,0:T(8,128)S(1)} %pad_maximum_fusion.7), channel_id=1, source_target_pairs={{0,1},{1,0},{2,3},{3,2},{4,5},{5,4},{6,7},{7,6},{8,9},{9,8},{10,11... | collective-permute-start | bytes 786440 | tf_op jit(solution)/shard_map/ppermute | solution.py:574
  81.8 6.0 %collective-permute-start.18 = (f32[1,264,128]{2,1,0:T(8,128)S(1)}, f32[1,264,128]{2,1,0:T(8,128)S(1)}, u32[]{:S(2)}, u32[]{:S(2)}) collective-permute-start(f32[1,264,128]{2,1,0:T(8,128)S(1)} %bitcast.22), channel_id=1, source_target_pairs={{0,2},{1,3},{2,0},{3,1},{4,6},{5,7},{6,4},{7,5},{8,10},{9,11},{10,... | collective-permute-start | bytes 405512 | tf_op jit(solution)/shard_map/ppermute | solution.py:574
  87.8 1.6 %collective-permute-start.19 = (f32[2,264,128]{2,1,0:T(8,128)S(1)}, f32[2,264,128]{2,1,0:T(8,128)S(1)}, u32[]{:S(2)}, u32[]{:S(2)}) collective-permute-start(f32[2,264,128]{2,1,0:T(8,128)S(1)} %pad_maximum_fusion.5), channel_id=1, source_target_pairs={{0,1},{1,0},{2,3},{3,2},{4,5},{5,4},{6,7},{7,6},{8,9},{9,8},{10,11... | collective-permute-start | bytes 811016 | tf_op jit(solution)/shard_map/ppermute | solution.py:574
